TPU v7x, 32 devices: a whole 2x2x4 slice. The times are simulated.
32 devices in a mesh: dp: 2 (over x), expert: 8 (over z, y), tensor: 2 (over core).
Axes of the slice: x: 2, y: 2, z: 4, core: 2. Of those that a mesh axis runs over, the one named last changes fastest.
Arguments:
- tokens: bfloat16 [2048, 2048], P(('dp', 'expert')), may hold values from -6 to 6
- norm_gain: float32 [2048], replicated, may hold values from 0.1 to 1.9
- router: bfloat16 [2048, 8], replicated, may hold values from -0.125 to 0.125
- expert_ids: int32 [2048, 4], P(('dp', 'expert')), may hold values from 0 to 7, all different within a row; in each aligned block of 128 rows (0 to 127, 128 to 255, ...) at most 80 rows name the same one
- modality: int32 [2048], P(('dp', 'expert')), may hold values from 0 to 1, as said below
- expert_gate: bfloat16 [8, 2048, 1408], P('expert', None, 'tensor'), may hold values from -0.125 to 0.125
- expert_up: bfloat16 [8, 2048, 1408], P('expert', None, 'tensor'), may hold values from -0.125 to 0.125
- expert_down: bfloat16 [8, 1408, 2048], P('expert', 'tensor'), may hold values from -0.15625 to 0.15625
- shared_gate: bfloat16 [2, 2048, 704], P(None, None, ('dp', 'tensor')), may hold values from -0.125 to 0.125
- shared_up: bfloat16 [2, 2048, 704], P(None, None, ('dp', 'tensor')), may hold values from -0.125 to 0.125
- shared_down: bfloat16 [2, 704, 2048], P(None, ('dp', 'tensor')), may hold values from -0.21875 to 0.21875
Outputs:
- mixed: bfloat16 [2048, 2048], P(('dp', 'expert'), 'tensor')
Inputs may be any that keep to these rules, and one draw needn't show every extreme that they name: `expert_ids`: each token names 4 different experts; among the 128 tokens of one device (aligned blocks of rows) no expert is named by more than 80 tokens, and some expert reaches 80. `modality`: within each aligned block of 128 tokens the image patches form one run (taken cyclically) that covers from an eighth to seven eighths of the block.
All inputs are finite; a program needn't handle non-finite values.
Results may differ from a plain program's by a relative error of at most 0.0073.
Values may be sent and summed in bfloat16 or wider, within the bound.
No kernel may reach another device: no remote copies, remote signals or barrier semaphores. Data moves between devices by JAX's collectives and lax.ppermute only.
A program may use at most 128 MiB of HBM per device.

v0:
```python
import jax
import jax.numpy as jnp
from jax import lax
from jax.sharding import PartitionSpec as P

epsilon = 1e-06


def rms_normed(tokens, norm_gain):
    values = tokens.astype(jnp.float32)
    inv_scale = lax.rsqrt(jnp.mean(values * values, axis=-1, keepdims=True) + epsilon)
    return (values * inv_scale * norm_gain).astype(jnp.bfloat16)


def route_weights(normed, router, expert_ids):
    logits = jnp.dot(normed, router, preferred_element_type=jnp.float32)
    chosen = jnp.take_along_axis(logits, expert_ids, axis=1)
    scores = jax.nn.sigmoid(chosen)
    return scores / jnp.sum(scores, axis=1, keepdims=True)


def capacity_slots(expert_ids, expert_count, block_rows):
    row_count, top_count = expert_ids.shape
    onehot = (
        expert_ids[:, :, None] == jnp.arange(expert_count, dtype=jnp.int32)[None, None, :]
    ).astype(jnp.int32)
    grouped = onehot.reshape(row_count // block_rows, block_rows * top_count, expert_count)
    running = (jnp.cumsum(grouped, axis=1, dtype=jnp.int32) - 1).reshape(
        row_count, top_count, expert_count
    )
    return jnp.sum(running * onehot, axis=-1, dtype=jnp.int32)


def per_device(
    tokens,
    norm_gain,
    router,
    expert_ids,
    modality,
    expert_gate,
    expert_up,
    expert_down,
    shared_gate,
    shared_up,
    shared_down,
):
    normed = rms_normed(tokens, norm_gain)
    weights = route_weights(normed, router, expert_ids)
    tok_rows, model_width = normed.shape
    top_count = expert_ids.shape[1]
    groups = lax.axis_size("expert")
    pair_count = lax.axis_size("tensor")
    dp_count = lax.axis_size("dp")
    half_width = model_width // pair_count
    expert_count = groups * expert_gate.shape[0]
    capacity = pair_count * (
        (5 * tok_rows * top_count + 4 * expert_count * pair_count - 1)
        // (4 * expert_count * pair_count)
    )
    slot_rank = capacity_slots(expert_ids, expert_count, tok_rows)
    target = expert_ids * capacity + slot_rank
    positions = jnp.arange(expert_count * capacity, dtype=jnp.int32)
    placing = jnp.any(positions[:, None, None] == target[None, :, :], axis=2).astype(jnp.bfloat16)
    outgoing = jnp.dot(placing, normed, preferred_element_type=jnp.float32).astype(jnp.bfloat16)
    outgoing = outgoing.reshape(groups, capacity, model_width)
    received = lax.all_to_all(outgoing, "expert", split_axis=0, concat_axis=0, tiled=True)
    flat_rows = received.reshape(-1, model_width)
    gate_value = jnp.dot(flat_rows, expert_gate[0], preferred_element_type=jnp.float32)
    up_value = jnp.dot(flat_rows, expert_up[0], preferred_element_type=jnp.float32)
    hidden = (jax.nn.silu(gate_value) * up_value).astype(jnp.bfloat16)
    result = jnp.dot(hidden, expert_down[0], preferred_element_type=jnp.float32)
    partials = result.reshape(received.shape[0], received.shape[1], model_width)
    reduced = lax.psum_scatter(partials, "tensor", scatter_dimension=2, tiled=True)
    returned = lax.all_to_all(reduced, "expert", split_axis=0, concat_axis=0, tiled=True)
    picked = returned.reshape(-1, returned.shape[2])[target]
    routed = jnp.sum(weights[:, :, None] * picked, axis=1)
    everyone, kind_flags = (
        lax.all_gather(normed, "dp", axis=0, tiled=True),
        lax.all_gather(modality, "dp", axis=0, tiled=True),
    )
    image_flag = kind_flags.astype(jnp.float32)[:, None]

    def shared_hidden(modal_index, keep):
        gate_value = jnp.dot(everyone, shared_gate[modal_index], preferred_element_type=jnp.float32)
        up_value = jnp.dot(everyone, shared_up[modal_index], preferred_element_type=jnp.float32)
        return (jax.nn.silu(gate_value) * up_value * keep).astype(jnp.bfloat16)

    joined = jnp.concatenate(
        [shared_hidden(0, image_flag), shared_hidden(1, 1.0 - image_flag)], axis=1
    )
    down_blocks = shared_down.reshape(-1, pair_count, half_width)
    split_rows = joined.reshape(dp_count, tok_rows, joined.shape[1])
    shared_term = jnp.einsum(
        "pks,std->ptkd", split_rows, down_blocks, preferred_element_type=jnp.float32
    )
    shared_sum = lax.psum_scatter(
        shared_term.reshape(-1, half_width), ("dp", "tensor"), scatter_dimension=0, tiled=True
    )
    total = shared_sum + routed
    return total.astype(jnp.bfloat16)


def solution(mesh):
    in_specs = (
        P(("dp", "expert"), None),
        P(),
        P(),
        P(("dp", "expert"), None),
        P(("dp", "expert")),
        P("expert", None, "tensor"),
        P("expert", None, "tensor"),
        P("expert", "tensor", None),
        P(None, None, ("dp", "tensor")),
        P(None, None, ("dp", "tensor")),
        P(None, ("dp", "tensor"), None),
    )
    out_specs = P(("dp", "expert"), "tensor")
    return jax.shard_map(
        per_device, mesh=mesh, in_specs=in_specs, out_specs=out_specs, check_vma=False
    )
```

profile of v0, /device:TPU:0, one launch (start us, length us, event | category | flops | bytes accessed | tf_op | source)
XLA Modules:
  0.0 199.3 jit_solution(18202294359154056301)
XLA Ops:
  7.4 0.9 copy.56
  8.4 1.1 reduce-window.6
  9.6 0.2 slice_reduce_fusion
  10.1 0.7 compare_select_fusion
  11.0 1.2 fusion.16
  12.2 1.2 fusion.18
  13.5 2.4 %convolution_convert_fusion = bf16[640,2048]{1,0:T(8,128)(2,1)} fusion(pred[640,128]{1,0:T(8,128)(4,1)S(1)} %fusion.11, bf16[128,2048]{1,0:T(8,128)(2,1)S(1)} %fusion.18), kind=kOutput, calls=%fused_computation.2 | convolution fusion | flops 336855040 | bytes 3227648 | tf_op jit(solution)/shard_map/dot_general | solution.py:64
  15.8 7.3 %all-to-all-start = ((bf16[8,80,2048]{2,1,0:T(8,128)(2,1)}), bf16[8,80,2048]{2,1,0:T(8,128)(2,1)}, u32[]{:S(2)}, u32[]{:S(2)}) async-start(bf16[8,80,2048]{2,1,0:T(8,128)(2,1)} %bitcast.73), calls=%async_computation.1 | async-start | bytes 5242880 | tf_op jit(solution)/shard_map/all_to_all | solution.py:66
  23.2 0.7 all-gather.3.cloned.1.call-update
  23.9 58.8 %all-to-all-done = bf16[8,80,2048]{2,1,0:T(8,128)(2,1)} async-done(((bf16[8,80,2048]{2,1,0:T(8,128)(2,1)}), bf16[8,80,2048]{2,1,0:T(8,128)(2,1)}, u32[]{:S(2)}, u32[]{:S(2)}) %all-to-all-start) | async-done | bytes 2621472 | tf_op jit(solution)/shard_map/all_to_all | solution.py:66
  82.7 5.2 %fusion.4 = f32[640,704]{0,1:T(8,128)S(1)} fusion(bf16[640,2048]{1,0:T(8,128)(2,1)} %bitcast.18, bf16[1,2048,704]{1,2,0:T(8,128)(2,1)} %param.16), kind=kOutput, calls=%fused_computation.7 | convolution fusion | flops 1845493760 | bytes 7307264 | tf_op jit(solution)/shard_map/dot_general | solution.py:68
  87.9 5.2 %multiply_convert_fusion = bf16[640,704]{0,1:T(8,128)(2,1)} fusion(f32[640,704]{0,1:T(8,128)S(1)} %fusion.4, bf16[640,2048]{1,0:T(8,128)(2,1)} %bitcast.18, bf16[1,2048,704]{1,2,0:T(8,128)(2,1)S(1)} %copy-done.5), kind=kOutput, calls=%fused_computation.10 | convolution fusion | flops 1848197120 | bytes 8208384 | tf_op jit(solution)/shard_map/dot_general | solution.py:69
  93.1 2.3 %copy.58 = bf16[640,704]{1,0:T(8,128)(2,1)} copy(bf16[640,704]{0,1:T(8,128)(2,1)} %multiply_convert_fusion) | data formatting | bytes 1802240 | tf_op jit(solution)/shard_map/convert_element_type | solution.py:70
  95.4 5.7 %fusion = f32[8,80,2048]{2,1,0:T(8,128)} fusion(bf16[8,80,704]{2,1,0:T(8,128)(2,1)} %bitcast.75, bf16[1,704,2048]{2,1,0:T(8,128)(2,1)S(1)} %copy-done), kind=kOutput, calls=%fused_computation.3 | convolution fusion | flops 1845493760 | bytes 9027584 | tf_op jit(solution)/shard_map/dot_general | solution.py:71
  101.1 0.6 copy-done.8
  101.8 4.2 %all-gather = s32[2,1,128]{2,1,0:T(1,128)S(1)} all-gather(s32[1,1,128]{2,1,0:T(1,128)S(1)} %bitcast.80), channel_id=1, replica_groups=mesh['dp'=2,'expert'=8,'tensor'=2] {'dp'}, dimensions={0}, use_global_device_ids=true | all-gather | bytes 1536 | tf_op jit(solution)/shard_map/all_gather | solution.py:79
  106.0 4.9 %reshape.152 = bf16[352,2,1024]{2,1,0:T(2,128)(2,1)} reshape(bf16[2,176,2048]{2,1,0:T(8,128)(2,1)} %param.21) | data formatting | bytes 2883584 | tf_op jit(solution)/shard_map/reshape | solution.py:91
  111.0 2.2 %fusion.20 = f32[256,176]{0,1:T(8,128)S(1)} fusion(bf16[256,2048]{1,0:T(8,128)(2,1)} %all-gather.3.cloned.1.call-done, bf16[2,2048,176]{1,2,0:T(8,128)(2,1)} %param.19), kind=kOutput, calls=%fused_computation.28 | convolution fusion | flops 184549376 | bytes 1949696 | tf_op jit(solution)/shard_map/dot_general | solution.py:84
  113.2 1.9 fusion.23
  115.1 0.5 fusion.14
  115.7 4.4 %all-to-all-start.1 = ((f32[8,80,1024]{2,1,0:T(8,128)}), f32[8,80,1024]{2,1,0:T(8,128)}, u32[]{:S(2)}, u32[]{:S(2)}) async-start(f32[8,80,1024]{2,1,0:T(8,128)} %reduce-scatter.5.cloned.1.call-done), calls=%async_computation.3 | async-start | bytes 5242880 | tf_op jit(solution)/shard_map/all_to_all | solution.py:74
  120.1 0.2 reduce-scatter.3.cloned.1.call-start
  120.3 1.9 fusion.15
  122.3 3.4 %fusion.8 = f32[2,128,2,1024]{3,1,2,0:T(8,128)} fusion(bf16[352,2,1024]{2,1,0:T(2,128)(2,1)} %reshape.152, bf16[2,128,352,1]{1,0,2,3:T(2,128)(2,1)S(1)} %bitcast.76), kind=kOutput, calls=%fused_computation.11 | convolution fusion | flops 369098752 | bytes 3719168 | tf_op jit(solution)/shard_map/pks,std->ptkd/dot_general | solution.py:93
  126.2 0.5 copy-done.2
  126.8 0.2 fusion.32
  127.0 2.6 %gather_fusion.1 = f32[512]{0:T(512)S(1)} fusion(f32[128,8]{0,1:T(8,128)S(1)} %fusion.32, s32[512]{0:T(512)S(1)} %reshape.172), kind=kCustom, calls=%fused_computation.1 | custom fusion | bytes 8192 | tf_op jit(solution)/shard_map/jit(take_along_axis)/gather | solution.py:17
  130.0 48.9 %all-to-all-done.1 = f32[8,80,1024]{2,1,0:T(8,128)} async-done(((f32[8,80,1024]{2,1,0:T(8,128)}), f32[8,80,1024]{2,1,0:T(8,128)}, u32[]{:S(2)}, u32[]{:S(2)}) %all-to-all-start.1) | async-done | bytes 2621472 | tf_op jit(solution)/shard_map/all_to_all | solution.py:74
  178.8 5.4 %gather_fusion = f32[512,1024]{1,0:T(8,128)} fusion(f32[640,1024]{1,0:T(8,128)} %bitcast.24, s32[1024]{0:T(1024)S(1)} %pad_clamp_fusion), kind=kCustom, calls=%fused_computation | custom fusion | bytes 4196352 | tf_op jit(solution)/shard_map/gather | solution.py:75
  184.2 2.9 %reshape.165 = f32[128,4,1024]{2,1,0:T(4,128)} reshape(f32[512,1024]{1,0:T(8,128)} %gather_fusion) | data formatting | bytes 4194304 | tf_op jit(solution)/shard_map/gather | solution.py:75
  187.1 3.0 %multiply_reduce_fusion = f32[128,1024]{1,0:T(8,128)S(1)} fusion(f32[128,4,1024]{2,1,0:T(4,128)} %reshape.165, f32[128,4]{1,0:T(8,128)S(1)} %copy.55), kind=kLoop, calls=%fused_computation.9 | loop fusion | flops 917504 | bytes 2623488 | tf_op jit(solution)/shard_map/reduce_sum | solution.py:76
  190.1 1.8 add_convert_fusion
  (47 shorter events, 1.6 us)
Async XLA Ops:
  7.4 88.0 %copy-start = (bf16[1,704,2048]{2,1,0:T(8,128)(2,1)S(1)}, bf16[1,704,2048]{2,1,0:T(8,128)(2,1)}, u32[]{:S(2)}) copy-start(bf16[1,704,2048]{2,1,0:T(8,128)(2,1)} %param.18) | copy-start | bytes 8650756
  13.5 2.4 %copy-start.1 = (bf16[128,2048]{1,0:T(8,128)(2,1)}, bf16[128,2048]{1,0:T(8,128)(2,1)S(1)}, u32[]{:S(2)}) copy-start(bf16[128,2048]{1,0:T(8,128)(2,1)S(1)} %fusion.18) | copy-start | bytes 1572868
  15.8 66.9 %all-to-all-start = ((bf16[8,80,2048]{2,1,0:T(8,128)(2,1)}), bf16[8,80,2048]{2,1,0:T(8,128)(2,1)}, u32[]{:S(2)}, u32[]{:S(2)}) async-start(bf16[8,80,2048]{2,1,0:T(8,128)(2,1)} %bitcast.73), calls=%async_computation.1 | async-start | bytes 5242880 | tf_op jit(solution)/shard_map/all_to_all | solution.py:66
  23.1 87.8 %all-gather.3.cloned.1.call-start = ((), (), s32[]{:S(2)}) async-start(), calls=%async_computation.4 | async-start | bytes 1572864 | tf_op jit(solution)/shard_map/all_gather | solution.py:78
  23.9 91.8 %reduce-scatter.5.cloned.1.call-start = ((), (), s32[]{:S(2)}) async-start(), calls=%async_computation.6 | async-start | bytes 7864320 | tf_op jit(solution)/shard_map/reduce_scatter | solution.py:73
  82.7 5.2 %copy-start.5 = (bf16[1,2048,704]{1,2,0:T(8,128)(2,1)S(1)}, bf16[1,2048,704]{1,2,0:T(8,128)(2,1)}, u32[]{:S(2)}) copy-start(bf16[1,2048,704]{1,2,0:T(8,128)(2,1)} %param.17) | copy-start | bytes 8650756
  101.1 0.7 copy-start.8
  110.9 4.2 %copy-start.6 = (bf16[2,2048,176]{1,2,0:T(8,128)(2,1)S(1)}, bf16[2,2048,176]{1,2,0:T(8,128)(2,1)}, u32[]{:S(2)}) copy-start(bf16[2,2048,176]{1,2,0:T(8,128)(2,1)} %param.20) | copy-start | bytes 4325380
  110.9 4.2 %copy-start.7 = (bf16[256,2048]{1,0:T(8,128)(2,1)S(1)}, bf16[256,2048]{1,0:T(8,128)(2,1)}, u32[]{:S(2)}) copy-start(bf16[256,2048]{1,0:T(8,128)(2,1)} %all-gather.3.cloned.1.call-done) | copy-start | bytes 3145732
  115.7 63.2 %all-to-all-start.1 = ((f32[8,80,1024]{2,1,0:T(8,128)}), f32[8,80,1024]{2,1,0:T(8,128)}, u32[]{:S(2)}, u32[]{:S(2)}) async-start(f32[8,80,1024]{2,1,0:T(8,128)} %reduce-scatter.5.cloned.1.call-done), calls=%async_computation.3 | async-start | bytes 5242880 | tf_op jit(solution)/shard_map/all_to_all | solution.py:74
  120.1 70.0 %reduce-scatter.3.cloned.1.call-start = ((), (), s32[]{:S(2)}) async-start(), calls=%async_computation.5 | async-start | bytes 2621440 | tf_op jit(solution)/shard_map/reduce_scatter | solution.py:96
  122.3 3.7 %copy-start.3 = (s32[128,4]{0,1:T(4,128)S(1)}, s32[128,4]{0,1:T(4,128)}, u32[]{:S(2)}) copy-start(s32[128,4]{0,1:T(4,128)} %param.14) | copy-start | bytes 6148
  125.8 1.0 copy-start.2
  125.8 1.0 copy-start.4
Sparse Core Ops, SparseCore 0:
  25.5 22.6 all-gather.2
  125.9 32.3 reduce-scatter.2
Sparse Core Ops, SparseCore 1:
  101.2 11.8 reduce-scatter.4
where the time goes:
time: 200 us; the launch traced here: 199 us
  waiting for transfers between devices  108 us (54%)
  matrix products  28.7 us (14%)
  local copies, waits for them, and re-layouts  21.4 us (11%)
  between operations  15.1 us (8%)
  starting transfers between devices  12 us (6%)
  other arithmetic  9.49 us (5%)
  blocking collectives  4.22 us (2%)
    all_to_all x1, waiting for transfers between devices, per_device(): lax.all_to_all(outgoing, 'expert', split_axis=0, concat_axis=0, tiled=True)  58.8 us
    all_to_all x1, waiting for transfers between devices, per_device(): lax.all_to_all(reduced, 'expert', split_axis=0, concat_axis=0, tiled=True)  48.9 us
    gather x2, local copies, waits for them, and re-layouts, per_device(): picked = returned.reshape(-1, returned.shape[2])[target]  8.24 us
    all_to_all x1, starting transfers between devices, per_device(): lax.all_to_all(outgoing, 'expert', split_axis=0, concat_axis=0, tiled=True)  7.31 us
    dot_general x1, matrix products, per_device(): result = jnp.dot(hidden, expert_down[0], preferred_element_type=jnp.float32)  5.71 us
    dot_general x1, matrix products, per_device(): jnp.dot(flat_rows, expert_up[0], preferred_element_type=jnp.float32)  5.19 us
    dot_general x1, matrix products, per_device(): jnp.dot(flat_rows, expert_gate[0], preferred_element_type=jnp.float32)  5.19 us
    reshape x1, local copies, waits for them, and re-layouts, per_device(): down_blocks = shared_down.reshape(-1, pair_count, half_width)  4.94 us
  transfers between devices with their start and end apart: 5, of which 2 were waited for; matrix products, arithmetic and copies ran while one was open for 24% of the time, Pallas kernels for 0%

commit v1 on v0

v1 whole, which is shorter than its diff:
```python
import jax
import jax.numpy as jnp
from jax import lax
from jax.experimental import pallas as pl
from jax.experimental.pallas import tpu as pltpu
from jax.sharding import PartitionSpec as P

epsilon = 1e-06
LANES = 128
MIB = 2**20
NT = (((1,), (1,)), ((), ()))
TN = (((0,), (0,)), ((), ()))


def dot(a, b, dims):
    return lax.dot_general(a, b, dims, preferred_element_type=jnp.float32)


def ring_order(count):
    return list(range(0, count, 2)) + list(range(count - 1, 0, -2))


def call(body, outs, args, name, limit, flops=0, moved=0):
    vmem = pl.BlockSpec(memory_space=pltpu.VMEM)
    return pl.pallas_call(
        body,
        out_shape=outs,
        in_specs=[vmem] * len(args),
        out_specs=jax.tree.map(lambda _: vmem, outs),
        compiler_params=pltpu.CompilerParams(vmem_limit_bytes=limit * MIB),
        cost_estimate=pl.CostEstimate(flops=flops, bytes_accessed=moved, transcendentals=0),
        name=name,
    )(*args)


def prologue_body(expert_count, tokens, gain, router, ids, modality, packed):
    width = tokens.shape[1]
    values = tokens[...].astype(jnp.float32)
    scale = lax.rsqrt(jnp.mean(values * values, axis=1, keepdims=True) + epsilon)
    normed = (values * scale * gain[...]).astype(jnp.bfloat16)
    packed[:, :width] = normed
    scores = 1.0 / (1.0 + jnp.exp(-dot(router[...], normed, NT)))
    which = lax.broadcasted_iota(jnp.int32, scores.shape, 0)
    chosen = which == ids[0:1, :]
    for k in range(1, ids.shape[0]):
        chosen = chosen | (which == ids[k : k + 1, :])
    scores = jnp.where(chosen, scores, 0.0)
    weights = scores / jnp.sum(scores, axis=0, keepdims=True)
    rounded = weights.astype(jnp.bfloat16).astype(jnp.float32)
    image = (modality[...] == 1).astype(jnp.float32)
    rows = packed.shape[1] - width - 2 * expert_count
    first = lax.broadcasted_iota(jnp.int32, (rows, image.shape[1]), 0) == 0
    table = jnp.concatenate([rounded, weights - rounded, jnp.where(first, image, 0.0)], axis=0)
    packed[:, width:] = table.T.astype(jnp.bfloat16)


def side_rows(packed, width, lanes):
    side = packed[:, width:]
    lane = lax.broadcasted_iota(jnp.int32, (8, side.shape[1]), 1)
    picked = lane == lanes[0]
    for other in lanes[1:]:
        picked = picked | (lane == other)
    return dot(picked.astype(jnp.bfloat16), side, NT)[0:1, :]


def gated(gate, up, factor):
    return (gate / (1.0 + jnp.exp(-gate)) * up * factor).astype(jnp.bfloat16)


def expert_body(expert_count, inputs, *refs):
    blocks, (gate, up, down), outs = refs[:inputs], refs[inputs : inputs + 3], refs[inputs + 3 :]
    width = gate.shape[1]
    rows = blocks[0][...]
    if inputs == 2:
        rows = jnp.concatenate([rows, blocks[1][...]], axis=0)
    me = lax.axis_index("expert")
    factor = side_rows(rows, width, (me, me + expert_count))
    rows = rows[:, :width]
    hidden = gated(dot(gate[...], rows, NT), dot(up[...], rows, NT), factor)
    result = dot(hidden, down[...], TN)
    start = 0
    for out in outs:
        out[...] = result[start : start + out.shape[0]].astype(out.dtype)
        start += out.shape[0]


def shared_body(expert_count, own, other, gate, up, down, own_out, other_out):
    width = gate.shape[1]
    rows = jnp.concatenate([own[...], other[...]], axis=0)
    image = side_rows(rows, width, (2 * expert_count,))
    rows = rows[:, :width]
    gate_value, up_value = dot(gate[...], rows, NT), dot(up[...], rows, NT)
    kind = lax.broadcasted_iota(jnp.int32, gate_value.shape, 0) < gate_value.shape[0] // 2
    hidden = gated(gate_value, up_value, jnp.where(kind, image, 1.0 - image))
    result = dot(hidden, down[...], TN)
    own_out[...] = result[: own_out.shape[0]]
    other_out[...] = result[own_out.shape[0] :].astype(other_out.dtype)


def first_add_body(mine, partner, arrived, out):
    total = mine[...] + partner[...].astype(jnp.float32)
    out[...] = total.astype(out.dtype)
    half = arrived.shape[0]
    start = pl.multiple_of((1 - lax.axis_index("tensor")) * half, half)
    place = pl.ds(start, half)
    part = mine[place, :] + partner[place, :].astype(jnp.float32)
    out[place, :] = (part + arrived[...].astype(jnp.float32)).astype(out.dtype)


def last_add_body(*refs):
    terms, (stay, cross) = refs[:-2], refs[-2:]
    half = stay.shape[1]
    core = lax.axis_index("tensor")
    for out, index in ((stay, core), (cross, 1 - core)):
        place = pl.ds(pl.multiple_of(index * half, half), half)
        total = terms[0][:, place].astype(jnp.float32)
        for term in terms[1:]:
            total = total + term[:, place].astype(jnp.float32)
        out[...] = total.astype(out.dtype)


def per_device(
    tokens,
    norm_gain,
    router,
    expert_ids,
    modality,
    expert_gate,
    expert_up,
    expert_down,
    shared_gate,
    shared_up,
    shared_down,
):
    tok_rows, width = tokens.shape
    half_rows, half_width = tok_rows // 2, width // 2
    experts = lax.axis_size("expert")
    side = -(-(2 * experts + 1) // LANES) * LANES
    middle = experts // 2
    shape = jax.ShapeDtypeStruct
    f32, bf16 = jnp.float32, jnp.bfloat16

    order = ring_order(experts)
    onward, across = [], []
    for here, there in zip(order, order[1:] + order[:1]):
        onward += [(2 * here, 2 * there), (2 * there + 1, 2 * here + 1)]
        across += [(2 * here, 2 * there + 1), (2 * there + 1, 2 * here)]
    hop = lambda x: lax.ppermute(x, ("expert", "tensor"), onward)
    cross_hop = lambda x: lax.ppermute(x, ("expert", "tensor"), across)
    swap = lambda x: lax.ppermute(x, "tensor", [(0, 1), (1, 0)])
    dp_swap = lambda x: lax.ppermute(x, "dp", [(0, 1), (1, 0)])

    gate, up = expert_gate[0].T, expert_up[0].T
    down = expert_down[0]
    hidden_units = down.shape[0]
    shared_units = 2 * shared_down.shape[1]
    shared_gate = jnp.swapaxes(shared_gate, 1, 2).reshape(shared_units, width)
    shared_up = jnp.swapaxes(shared_up, 1, 2).reshape(shared_units, width)
    shared_down = shared_down.reshape(shared_units, width)

    own = call(
        lambda *refs: prologue_body(experts, *refs),
        shape((tok_rows, width + side), bf16),
        (tokens, norm_gain[None, :], router.T, expert_ids.T, modality[None, :]),
        "prologue",
        12,
        4 * MIB,
        MIB,
    )

    def experts_of(blocks, outs):
        rows = sum(block.shape[0] for block in blocks)
        return call(
            lambda *refs: expert_body(experts, len(blocks), *refs),
            outs,
            (*blocks, gate, up, down),
            "experts",
            20,
            6 * rows * width * hidden_units,
            6 * width * hidden_units,
        )

    other_dp = dp_swap(own)
    kept, sent = {}, {}
    block = own
    for k in range(1, middle + 1):
        if k == middle:
            start = lax.axis_index("tensor") * half_rows
            block = lax.dynamic_slice_in_dim(block, start, half_rows, axis=0)
        block = hop(block)
        partner = swap(block)
        rows = block.shape[0]
        give, kept[k] = experts_of(
            (block, partner), (shape((rows, width), bf16), shape((rows, width), f32))
        )
        sent[k] = swap(give)

    own_part = experts_of((own,), (shape((tok_rows, width), f32),))[0]
    shared_own, shared_other = call(
        lambda *refs: shared_body(experts, *refs),
        (shape((tok_rows, width), f32), shape((tok_rows, width), bf16)),
        (own, other_dp, shared_gate, shared_up, shared_down),
        "shared",
        16,
        12 * tok_rows * width * shared_units,
        6 * width * shared_units,
    )
    shared_back = dp_swap(shared_other)
    halves = (shape((tok_rows, half_width), bf16),) * 2
    local_stay, local_cross = call(
        last_add_body, (shape((tok_rows, half_width), f32), halves[0]),
        (own_part, shared_own, shared_back), "local_add", 8,
    )
    local_recv = swap(local_cross)

    running = (kept[middle] + sent[middle].astype(f32)).astype(bf16)
    for k in range(middle - 1, 0, -1):
        arrived = hop(running)
        if k == 1:
            stay, cross = call(
                last_add_body, halves, (kept[k], sent[k], arrived), "last_add", 8
            )
        elif k == middle - 1:
            running = call(
                first_add_body, shape((tok_rows, width), bf16),
                (kept[k], sent[k], arrived), "first_add", 8,
            )
        else:
            running = (kept[k] + sent[k].astype(f32) + arrived.astype(f32)).astype(bf16)
    stay, cross = hop(stay), cross_hop(cross)
    total = local_stay + local_recv.astype(f32) + stay.astype(f32) + cross.astype(f32)
    return total.astype(bf16)


def solution(mesh):
    in_specs = (
        P(("dp", "expert"), None),
        P(),
        P(),
        P(("dp", "expert"), None),
        P(("dp", "expert")),
        P("expert", None, "tensor"),
        P("expert", None, "tensor"),
        P("expert", "tensor", None),
        P(None, None, ("dp", "tensor")),
        P(None, None, ("dp", "tensor")),
        P(None, ("dp", "tensor"), None),
    )
    out_specs = P(("dp", "expert"), "tensor")
    return jax.shard_map(
        per_device, mesh=mesh, in_specs=in_specs, out_specs=out_specs, check_vma=False
    )
```

time: 200 us -> 91 us (0.46)
  waiting for transfers between devices: 108 us -> 43.6 us
  matrix products: 28.7 us -> 0 us
  Pallas kernels: 0 us -> 15 us
  between operations: 15.1 us -> 0.17 us
  local copies, waits for them, and re-layouts: 21.4 us -> 9.32 us
  starting transfers between devices: 12 us -> 21.4 us
  other arithmetic: 9.49 us -> 1.08 us
  blocking collectives: 4.22 us -> 0 us
    all_to_all x2 -> x0, waiting for transfers between devices: 108 us -> none  [the longest x1 58.8 us: per_device(): lax.all_to_all(outgoing, 'expert', split_axis=0, concat_axis=0, tiled=True)]
    ppermute x0 -> x20, waiting for transfers between devices: none -> 43.6 us  [the longest x8 33.1 us: per_device(): hop = lambda x: lax.ppermute(x, ('expert', 'tensor'), onward)]
    dot_general x10 -> x0, matrix products: 28.7 us -> none  [the longest x1 5.71 us: per_device(): result = jnp.dot(hidden, expert_down[0], preferred_element_type=jnp.float32)]
    ppermute x0 -> x20, starting transfers between devices: none -> 21.4 us  [the longest x8 15.9 us: per_device(): hop = lambda x: lax.ppermute(x, ('expert', 'tensor'), onward)]
    pallas_call x0 -> x10, Pallas kernels: none -> 15 us  [call(): pl.pallas_call(body, out_shape=outs, in_specs=[vmem] * len(args), out_spe...]
    all_to_all x2 -> x0, starting transfers between devices: 11.7 us -> none  [the longest x1 7.31 us: per_device(): lax.all_to_all(outgoing, 'expert', split_axis=0, concat_axis=0, tiled=True)]
    gather x7 -> x0, local copies, waits for them, and re-layouts: 11.2 us -> none  [the longest x2 8.24 us: per_device(): picked = returned.reshape(-1, returned.shape[2])[target]]
    unnamed x19 -> x24, local copies, waits for them, and re-layouts: 2.15 us -> 9.3 us
  transfers between devices with their start and end apart: 5 -> 20, of which waited for: 2 -> 11; matrix products, arithmetic and copies ran while one was open for 24% -> 0% of each run, Pallas kernels for 0% -> 16%
where the time goes in v1:
time: 91 us; the launch traced here: 90.6 us
  waiting for transfers between devices  43.6 us (48%)
  starting transfers between devices  21.4 us (24%)
  Pallas kernels  15 us (16%)
  local copies, waits for them, and re-layouts  9.32 us (10%)
  other arithmetic  1.08 us (1%)
    ppermute x8, waiting for transfers between devices, per_device(): hop = lambda x: lax.ppermute(x, ('expert', 'tensor'), onward)  33.1 us
    ppermute x8, starting transfers between devices, per_device(): hop = lambda x: lax.ppermute(x, ('expert', 'tensor'), onward)  15.9 us
    pallas_call x10, Pallas kernels, call(): pl.pallas_call(body, out_shape=outs, in_specs=[vmem] * len(args), out_spe...  15 us
    unnamed x24, local copies, waits for them, and re-layouts  9.3 us
    ppermute x2, waiting for transfers between devices, per_device(): dp_swap = lambda x: lax.ppermute(x, 'dp', [(0, 1), (1, 0)])  6.72 us
    ppermute x2, starting transfers between devices, per_device(): dp_swap = lambda x: lax.ppermute(x, 'dp', [(0, 1), (1, 0)])  3.8 us
    ppermute x1, waiting for transfers between devices, per_device(): cross_hop = lambda x: lax.ppermute(x, ('expert', 'tensor'), across)  2.24 us
  transfers between devices with their start and end apart: 20, of which 11 were waited for; matrix products, arithmetic and copies ran while one was open for 0% of the time, Pallas kernels for 16%

profile of v1, /device:TPU:0, one launch (start us, length us, event | category | flops | bytes accessed | tf_op | source)
XLA Modules:
  0.0 90.6 jit_solution(15851405032673545499)
XLA Ops:
  0.0 1.0 %copy-done.7 = bf16[128,2048]{1,0:T(8,128)(2,1)S(1)} copy-done((bf16[128,2048]{1,0:T(8,128)(2,1)S(1)}, bf16[128,2048]{1,0:T(8,128)(2,1)}, u32[]{:S(2)}) %copy-start.7) | copy-done | bytes 524312
  1.0 0.8 copy-done.8
  4.4 3.1 %collective-permute-start.3 = (bf16[128,2176]{1,0:T(8,128)(2,1)S(1)}, bf16[128,2176]{1,0:T(8,128)(2,1)S(1)}, u32[]{:S(2)}, u32[]{:S(2)}) collective-permute-start(bf16[128,2176]{1,0:T(8,128)(2,1)S(1)} %prologue.1.refs_0_), channel_id=1, source_target_pairs={{0,4},{5,1},{4,8},{9,5},{8,12},{13,9},{12,14},{15,13},{14,10},{11,... | collective-permute-start | bytes 1671176 | tf_op jit(solution)/shard_map/ppermute | solution.py:148
  7.5 7.5 %collective-permute-done.3.refs_0_ = bf16[128,2176]{1,0:T(8,128)(2,1)S(1)} collective-permute-done((bf16[128,2176]{1,0:T(8,128)(2,1)S(1)}, bf16[128,2176]{1,0:T(8,128)(2,1)S(1)}, u32[]{:S(2)}, u32[]{:S(2)}) %collective-permute-start.3) | collective-permute-done | bytes 557088 | tf_op jit(solution)/shard_map/ppermute | solution.py:148
  14.9 2.1 %collective-permute-start.6 = (bf16[128,2176]{1,0:T(8,128)(2,1)S(1)}, bf16[128,2176]{1,0:T(8,128)(2,1)S(1)}, u32[]{:S(2)}, u32[]{:S(2)}) collective-permute-start(bf16[128,2176]{1,0:T(8,128)(2,1)S(1)} %collective-permute-done.3.refs_0_), channel_id=1, source_target_pairs={{0,4},{5,1},{4,8},{9,5},{8,12},{13,9},{12,14},{15,13},{14,10},{11,... | collective-permute-start | bytes 1671176 | tf_op jit(solution)/shard_map/ppermute | solution.py:148
  17.0 7.5 %collective-permute-done.6.refs_0_ = bf16[128,2176]{1,0:T(8,128)(2,1)S(1)} collective-permute-done((bf16[128,2176]{1,0:T(8,128)(2,1)S(1)}, bf16[128,2176]{1,0:T(8,128)(2,1)S(1)}, u32[]{:S(2)}, u32[]{:S(2)}) %collective-permute-start.6) | collective-permute-done | bytes 557088 | tf_op jit(solution)/shard_map/ppermute | solution.py:148
  24.5 2.1 %collective-permute-start.9 = (bf16[128,2176]{1,0:T(8,128)(2,1)S(1)}, bf16[128,2176]{1,0:T(8,128)(2,1)S(1)}, u32[]{:S(2)}, u32[]{:S(2)}) collective-permute-start(bf16[128,2176]{1,0:T(8,128)(2,1)S(1)} %collective-permute-done.6.refs_0_), channel_id=1, source_target_pairs={{0,4},{5,1},{4,8},{9,5},{8,12},{13,9},{12,14},{15,13},{14,10},{11,... | collective-permute-start | bytes 1671176 | tf_op jit(solution)/shard_map/ppermute | solution.py:148
  26.6 7.5 %collective-permute-done.9.refs_0_ = bf16[128,2176]{1,0:T(8,128)(2,1)S(1)} collective-permute-done((bf16[128,2176]{1,0:T(8,128)(2,1)S(1)}, bf16[128,2176]{1,0:T(8,128)(2,1)S(1)}, u32[]{:S(2)}, u32[]{:S(2)}) %collective-permute-start.9) | collective-permute-done | bytes 557088 | tf_op jit(solution)/shard_map/ppermute | solution.py:148
  34.0 2.1 %collective-permute-start.12 = (bf16[64,2176]{1,0:T(8,128)(2,1)S(1)}, bf16[64,2176]{1,0:T(8,128)(2,1)S(1)}, u32[]{:S(2)}, u32[]{:S(2)}) collective-permute-start(bf16[64,2176]{1,0:T(8,128)(2,1)S(1)} %constant_dynamic-slice_fusion), channel_id=1, source_target_pairs={{0,4},{5,1},{4,8},{9,5},{8,12},{13,9},{12,14},{15,13},{14,10},{11,... | collective-permute-start | bytes 835592 | tf_op jit(solution)/shard_map/ppermute | solution.py:148
  36.2 4.5 %collective-permute-done.12.refs_0_ = bf16[64,2176]{1,0:T(8,128)(2,1)S(1)} collective-permute-done((bf16[64,2176]{1,0:T(8,128)(2,1)S(1)}, bf16[64,2176]{1,0:T(8,128)(2,1)S(1)}, u32[]{:S(2)}, u32[]{:S(2)}) %collective-permute-start.12) | collective-permute-done | bytes 278560 | tf_op jit(solution)/shard_map/ppermute | solution.py:148
  40.6 1.6 %collective-permute-done.13.refs_1_ = bf16[64,2176]{1,0:T(8,128)(2,1)S(1)} collective-permute-done((bf16[64,2176]{1,0:T(8,128)(2,1)S(1)}, bf16[64,2176]{1,0:T(8,128)(2,1)S(1)}, u32[]{:S(2)}, u32[]{:S(2)}) %collective-permute-start.13) | collective-permute-done | bytes 278560 | tf_op jit(solution)/shard_map/ppermute | solution.py:150
  42.2 1.8 %copy-done = bf16[1,2048,704]{1,2,0:T(8,128)(2,1)S(1)} copy-done((bf16[1,2048,704]{1,2,0:T(8,128)(2,1)S(1)}, bf16[1,2048,704]{1,2,0:T(8,128)(2,1)}, u32[]{:S(2)}) %copy-start) | copy-done | bytes 2883608
  44.0 1.8 %copy-done.2 = bf16[1,2048,704]{1,2,0:T(8,128)(2,1)S(1)} copy-done((bf16[1,2048,704]{1,2,0:T(8,128)(2,1)S(1)}, bf16[1,2048,704]{1,2,0:T(8,128)(2,1)}, u32[]{:S(2)}) %copy-start.2) | copy-done | bytes 2883608
  45.8 1.8 %copy-done.3 = bf16[1,704,2048]{2,1,0:T(8,128)(2,1)S(1)} copy-done((bf16[1,704,2048]{2,1,0:T(8,128)(2,1)S(1)}, bf16[1,704,2048]{2,1,0:T(8,128)(2,1)}, u32[]{:S(2)}) %copy-start.3) | copy-done | bytes 2883608
  47.6 2.2 %experts.9 = (bf16[64,2048]{1,0:T(8,128)(2,1)S(1)}, f32[64,2048]{1,0:T(8,128)S(1)}) custom-call(bf16[64,2176]{1,0:T(8,128)(2,1)S(1)} %collective-permute-done.12.refs_0_, bf16[64,2176]{1,0:T(8,128)(2,1)S(1)} %collective-permute-done.13.refs_1_, bf16[704,2048]{1,0:T(8,128)(2,1)S(1)} %bitcast.18, bf16[704,2048]{1,0:T(8,128)(2,1)S(1)} %bitcast.23, ...), custom_call_target="tpu_custom_call" | custom-call | flops 1107296256 | bytes 8650752 | tf_op jit(solution)/shard_map/experts/pallas_call | solution.py:25
  50.1 2.0 %collective-permute-start = (bf16[128,2176]{1,0:T(8,128)(2,1)S(1)}, bf16[128,2176]{1,0:T(8,128)(2,1)S(1)}, u32[]{:S(2)}, u32[]{:S(2)}) collective-permute-start(bf16[128,2176]{1,0:T(8,128)(2,1)S(1)} %prologue.1.refs_0_), channel_id=1, source_target_pairs={{0,16},{16,0},{1,17},{17,1},{2,18},{18,2},{3,19},{19,3},{4,20},{20... | collective-permute-start | bytes 1671176 | tf_op jit(solution)/shard_map/ppermute | solution.py:151
  52.2 2.6 %experts.8 = (bf16[128,2048]{1,0:T(8,128)(2,1)S(1)}, f32[128,2048]{1,0:T(8,128)S(1)}) custom-call(bf16[128,2176]{1,0:T(8,128)(2,1)S(1)} %collective-permute-done.9.refs_0_, bf16[128,2176]{1,0:T(8,128)(2,1)S(1)} %collective-permute-done.10.refs_1_, bf16[704,2048]{1,0:T(8,128)(2,1)S(1)} %bitcast.19, bf16[704,2048]{1,0:T(8,128)(2,1)S(1)} %bitcast.24, ...), custom_call_target="tpu_custom_call" | custom-call | flops 2214592512 | bytes 8650752 | tf_op jit(solution)/shard_map/experts/pallas_call | solution.py:25
  55.3 1.6 %collective-permute-start.15 = (bf16[64,2048]{1,0:T(8,128)(2,1)S(1)}, bf16[64,2048]{1,0:T(8,128)(2,1)S(1)}, u32[]{:S(2)}, u32[]{:S(2)}) collective-permute-start(bf16[64,2048]{1,0:T(8,128)(2,1)S(1)} %add_convert_fusion.2), channel_id=1, source_target_pairs={{0,4},{5,1},{4,8},{9,5},{8,12},{13,9},{12,14},{15,13},{14,10},{11,... | collective-permute-start | bytes 786440 | tf_op jit(solution)/shard_map/ppermute | solution.py:148
  57.0 2.6 %experts.7 = (bf16[128,2048]{1,0:T(8,128)(2,1)S(1)}, f32[128,2048]{1,0:T(8,128)S(1)}) custom-call(bf16[128,2176]{1,0:T(8,128)(2,1)S(1)} %collective-permute-done.6.refs_0_, bf16[128,2176]{1,0:T(8,128)(2,1)S(1)} %collective-permute-done.7.refs_1_, bf16[704,2048]{1,0:T(8,128)(2,1)S(1)} %bitcast.20, bf16[704,2048]{1,0:T(8,128)(2,1)S(1)} %bitcast.25, ...), custom_call_target="tpu_custom_call" | custom-call | flops 2214592512 | bytes 8650752 | tf_op jit(solution)/shard_map/experts/pallas_call | solution.py:25
  60.2 1.6 %collective-permute-done.15.arrived = bf16[64,2048]{1,0:T(8,128)(2,1)S(1)} collective-permute-done((bf16[64,2048]{1,0:T(8,128)(2,1)S(1)}, bf16[64,2048]{1,0:T(8,128)(2,1)S(1)}, u32[]{:S(2)}, u32[]{:S(2)}) %collective-permute-start.15) | collective-permute-done | bytes 262176 | tf_op jit(solution)/shard_map/ppermute | solution.py:148
  61.9 1.6 %collective-permute-start.16 = (bf16[128,2048]{1,0:T(8,128)(2,1)S(1)}, bf16[128,2048]{1,0:T(8,128)(2,1)S(1)}, u32[]{:S(2)}, u32[]{:S(2)}) collective-permute-start(bf16[128,2048]{1,0:T(8,128)(2,1)S(1)} %first_add.1), channel_id=1, source_target_pairs={{0,4},{5,1},{4,8},{9,5},{8,12},{13,9},{12,14},{15,13},{14,10},{11,... | collective-permute-start | bytes 1572872 | tf_op jit(solution)/shard_map/ppermute | solution.py:148
  63.6 1.7 %collective-permute-done.refs_1_ = bf16[128,2176]{1,0:T(8,128)(2,1)S(1)} collective-permute-done((bf16[128,2176]{1,0:T(8,128)(2,1)S(1)}, bf16[128,2176]{1,0:T(8,128)(2,1)S(1)}, u32[]{:S(2)}, u32[]{:S(2)}) %collective-permute-start) | collective-permute-done | bytes 557088 | tf_op jit(solution)/shard_map/ppermute | solution.py:151
  65.3 1.7 %shared.1 = (f32[128,2048]{1,0:T(8,128)S(1)}, bf16[128,2048]{1,0:T(8,128)(2,1)S(1)}) custom-call(bf16[128,2176]{1,0:T(8,128)(2,1)S(1)} %prologue.1.refs_0_, bf16[128,2176]{1,0:T(8,128)(2,1)S(1)} %collective-permute-done.refs_1_, bf16[352,2048]{1,0:T(8,128)(2,1)S(1)} %bitcast.33, bf16[352,2048]{1,0:T(8,128)(2,1)S(1)} %bitcast.34, bf16[352,2048]{1,0:T(8,128)(2,1)S(1)} %bitcast.35), custom_call_target="tpu_custom_call" | custom-call | flops 1107296256 | bytes 4325376 | tf_op jit(solution)/shard_map/shared/pallas_call | solution.py:25
  66.9 1.8 %collective-permute-start.1 = (bf16[128,2048]{1,0:T(8,128)(2,1)S(1)}, bf16[128,2048]{1,0:T(8,128)(2,1)S(1)}, u32[]{:S(2)}, u32[]{:S(2)}) collective-permute-start(bf16[128,2048]{1,0:T(8,128)(2,1)S(1)} %get-tuple-element.20), channel_id=1, source_target_pairs={{0,16},{16,0},{1,17},{17,1},{2,18},{18,2},{3,19},{19,3},{4,20},{20... | collective-permute-start | bytes 1572872 | tf_op jit(solution)/shard_map/ppermute | solution.py:151
  68.7 2.6 %experts.6 = (bf16[128,2048]{1,0:T(8,128)(2,1)S(1)}, f32[128,2048]{1,0:T(8,128)S(1)}) custom-call(bf16[128,2176]{1,0:T(8,128)(2,1)S(1)} %collective-permute-done.3.refs_0_, bf16[128,2176]{1,0:T(8,128)(2,1)S(1)} %collective-permute-done.4.refs_1_, bf16[704,2048]{1,0:T(8,128)(2,1)S(1)} %bitcast.21, bf16[704,2048]{1,0:T(8,128)(2,1)S(1)} %bitcast.26, ...), custom_call_target="tpu_custom_call" | custom-call | flops 2214592512 | bytes 8650752 | tf_op jit(solution)/shard_map/experts/pallas_call | solution.py:25
  71.7 1.6 %collective-permute-start.17 = (bf16[128,2048]{1,0:T(8,128)(2,1)S(1)}, bf16[128,2048]{1,0:T(8,128)(2,1)S(1)}, u32[]{:S(2)}, u32[]{:S(2)}) collective-permute-start(bf16[128,2048]{1,0:T(8,128)(2,1)S(1)} %add_convert_fusion), channel_id=1, source_target_pairs={{0,4},{5,1},{4,8},{9,5},{8,12},{13,9},{12,14},{15,13},{14,10},{11,... | collective-permute-start | bytes 1572872 | tf_op jit(solution)/shard_map/ppermute | solution.py:148
  73.3 2.2 %experts.5.refs_0_ = f32[128,2048]{1,0:T(8,128)S(1)} custom-call(bf16[128,2176]{1,0:T(8,128)(2,1)S(1)} %prologue.1.refs_0_, bf16[704,2048]{1,0:T(8,128)(2,1)S(1)} %bitcast.22, bf16[704,2048]{1,0:T(8,128)(2,1)S(1)} %bitcast.27, bf16[704,2048]{1,0:T(8,128)(2,1)S(1)} %bitcast.32), custom_call_target="tpu_custom_call" | custom-call | flops 1107296256 | bytes 8650752 | tf_op jit(solution)/shard_map/experts/pallas_call | solution.py:25
  75.5 5.1 %collective-permute-done.1.refs_2_ = bf16[128,2048]{1,0:T(8,128)(2,1)S(1)} collective-permute-done((bf16[128,2048]{1,0:T(8,128)(2,1)S(1)}, bf16[128,2048]{1,0:T(8,128)(2,1)S(1)}, u32[]{:S(2)}, u32[]{:S(2)}) %collective-permute-start.1) | collective-permute-done | bytes 524320 | tf_op jit(solution)/shard_map/ppermute | solution.py:151
  81.1 1.6 %collective-permute-start.18 = (bf16[128,1024]{1,0:T(8,128)(2,1)S(1)}, bf16[128,1024]{1,0:T(8,128)(2,1)S(1)}, u32[]{:S(2)}, u32[]{:S(2)}) collective-permute-start(bf16[128,1024]{1,0:T(8,128)(2,1)S(1)} %get-tuple-element.31), channel_id=1, source_target_pairs={{0,4},{5,1},{4,8},{9,5},{8,12},{13,9},{12,14},{15,13},{14,10},{11,... | collective-permute-start | bytes 786440 | tf_op jit(solution)/shard_map/ppermute | solution.py:148
  82.9 4.6 %collective-permute-done.18 = bf16[128,1024]{1,0:T(8,128)(2,1)S(1)} collective-permute-done((bf16[128,1024]{1,0:T(8,128)(2,1)S(1)}, bf16[128,1024]{1,0:T(8,128)(2,1)S(1)}, u32[]{:S(2)}, u32[]{:S(2)}) %collective-permute-start.18) | collective-permute-done | bytes 262176 | tf_op jit(solution)/shard_map/ppermute | solution.py:148
  87.5 2.2 %collective-permute-done.19 = bf16[128,1024]{1,0:T(8,128)(2,1)S(1)} collective-permute-done((bf16[128,1024]{1,0:T(8,128)(2,1)S(1)}, bf16[128,1024]{1,0:T(8,128)(2,1)S(1)}, u32[]{:S(2)}, u32[]{:S(2)}) %collective-permute-start.19) | collective-permute-done | bytes 262176 | tf_op jit(solution)/shard_map/ppermute | solution.py:149
  89.7 0.8 add_convert_fusion.1
  (46 shorter events, 5.1 us)
Async XLA Ops:
  0.0 1.0 %copy-start.7 = (bf16[128,2048]{1,0:T(8,128)(2,1)S(1)}, bf16[128,2048]{1,0:T(8,128)(2,1)}, u32[]{:S(2)}) copy-start(bf16[128,2048]{1,0:T(8,128)(2,1)} %refs_0_.1) | copy-start | bytes 1572868
  1.0 0.8 copy-start.8
  1.8 0.7 copy-start.9
  2.5 0.7 copy-start.10
  3.2 0.7 copy-start.11
  4.4 10.6 %collective-permute-start.3 = (bf16[128,2176]{1,0:T(8,128)(2,1)S(1)}, bf16[128,2176]{1,0:T(8,128)(2,1)S(1)}, u32[]{:S(2)}, u32[]{:S(2)}) collective-permute-start(bf16[128,2176]{1,0:T(8,128)(2,1)S(1)} %prologue.1.refs_0_), channel_id=1, source_target_pairs={{0,4},{5,1},{4,8},{9,5},{8,12},{13,9},{12,14},{15,13},{14,10},{11,... | collective-permute-start | bytes 1671176 | tf_op jit(solution)/shard_map/ppermute | solution.py:148
  14.9 9.5 %collective-permute-start.6 = (bf16[128,2176]{1,0:T(8,128)(2,1)S(1)}, bf16[128,2176]{1,0:T(8,128)(2,1)S(1)}, u32[]{:S(2)}, u32[]{:S(2)}) collective-permute-start(bf16[128,2176]{1,0:T(8,128)(2,1)S(1)} %collective-permute-done.3.refs_0_), channel_id=1, source_target_pairs={{0,4},{5,1},{4,8},{9,5},{8,12},{13,9},{12,14},{15,13},{14,10},{11,... | collective-permute-start | bytes 1671176 | tf_op jit(solution)/shard_map/ppermute | solution.py:148
  24.5 9.5 %collective-permute-start.9 = (bf16[128,2176]{1,0:T(8,128)(2,1)S(1)}, bf16[128,2176]{1,0:T(8,128)(2,1)S(1)}, u32[]{:S(2)}, u32[]{:S(2)}) collective-permute-start(bf16[128,2176]{1,0:T(8,128)(2,1)S(1)} %collective-permute-done.6.refs_0_), channel_id=1, source_target_pairs={{0,4},{5,1},{4,8},{9,5},{8,12},{13,9},{12,14},{15,13},{14,10},{11,... | collective-permute-start | bytes 1671176 | tf_op jit(solution)/shard_map/ppermute | solution.py:148
  34.0 6.6 %collective-permute-start.12 = (bf16[64,2176]{1,0:T(8,128)(2,1)S(1)}, bf16[64,2176]{1,0:T(8,128)(2,1)S(1)}, u32[]{:S(2)}, u32[]{:S(2)}) collective-permute-start(bf16[64,2176]{1,0:T(8,128)(2,1)S(1)} %constant_dynamic-slice_fusion), channel_id=1, source_target_pairs={{0,4},{5,1},{4,8},{9,5},{8,12},{13,9},{12,14},{15,13},{14,10},{11,... | collective-permute-start | bytes 835592 | tf_op jit(solution)/shard_map/ppermute | solution.py:148
  36.2 16.0 %collective-permute-start.10 = (bf16[128,2176]{1,0:T(8,128)(2,1)S(1)}, bf16[128,2176]{1,0:T(8,128)(2,1)S(1)}, u32[]{:S(2)}, u32[]{:S(2)}) collective-permute-start(bf16[128,2176]{1,0:T(8,128)(2,1)S(1)} %collective-permute-done.9.refs_0_), channel_id=1, source_target_pairs={{0,1},{1,0},{2,3},{3,2},{4,5},{5,4},{6,7},{7,6},{8,9},{9,8},{10,11... | collective-permute-start | bytes 1671176 | tf_op jit(solution)/shard_map/ppermute | solution.py:150
  40.6 1.6 %collective-permute-start.13 = (bf16[64,2176]{1,0:T(8,128)(2,1)S(1)}, bf16[64,2176]{1,0:T(8,128)(2,1)S(1)}, u32[]{:S(2)}, u32[]{:S(2)}) collective-permute-start(bf16[64,2176]{1,0:T(8,128)(2,1)S(1)} %collective-permute-done.12.refs_0_), channel_id=1, source_target_pairs={{0,1},{1,0},{2,3},{3,2},{4,5},{5,4},{6,7},{7,6},{8,9},{9,8},{10,11... | collective-permute-start | bytes 835592 | tf_op jit(solution)/shard_map/ppermute | solution.py:150
  42.2 1.8 %copy-start = (bf16[1,2048,704]{1,2,0:T(8,128)(2,1)S(1)}, bf16[1,2048,704]{1,2,0:T(8,128)(2,1)}, u32[]{:S(2)}) copy-start(bf16[1,2048,704]{1,2,0:T(8,128)(2,1)} %param.16) | copy-start | bytes 8650756
  44.0 1.8 %copy-start.2 = (bf16[1,2048,704]{1,2,0:T(8,128)(2,1)S(1)}, bf16[1,2048,704]{1,2,0:T(8,128)(2,1)}, u32[]{:S(2)}) copy-start(bf16[1,2048,704]{1,2,0:T(8,128)(2,1)} %param.17) | copy-start | bytes 8650756
  45.8 1.8 %copy-start.3 = (bf16[1,704,2048]{2,1,0:T(8,128)(2,1)S(1)}, bf16[1,704,2048]{2,1,0:T(8,128)(2,1)}, u32[]{:S(2)}) copy-start(bf16[1,704,2048]{2,1,0:T(8,128)(2,1)} %param.18) | copy-start | bytes 8650756
  49.9 5.4 %collective-permute-start.14 = (bf16[64,2048]{1,0:T(8,128)(2,1)S(1)}, bf16[64,2048]{1,0:T(8,128)(2,1)S(1)}, u32[]{:S(2)}, u32[]{:S(2)}) collective-permute-start(bf16[64,2048]{1,0:T(8,128)(2,1)S(1)} %get-tuple-element.30), channel_id=1, source_target_pairs={{0,1},{1,0},{2,3},{3,2},{4,5},{5,4},{6,7},{7,6},{8,9},{9,8},{10,11... | collective-permute-start | bytes 786440 | tf_op jit(solution)/shard_map/ppermute | solution.py:150
  50.1 15.2 %collective-permute-start = (bf16[128,2176]{1,0:T(8,128)(2,1)S(1)}, bf16[128,2176]{1,0:T(8,128)(2,1)S(1)}, u32[]{:S(2)}, u32[]{:S(2)}) collective-permute-start(bf16[128,2176]{1,0:T(8,128)(2,1)S(1)} %prologue.1.refs_0_), channel_id=1, source_target_pairs={{0,16},{16,0},{1,17},{17,1},{2,18},{18,2},{3,19},{19,3},{4,20},{20... | collective-permute-start | bytes 1671176 | tf_op jit(solution)/shard_map/ppermute | solution.py:151
  52.1 4.9 %collective-permute-start.7 = (bf16[128,2176]{1,0:T(8,128)(2,1)S(1)}, bf16[128,2176]{1,0:T(8,128)(2,1)S(1)}, u32[]{:S(2)}, u32[]{:S(2)}) collective-permute-start(bf16[128,2176]{1,0:T(8,128)(2,1)S(1)} %collective-permute-done.6.refs_0_), channel_id=1, source_target_pairs={{0,1},{1,0},{2,3},{3,2},{4,5},{5,4},{6,7},{7,6},{8,9},{9,8},{10,11... | collective-permute-start | bytes 1671176 | tf_op jit(solution)/shard_map/ppermute | solution.py:150
  54.8 7.0 %collective-permute-start.11 = (bf16[128,2048]{1,0:T(8,128)(2,1)S(1)}, bf16[128,2048]{1,0:T(8,128)(2,1)S(1)}, u32[]{:S(2)}, u32[]{:S(2)}) collective-permute-start(bf16[128,2048]{1,0:T(8,128)(2,1)S(1)} %get-tuple-element.28), channel_id=1, source_target_pairs={{0,1},{1,0},{2,3},{3,2},{4,5},{5,4},{6,7},{7,6},{8,9},{9,8},{10,11... | collective-permute-start | bytes 1572872 | tf_op jit(solution)/shard_map/ppermute | solution.py:150
  55.3 6.4 %collective-permute-start.15 = (bf16[64,2048]{1,0:T(8,128)(2,1)S(1)}, bf16[64,2048]{1,0:T(8,128)(2,1)S(1)}, u32[]{:S(2)}, u32[]{:S(2)}) collective-permute-start(bf16[64,2048]{1,0:T(8,128)(2,1)S(1)} %add_convert_fusion.2), channel_id=1, source_target_pairs={{0,4},{5,1},{4,8},{9,5},{8,12},{13,9},{12,14},{15,13},{14,10},{11,... | collective-permute-start | bytes 786440 | tf_op jit(solution)/shard_map/ppermute | solution.py:148
  57.0 11.8 %collective-permute-start.4 = (bf16[128,2176]{1,0:T(8,128)(2,1)S(1)}, bf16[128,2176]{1,0:T(8,128)(2,1)S(1)}, u32[]{:S(2)}, u32[]{:S(2)}) collective-permute-start(bf16[128,2176]{1,0:T(8,128)(2,1)S(1)} %collective-permute-done.3.refs_0_), channel_id=1, source_target_pairs={{0,1},{1,0},{2,3},{3,2},{4,5},{5,4},{6,7},{7,6},{8,9},{9,8},{10,11... | collective-permute-start | bytes 1671176 | tf_op jit(solution)/shard_map/ppermute | solution.py:150
  57.0 8.3 %copy-start.5 = (bf16[2,2048,176]{1,2,0:T(8,128)(2,1)S(1)}, bf16[2,2048,176]{1,2,0:T(8,128)(2,1)}, u32[]{:S(2)}) copy-start(bf16[2,2048,176]{1,2,0:T(8,128)(2,1)} %param.20) | copy-start | bytes 4325380
  57.0 8.3 %copy-start.6 = (bf16[2,176,2048]{2,1,0:T(8,128)(2,1)S(1)}, bf16[2,176,2048]{2,1,0:T(8,128)(2,1)}, u32[]{:S(2)}) copy-start(bf16[2,176,2048]{2,1,0:T(8,128)(2,1)} %param.21) | copy-start | bytes 4325380
  59.6 5.6 %copy-start.4 = (bf16[2,2048,176]{1,2,0:T(8,128)(2,1)S(1)}, bf16[2,2048,176]{1,2,0:T(8,128)(2,1)}, u32[]{:S(2)}) copy-start(bf16[2,2048,176]{1,2,0:T(8,128)(2,1)} %param.19) | copy-start | bytes 4325380
  59.6 11.8 %collective-permute-start.8 = (bf16[128,2048]{1,0:T(8,128)(2,1)S(1)}, bf16[128,2048]{1,0:T(8,128)(2,1)S(1)}, u32[]{:S(2)}, u32[]{:S(2)}) collective-permute-start(bf16[128,2048]{1,0:T(8,128)(2,1)S(1)} %get-tuple-element.26), channel_id=1, source_target_pairs={{0,1},{1,0},{2,3},{3,2},{4,5},{5,4},{6,7},{7,6},{8,9},{9,8},{10,11... | collective-permute-start | bytes 1572872 | tf_op jit(solution)/shard_map/ppermute | solution.py:150
  61.9 6.8 %copy-start.1 = (bf16[1,2048,704]{1,2,0:T(8,128)(2,1)S(1)}, bf16[1,2048,704]{1,2,0:T(8,128)(2,1)}, u32[]{:S(2)}) copy-start(bf16[1,2048,704]{1,2,0:T(8,128)(2,1)} %param.16) | copy-start | bytes 8650756
  61.9 9.5 %collective-permute-start.16 = (bf16[128,2048]{1,0:T(8,128)(2,1)S(1)}, bf16[128,2048]{1,0:T(8,128)(2,1)S(1)}, u32[]{:S(2)}, u32[]{:S(2)}) collective-permute-start(bf16[128,2048]{1,0:T(8,128)(2,1)S(1)} %first_add.1), channel_id=1, source_target_pairs={{0,4},{5,1},{4,8},{9,5},{8,12},{13,9},{12,14},{15,13},{14,10},{11,... | collective-permute-start | bytes 1572872 | tf_op jit(solution)/shard_map/ppermute | solution.py:148
  66.9 13.7 %collective-permute-start.1 = (bf16[128,2048]{1,0:T(8,128)(2,1)S(1)}, bf16[128,2048]{1,0:T(8,128)(2,1)S(1)}, u32[]{:S(2)}, u32[]{:S(2)}) collective-permute-start(bf16[128,2048]{1,0:T(8,128)(2,1)S(1)} %get-tuple-element.20), channel_id=1, source_target_pairs={{0,16},{16,0},{1,17},{17,1},{2,18},{18,2},{3,19},{19,3},{4,20},{20... | collective-permute-start | bytes 1572872 | tf_op jit(solution)/shard_map/ppermute | solution.py:151
  71.4 9.4 %collective-permute-start.5 = (bf16[128,2048]{1,0:T(8,128)(2,1)S(1)}, bf16[128,2048]{1,0:T(8,128)(2,1)S(1)}, u32[]{:S(2)}, u32[]{:S(2)}) collective-permute-start(bf16[128,2048]{1,0:T(8,128)(2,1)S(1)} %get-tuple-element.24), channel_id=1, source_target_pairs={{0,1},{1,0},{2,3},{3,2},{4,5},{5,4},{6,7},{7,6},{8,9},{9,8},{10,11... | collective-permute-start | bytes 1572872 | tf_op jit(solution)/shard_map/ppermute | solution.py:150
  71.7 9.2 %collective-permute-start.17 = (bf16[128,2048]{1,0:T(8,128)(2,1)S(1)}, bf16[128,2048]{1,0:T(8,128)(2,1)S(1)}, u32[]{:S(2)}, u32[]{:S(2)}) collective-permute-start(bf16[128,2048]{1,0:T(8,128)(2,1)S(1)} %add_convert_fusion), channel_id=1, source_target_pairs={{0,4},{5,1},{4,8},{9,5},{8,12},{13,9},{12,14},{15,13},{14,10},{11,... | collective-permute-start | bytes 1572872 | tf_op jit(solution)/shard_map/ppermute | solution.py:148
  80.7 2.1 %collective-permute-start.2 = (bf16[128,1024]{1,0:T(8,128)(2,1)S(1)}, bf16[128,1024]{1,0:T(8,128)(2,1)S(1)}, u32[]{:S(2)}, u32[]{:S(2)}) collective-permute-start(bf16[128,1024]{1,0:T(8,128)(2,1)S(1)} %get-tuple-element.22), channel_id=1, source_target_pairs={{0,1},{1,0},{2,3},{3,2},{4,5},{5,4},{6,7},{7,6},{8,9},{9,8},{10,11... | collective-permute-start | bytes 786440 | tf_op jit(solution)/shard_map/ppermute | solution.py:150
  81.1 6.4 %collective-permute-start.18 = (bf16[128,1024]{1,0:T(8,128)(2,1)S(1)}, bf16[128,1024]{1,0:T(8,128)(2,1)S(1)}, u32[]{:S(2)}, u32[]{:S(2)}) collective-permute-start(bf16[128,1024]{1,0:T(8,128)(2,1)S(1)} %get-tuple-element.31), channel_id=1, source_target_pairs={{0,4},{5,1},{4,8},{9,5},{8,12},{13,9},{12,14},{15,13},{14,10},{11,... | collective-permute-start | bytes 786440 | tf_op jit(solution)/shard_map/ppermute | solution.py:148
  82.7 7.0 %collective-permute-start.19 = (bf16[128,1024]{1,0:T(8,128)(2,1)S(1)}, bf16[128,1024]{1,0:T(8,128)(2,1)S(1)}, u32[]{:S(2)}, u32[]{:S(2)}) collective-permute-start(bf16[128,1024]{1,0:T(8,128)(2,1)S(1)} %get-tuple-element.32), channel_id=1, source_target_pairs={{0,5},{5,0},{4,9},{9,4},{8,13},{13,8},{12,15},{15,12},{14,11},{11,... | collective-permute-start | bytes 786440 | tf_op jit(solution)/shard_map/ppermute | solution.py:149

commit v2 on v1

v2 whole, which is shorter than its diff:
```python
import jax
import jax.numpy as jnp
from jax import lax
from jax.experimental import pallas as pl
from jax.experimental.pallas import tpu as pltpu
from jax.sharding import PartitionSpec as P


epsilon = 1e-06
LANES = 128
MIB = 2**20
NT = (((1,), (1,)), ((), ()))
TN = (((0,), (0,)), ((), ()))


def dot(a, b, dims):
    return lax.dot_general(a, b, dims, preferred_element_type=jnp.float32)


def ring_order(count):
    return list(range(0, count, 2)) + list(range(count - 1, 0, -2))


def call(body, outs, args, limit, flops=0, moved=0, scratch=()):
    vmem = pl.BlockSpec(memory_space=pltpu.VMEM)
    return pl.pallas_call(
        body,
        out_shape=outs,
        in_specs=[vmem] * len(args),
        out_specs=jax.tree.map(lambda _: vmem, outs),
        scratch_shapes=scratch,
        compiler_params=pltpu.CompilerParams(vmem_limit_bytes=limit * MIB),
        cost_estimate=pl.CostEstimate(flops=flops, bytes_accessed=moved, transcendentals=0),
    )(*args)


def lead_body(out):
    out[...] = jnp.zeros_like(out)


def prologue_body(expert_count, lead, tokens, gain, router, ids, modality, packed, part):
    width = tokens.shape[1]
    values = tokens[...].astype(jnp.float32)
    scale = lax.rsqrt(jnp.mean(values * values, axis=1, keepdims=True) + epsilon)
    normed = (values * scale * gain[...]).astype(jnp.bfloat16)
    packed[:, :width] = normed
    scores = 1.0 / (1.0 + jnp.exp(-dot(router[...], normed, NT)))
    which = lax.broadcasted_iota(jnp.int32, scores.shape, 0)
    chosen = which == ids[0:1, :]
    for k in range(1, ids.shape[0]):
        chosen = chosen | (which == ids[k : k + 1, :])
    scores = jnp.where(chosen, scores, 0.0)
    weights = scores / jnp.sum(scores, axis=0, keepdims=True)
    rounded = weights.astype(jnp.bfloat16).astype(jnp.float32)
    image = (modality[...] == 1).astype(jnp.float32)
    rows = packed.shape[1] - width - 2 * expert_count
    first = lax.broadcasted_iota(jnp.int32, (rows, image.shape[1]), 0) == 0
    table = jnp.concatenate([rounded, weights - rounded, jnp.where(first, image, 0.0)], axis=0)
    packed[:, width:] = table.T.astype(jnp.bfloat16)
    half = part.shape[0]
    start = pl.multiple_of(lax.axis_index("tensor") * half, half)
    part[...] = packed[pl.ds(start, half), :]


def side_rows(rows, width, lanes):
    side = rows[:, width:]
    lane = lax.broadcasted_iota(jnp.int32, (8, side.shape[1]), 1)
    picked = lane == lanes[0]
    for other in lanes[1:]:
        picked = picked | (lane == other)
    return dot(picked.astype(jnp.bfloat16), side, NT)[0:1, :]


def gated(gate, up, factor):
    return (gate / (1.0 + jnp.exp(-gate)) * up * factor).astype(jnp.bfloat16)


def expert_hidden(expert_count, rows, gate, up):
    width = gate.shape[1]
    me = lax.axis_index("expert")
    factor = side_rows(rows, width, (me, me + expert_count))
    rows = rows[:, :width]
    return gated(dot(gate[...], rows, NT), dot(up[...], rows, NT), factor)


def pair_body(expert_count, up_own, down_own, up_other, down_other, gate, up, down, keep, give, rows):
    half = up_own.shape[0]
    mine = pl.multiple_of(lax.axis_index("tensor") * half, half)
    theirs = pl.multiple_of((1 - lax.axis_index("tensor")) * half, half)
    for base, own, other in ((0, up_own, up_other), (2 * half, down_own, down_other)):
        rows[pl.ds(base + mine, half), :] = own[...]
        rows[pl.ds(base + theirs, half), :] = other[...]
    split_down(expert_hidden(expert_count, rows[...], gate, up), down, keep, give)


def column_halves(hidden, down):
    half = down.shape[1] // 2
    core = lax.axis_index("tensor")
    places = [pl.ds(pl.multiple_of(i * half, half), half) for i in (core, 1 - core)]
    return [dot(hidden, down[:, place], TN) for place in places]


def split_down(hidden, down, keep, give):
    mine, theirs = column_halves(hidden, down)
    keep[...] = mine
    give[...] = theirs.astype(give.dtype)


def own_body(expert_count, own, gate, up, down, mine, theirs):
    hidden = expert_hidden(expert_count, own[...], gate, up)
    mine[...], theirs[...] = column_halves(hidden, down)


def far_body(expert_count, up_own, down_own, up_other, down_other, gate, up, down, keep, give, rows):
    part = up_own.shape[0]
    mine = pl.multiple_of(lax.axis_index("tensor") * 2 * part, 2 * part)
    theirs = pl.multiple_of((1 - lax.axis_index("tensor")) * 2 * part, 2 * part)
    rows[pl.ds(mine, part), :] = up_own[...]
    rows[pl.ds(mine + part, part), :] = down_own[...]
    rows[pl.ds(theirs, part), :] = up_other[...]
    rows[pl.ds(theirs + part, part), :] = down_other[...]
    split_down(expert_hidden(expert_count, rows[...], gate, up), down, keep, give)


def shared_body(expert_count, own, other, mine, theirs, gate, up, down, keep, give):
    width = gate.shape[1]
    rows = jnp.concatenate([own[...], other[...]], axis=0)
    image = side_rows(rows, width, (2 * expert_count,))
    rows = rows[:, :width]
    gate_value, up_value = dot(gate[...], rows, NT), dot(up[...], rows, NT)
    kind = lax.broadcasted_iota(jnp.int32, gate_value.shape, 0) < gate_value.shape[0] // 2
    hidden = gated(gate_value, up_value, jnp.where(kind, image, 1.0 - image))
    count = own.shape[0]
    for out, result, first in zip((keep, give), column_halves(hidden, down), (mine, theirs)):
        out[:count, :] = (result[:count] + first[...]).astype(out.dtype)
        out[count:, :] = result[count:].astype(out.dtype)


def far_add_body(keep, recv, upward, downward):
    half = upward.shape[0]
    total = keep[...] + recv[...].astype(jnp.float32)
    upward[...] = total[:half].astype(upward.dtype)
    downward[...] = total[half:].astype(downward.dtype)


def sum_body(bases, keep, recv, *refs):
    outs = refs[-len(bases) :]
    for index, (base, out) in enumerate(zip(bases, outs)):
        place = slice(base, base + out.shape[0])
        total = keep[place, :] + recv[place, :].astype(jnp.float32)
        if len(refs) > len(outs):
            total = total + refs[index][...].astype(jnp.float32)
        out[...] = total.astype(out.dtype)


def total_body(local, other, ahead_one, ahead_two, back_one, back_two, out):
    half = ahead_one.shape[0]
    for index, (one, two) in enumerate(((ahead_one, back_one), (ahead_two, back_two))):
        place = slice(index * half, index * half + half)
        total = local[place, :] + other[place, :].astype(jnp.float32)
        total = total + one[...].astype(jnp.float32) + two[...].astype(jnp.float32)
        out[place, :] = total.astype(out.dtype)


def per_device(
    tokens,
    norm_gain,
    router,
    expert_ids,
    modality,
    expert_gate,
    expert_up,
    expert_down,
    shared_gate,
    shared_up,
    shared_down,
):
    count, width = tokens.shape
    half, columns = count // 2, width // 2
    quarter = half // 2
    experts = lax.axis_size("expert")
    side = -(-(2 * experts + 1) // LANES) * LANES
    middle = experts // 2
    shape = jax.ShapeDtypeStruct
    f32, bf16 = jnp.float32, jnp.bfloat16

    order = ring_order(experts)
    onward = list(zip(order, order[1:] + order[:1]))
    backward = [(b, a) for a, b in onward]
    ahead = lambda x: lax.ppermute(x, "expert", onward)
    back = lambda x: lax.ppermute(x, "expert", backward)
    swap = lambda x: lax.ppermute(x, "tensor", [(0, 1), (1, 0)])
    dp_swap = lambda x: lax.ppermute(x, "dp", [(0, 1), (1, 0)])

    hidden_units = expert_down.shape[1]
    shared_units = 2 * shared_down.shape[1]
    stored = (
        expert_gate[0].T,
        expert_up[0].T,
        expert_down[0],
        jnp.swapaxes(shared_gate, 1, 2).reshape(shared_units, width),
        jnp.swapaxes(shared_up, 1, 2).reshape(shared_units, width),
        shared_down.reshape(shared_units, width),
    )
    inputs = (tokens, norm_gain[None, :], router.T, expert_ids.T, modality[None, :])
    lead = call(lead_body, shape((8, LANES), f32), (), 1, 2**34, MIB)
    own, part = call(
        lambda *refs: prologue_body(experts, *refs),
        (shape((count, width + side), bf16), shape((half, width + side), bf16)),
        (lead, *inputs),
        8,
        4 * MIB,
        MIB,
    )
    other = dp_swap(own)
    up_block, down_block = ahead(part), back(part)
    weights = stored

    def experts_of(body, *blocks):
        rows = 4 * blocks[0].shape[0]
        return call(
            lambda *refs: body(experts, *refs),
            (shape((rows, columns), f32), shape((rows, columns), bf16)),
            (*blocks, *weights[:3]),
            16,
            6 * rows * width * hidden_units,
            6 * width * hidden_units,
            [pltpu.VMEM((rows, width + side), bf16)],
        )

    def own_part(own):
        return call(
            lambda *refs: own_body(experts, *refs),
            (shape((count, columns), f32),) * 2,
            (own, *weights[:3]),
            16,
            6 * count * width * hidden_units,
            6 * width * hidden_units,
        )

    def shared_part(*values):
        return call(
            lambda *refs: shared_body(experts, *refs),
            (shape((2 * count, columns), f32), shape((2 * count, columns), bf16)),
            (*values, *weights[3:]),
            16,
            12 * shared_units * count * width,
            6 * width * shared_units,
        )

    def sums(k, bases, *arrived):
        return call(
            lambda *refs: sum_body(bases, *refs),
            (shape((half, columns), bf16),) * len(bases),
            (keep[k], recv[k], *arrived),
            8,
        )

    keep, recv = {}, {}
    own_sums = own_part(own)
    for k in range(1, middle + 1):
        rows = [up_block, down_block]
        if k == middle - 1:
            up_block, down_block = up_block[:quarter], down_block[quarter:]
        if k < middle:
            up_block = ahead(up_block)
            down_block = back(down_block)
        rows += [swap(rows[0]), swap(rows[1])]
        keep[k], give = experts_of(pair_body if k < middle else far_body, *rows)
        recv[k] = swap(give)

    ahead_base, back_base = count, 0
    short = sums(middle - 1, (ahead_base + half, back_base))
    long = call(far_add_body, (shape((half, columns), bf16),) * 2, (keep[middle], recv[middle]), 8)

    def travel(pair):
        return ahead(pair[0]), back(pair[1])

    for k in range(middle - 1, 0, -1):
        short = travel(short)
        long = travel(long)
        if k > 1:
            for way, base in enumerate((ahead_base + half, back_base)):
                part = sums(k - 1, (base,), short[way])
                short = (*part, short[1]) if way == 0 else (short[0], *part)
        for way, base in enumerate((ahead_base, back_base + half)):
            part = sums(k, (base,), long[way])
            long = (*part, long[1]) if way == 0 else (long[0], *part)
    long = travel(long)

    local, give = shared_part(own, other, *own_sums)
    local = local + swap(give).astype(f32)
    local_other = dp_swap(local[count:].astype(bf16))
    return call(
        total_body,
        shape((count, columns), bf16),
        (local, local_other, long[0], short[0], short[1], long[1]),
        8,
    )


def solution(mesh):
    in_specs = (
        P(("dp", "expert"), None),
        P(),
        P(),
        P(("dp", "expert"), None),
        P(("dp", "expert")),
        P("expert", None, "tensor"),
        P("expert", None, "tensor"),
        P("expert", "tensor", None),
        P(None, None, ("dp", "tensor")),
        P(None, None, ("dp", "tensor")),
        P(None, ("dp", "tensor"), None),
    )
    out_specs = P(("dp", "expert"), "tensor")

    return jax.shard_map(
        per_device, mesh=mesh, in_specs=in_specs, out_specs=out_specs, check_vma=False
    )
```

time: 91 us -> 79.5 us (0.87)
  waiting for transfers between devices: 43.6 us -> 31.1 us
  starting transfers between devices: 21.4 us -> 30.7 us
  local copies, waits for them, and re-layouts: 9.32 us -> 1.15 us
  Pallas kernels: 15 us -> 16 us
    ppermute x9 -> x22, starting transfers between devices: 16.1 us -> 24.6 us  [the longest x11 18 us: per_device(): back = lambda x: lax.ppermute(x, 'expert', backward)]
    unnamed x24 -> x22, local copies, waits for them, and re-layouts: 9.3 us -> 1.09 us
    ppermute x2, waiting for transfers between devices: 6.72 us -> 0.01 us  [per_device(): dp_swap = lambda x: lax.ppermute(x, 'dp', [(0, 1), (1, 0)])]
    ppermute x9 -> x22, waiting for transfers between devices: 35.4 us -> 31 us  [the longest x11 22.7 us: per_device(): back = lambda x: lax.ppermute(x, 'expert', backward)]
    ppermute x9 -> x13, waiting for transfers between devices: 1.58 us -> 0.03 us  [per_device(): swap = lambda x: lax.ppermute(x, 'tensor', [(0, 1), (1, 0)])]
    ppermute x9 -> x13, starting transfers between devices: 1.49 us -> 2.92 us  [per_device(): swap = lambda x: lax.ppermute(x, 'tensor', [(0, 1), (1, 0)])]
    convert_element_type x3 -> x0, other arithmetic: 1.08 us -> none  [the longest x1 0.85 us: per_device(): return total.astype(bf16)]
    pallas_call x10 -> x21, Pallas kernels: 15 us -> 16 us  [call(): pl.pallas_call(body, out_shape=outs, in_specs=[vmem] * len(args), out_spe...]
  transfers between devices with their start and end apart: 20 -> 37, of which waited for: 11 -> 13; matrix products, arithmetic and copies ran while one was open for 0% -> 0% of each run, Pallas kernels for 16% -> 18%
where the time goes in v2:
time: 79.5 us; the launch traced here: 79.4 us
  waiting for transfers between devices  31.1 us (39%)
  starting transfers between devices  30.7 us (39%)
  Pallas kernels  16 us (20%)
  local copies, waits for them, and re-layouts  1.15 us (1%)
    ppermute x11, waiting for transfers between devices, per_device(): back = lambda x: lax.ppermute(x, 'expert', backward)  22.7 us
    ppermute x11, starting transfers between devices, per_device(): back = lambda x: lax.ppermute(x, 'expert', backward)  18 us
    pallas_call x21, Pallas kernels, call(): pl.pallas_call(body, out_shape=outs, in_specs=[vmem] * len(args), out_spe...  16 us
    ppermute x11, waiting for transfers between devices, per_device(): ahead = lambda x: lax.ppermute(x, 'expert', onward)  8.28 us
    ppermute x11, starting transfers between devices, per_device(): ahead = lambda x: lax.ppermute(x, 'expert', onward)  6.58 us
    ppermute x2, starting transfers between devices, per_device(): dp_swap = lambda x: lax.ppermute(x, 'dp', [(0, 1), (1, 0)])  3.14 us
    ppermute x13, starting transfers between devices, per_device(): swap = lambda x: lax.ppermute(x, 'tensor', [(0, 1), (1, 0)])  2.92 us
  transfers between devices with their start and end apart: 37, of which 13 were waited for; matrix products, arithmetic and copies ran while one was open for 0% of the time, Pallas kernels for 18%

profile of v2, /device:TPU:0, one launch (start us, length us, event | category | flops | bytes accessed | tf_op | source)
XLA Modules:
  0.0 79.4 jit_solution(15523087874486883798)
XLA Ops:
  1.7 3.0 %collective-permute-start.4 = (bf16[64,2176]{1,0:T(8,128)(2,1)S(1)}, bf16[64,2176]{1,0:T(8,128)(2,1)S(1)}, u32[]{:S(2)}, u32[]{:S(2)}) collective-permute-start(bf16[64,2176]{1,0:T(8,128)(2,1)S(1)} %get-tuple-element.28), channel_id=1, source_target_pairs={{4,0},{8,4},{12,8},{14,12},{10,14},{6,10},{2,6},{0,2},{5,1},{9,5},... | collective-permute-start | bytes 835592 | tf_op jit(solution)/shard_map/ppermute | solution.py:191
  4.9 6.6 %collective-permute-done.4.refs_1_ = bf16[64,2176]{1,0:T(8,128)(2,1)S(1)} collective-permute-done((bf16[64,2176]{1,0:T(8,128)(2,1)S(1)}, bf16[64,2176]{1,0:T(8,128)(2,1)S(1)}, u32[]{:S(2)}, u32[]{:S(2)}) %collective-permute-start.4) | collective-permute-done | bytes 278560 | tf_op jit(solution)/shard_map/ppermute | solution.py:191
  11.5 1.7 %collective-permute-start.9 = (bf16[64,2176]{1,0:T(8,128)(2,1)S(1)}, bf16[64,2176]{1,0:T(8,128)(2,1)S(1)}, u32[]{:S(2)}, u32[]{:S(2)}) collective-permute-start(bf16[64,2176]{1,0:T(8,128)(2,1)S(1)} %collective-permute-done.4.refs_1_), channel_id=1, source_target_pairs={{4,0},{8,4},{12,8},{14,12},{10,14},{6,10},{2,6},{0,2},{5,1},{9,5},... | collective-permute-start | bytes 835592 | tf_op jit(solution)/shard_map/ppermute | solution.py:191
  13.5 1.7 %collective-permute-start = (bf16[128,2176]{1,0:T(8,128)(2,1)S(1)}, bf16[128,2176]{1,0:T(8,128)(2,1)S(1)}, u32[]{:S(2)}, u32[]{:S(2)}) collective-permute-start(bf16[128,2176]{1,0:T(8,128)(2,1)S(1)} %get-tuple-element.23.refs_0_), channel_id=1, source_target_pairs={{0,16},{16,0},{1,17},{17,1},{2,18},{18,2},{3,19},{19,3},{4,20},{20... | collective-permute-start | bytes 1671176 | tf_op jit(solution)/shard_map/ppermute | solution.py:193
  15.2 4.1 %collective-permute-done.9.refs_1_ = bf16[64,2176]{1,0:T(8,128)(2,1)S(1)} collective-permute-done((bf16[64,2176]{1,0:T(8,128)(2,1)S(1)}, bf16[64,2176]{1,0:T(8,128)(2,1)S(1)}, u32[]{:S(2)}, u32[]{:S(2)}) %collective-permute-start.9) | collective-permute-done | bytes 278560 | tf_op jit(solution)/shard_map/ppermute | solution.py:191
  19.3 1.4 %collective-permute-start.14 = (bf16[64,2176]{1,0:T(8,128)(2,1)S(1)}, bf16[64,2176]{1,0:T(8,128)(2,1)S(1)}, u32[]{:S(2)}, u32[]{:S(2)}) collective-permute-start(bf16[64,2176]{1,0:T(8,128)(2,1)S(1)} %collective-permute-done.9.refs_1_), channel_id=1, source_target_pairs={{4,0},{8,4},{12,8},{14,12},{10,14},{6,10},{2,6},{0,2},{5,1},{9,5},... | collective-permute-start | bytes 835592 | tf_op jit(solution)/shard_map/ppermute | solution.py:191
  21.3 4.9 %collective-permute-done.14.refs_1_ = bf16[64,2176]{1,0:T(8,128)(2,1)S(1)} collective-permute-done((bf16[64,2176]{1,0:T(8,128)(2,1)S(1)}, bf16[64,2176]{1,0:T(8,128)(2,1)S(1)}, u32[]{:S(2)}, u32[]{:S(2)}) %collective-permute-start.14) | collective-permute-done | bytes 278560 | tf_op jit(solution)/shard_map/ppermute | solution.py:191
  26.3 1.0 %collective-permute-done.13.refs_0_ = bf16[64,2176]{1,0:T(8,128)(2,1)S(1)} collective-permute-done((bf16[64,2176]{1,0:T(8,128)(2,1)S(1)}, bf16[64,2176]{1,0:T(8,128)(2,1)S(1)}, u32[]{:S(2)}, u32[]{:S(2)}) %collective-permute-start.13) | collective-permute-done | bytes 278560 | tf_op jit(solution)/shard_map/ppermute | solution.py:190
  27.3 2.2 %shard_map.111 = (f32[128,1024]{1,0:T(8,128)S(1)}, f32[128,1024]{1,0:T(8,128)S(1)}) custom-call(bf16[128,2176]{1,0:T(8,128)(2,1)S(1)} %get-tuple-element.23.refs_0_, bf16[704,2048]{1,0:T(8,128)(2,1)S(1)} %bitcast.18, bf16[704,2048]{1,0:T(8,128)(2,1)S(1)} %bitcast.23, bf16[704,2048]{1,0:T(8,128)(2,1)S(1)} %bitcast.28), custom_call_target="tpu_custom_call" | custom-call | flops 1107296256 | bytes 8650752 | tf_op jit(solution)/shard_map/pallas_call | solution.py:26
  30.7 1.7 %shard_map.112 = (f32[256,1024]{1,0:T(8,128)S(1)}, bf16[256,1024]{1,0:T(8,128)(2,1)S(1)}) custom-call(bf16[128,2176]{1,0:T(8,128)(2,1)S(1)} %get-tuple-element.23.refs_0_, bf16[128,2176]{1,0:T(8,128)(2,1)S(1)} %collective-permute-done.refs_1_, f32[128,1024]{1,0:T(8,128)S(1)} %get-tuple-element.24.refs_2_, f32[128,1024]{1,0:T(8,128)S(1)} %get-tuple-element.25.refs_3_, ...), custom_call_target="tpu_custom_call" | custom-call | flops 1107296256 | bytes 4325376 | tf_op jit(solution)/shard_map/pallas_call | solution.py:26
  32.4 1.6 %collective-permute-start.19 = (bf16[32,2176]{1,0:T(8,128)(2,1)S(1)}, bf16[32,2176]{1,0:T(8,128)(2,1)S(1)}, u32[]{:S(2)}, u32[]{:S(2)}) collective-permute-start(bf16[32,2176]{1,0:T(8,128)(2,1)S(1)} %slice.15), channel_id=1, source_target_pairs={{4,0},{8,4},{12,8},{14,12},{10,14},{6,10},{2,6},{0,2},{5,1},{9,5},... | collective-permute-start | bytes 417800 | tf_op jit(solution)/shard_map/ppermute | solution.py:191
  34.5 2.6 %shard_map.115 = (f32[256,1024]{1,0:T(8,128)S(1)}, bf16[256,1024]{1,0:T(8,128)(2,1)S(1)}) custom-call(bf16[64,2176]{1,0:T(8,128)(2,1)S(1)} %collective-permute-done.13.refs_0_, bf16[64,2176]{1,0:T(8,128)(2,1)S(1)} %collective-permute-done.14.refs_1_, bf16[64,2176]{1,0:T(8,128)(2,1)S(1)} %collective-permute-done.15.refs_2_, ...), custom_call_target="tpu_custom_call" | custom-call | flops 2214592512 | bytes 8650752 | tf_op jit(solution)/shard_map/pallas_call | solution.py:26
  37.2 0.9 %collective-permute-done.19.refs_1_ = bf16[32,2176]{1,0:T(8,128)(2,1)S(1)} collective-permute-done((bf16[32,2176]{1,0:T(8,128)(2,1)S(1)}, bf16[32,2176]{1,0:T(8,128)(2,1)S(1)}, u32[]{:S(2)}, u32[]{:S(2)}) %collective-permute-start.19) | collective-permute-done | bytes 139296 | tf_op jit(solution)/shard_map/ppermute | solution.py:191
  38.1 1.3 %collective-permute-done.18.refs_0_ = bf16[32,2176]{1,0:T(8,128)(2,1)S(1)} collective-permute-done((bf16[32,2176]{1,0:T(8,128)(2,1)S(1)}, bf16[32,2176]{1,0:T(8,128)(2,1)S(1)}, u32[]{:S(2)}, u32[]{:S(2)}) %collective-permute-start.18) | collective-permute-done | bytes 139296 | tf_op jit(solution)/shard_map/ppermute | solution.py:190
  39.9 2.6 %shard_map.114 = (f32[256,1024]{1,0:T(8,128)S(1)}, bf16[256,1024]{1,0:T(8,128)(2,1)S(1)}) custom-call(bf16[64,2176]{1,0:T(8,128)(2,1)S(1)} %collective-permute-done.8.refs_0_, bf16[64,2176]{1,0:T(8,128)(2,1)S(1)} %collective-permute-done.9.refs_1_, bf16[64,2176]{1,0:T(8,128)(2,1)S(1)} %collective-permute-done.10.refs_2_, ...), custom_call_target="tpu_custom_call" | custom-call | flops 2214592512 | bytes 8650752 | tf_op jit(solution)/shard_map/pallas_call | solution.py:26
  43.1 2.3 %shard_map.116 = (f32[128,1024]{1,0:T(8,128)S(1)}, bf16[128,1024]{1,0:T(8,128)(2,1)S(1)}) custom-call(bf16[32,2176]{1,0:T(8,128)(2,1)S(1)} %collective-permute-done.18.refs_0_, bf16[32,2176]{1,0:T(8,128)(2,1)S(1)} %collective-permute-done.19.refs_1_, bf16[32,2176]{1,0:T(8,128)(2,1)S(1)} %collective-permute-done.20.refs_2_, ...), custom_call_target="tpu_custom_call" | custom-call | flops 1107296256 | bytes 8650752 | tf_op jit(solution)/shard_map/pallas_call | solution.py:26
  45.6 2.6 %shard_map.113 = (f32[256,1024]{1,0:T(8,128)S(1)}, bf16[256,1024]{1,0:T(8,128)(2,1)S(1)}) custom-call(bf16[64,2176]{1,0:T(8,128)(2,1)S(1)} %collective-permute-done.3.refs_0_, bf16[64,2176]{1,0:T(8,128)(2,1)S(1)} %collective-permute-done.4.refs_1_, bf16[64,2176]{1,0:T(8,128)(2,1)S(1)} %collective-permute-done.5.refs_2_, ...), custom_call_target="tpu_custom_call" | custom-call | flops 2214592512 | bytes 8650752 | tf_op jit(solution)/shard_map/pallas_call | solution.py:26
  48.8 1.6 %collective-permute-start.33 = (bf16[64,1024]{1,0:T(8,128)(2,1)S(1)}, bf16[64,1024]{1,0:T(8,128)(2,1)S(1)}, u32[]{:S(2)}, u32[]{:S(2)}) collective-permute-start(bf16[64,1024]{1,0:T(8,128)(2,1)S(1)} %get-tuple-element.40), channel_id=1, source_target_pairs={{4,0},{8,4},{12,8},{14,12},{10,14},{6,10},{2,6},{0,2},{5,1},{9,5},... | collective-permute-start | bytes 393224 | tf_op jit(solution)/shard_map/ppermute | solution.py:191
  50.9 3.4 %collective-permute-done.33.refs_2_ = bf16[64,1024]{1,0:T(8,128)(2,1)S(1)} collective-permute-done((bf16[64,1024]{1,0:T(8,128)(2,1)S(1)}, bf16[64,1024]{1,0:T(8,128)(2,1)S(1)}, u32[]{:S(2)}, u32[]{:S(2)}) %collective-permute-start.33) | collective-permute-done | bytes 131104 | tf_op jit(solution)/shard_map/ppermute | solution.py:191
  55.6 1.6 %collective-permute-start.30 = (bf16[64,1024]{1,0:T(8,128)(2,1)S(1)}, bf16[64,1024]{1,0:T(8,128)(2,1)S(1)}, u32[]{:S(2)}, u32[]{:S(2)}) collective-permute-start(bf16[64,1024]{1,0:T(8,128)(2,1)S(1)} %get-tuple-element.39), channel_id=1, source_target_pairs={{4,0},{8,4},{12,8},{14,12},{10,14},{6,10},{2,6},{0,2},{5,1},{9,5},... | collective-permute-start | bytes 393224 | tf_op jit(solution)/shard_map/ppermute | solution.py:191
  57.8 1.6 %collective-permute-start.34 = (bf16[64,1024]{1,0:T(8,128)(2,1)S(1)}, bf16[64,1024]{1,0:T(8,128)(2,1)S(1)}, u32[]{:S(2)}, u32[]{:S(2)}) collective-permute-start(bf16[64,1024]{1,0:T(8,128)(2,1)S(1)} %shard_map.126), channel_id=1, source_target_pairs={{4,0},{8,4},{12,8},{14,12},{10,14},{6,10},{2,6},{0,2},{5,1},{9,5},... | collective-permute-start | bytes 393224 | tf_op jit(solution)/shard_map/ppermute | solution.py:191
  59.6 2.7 %collective-permute-done.24.refs_2_ = bf16[64,1024]{1,0:T(8,128)(2,1)S(1)} collective-permute-done((bf16[64,1024]{1,0:T(8,128)(2,1)S(1)}, bf16[64,1024]{1,0:T(8,128)(2,1)S(1)}, u32[]{:S(2)}, u32[]{:S(2)}) %collective-permute-start.24) | collective-permute-done | bytes 131104 | tf_op jit(solution)/shard_map/ppermute | solution.py:190
  62.8 1.5 %collective-permute-start.2 = (bf16[128,1024]{1,0:T(8,128)(2,1)S(1)}, bf16[128,1024]{1,0:T(8,128)(2,1)S(1)}, u32[]{:S(2)}, u32[]{:S(2)}) collective-permute-start(bf16[128,1024]{1,0:T(8,128)(2,1)S(1)} %slice.17), channel_id=1, source_target_pairs={{0,16},{16,0},{1,17},{17,1},{2,18},{18,2},{3,19},{19,3},{4,20},{20... | collective-permute-start | bytes 786440 | tf_op jit(solution)/shard_map/ppermute | solution.py:193
  65.2 1.3 %collective-permute-start.31 = (bf16[64,1024]{1,0:T(8,128)(2,1)S(1)}, bf16[64,1024]{1,0:T(8,128)(2,1)S(1)}, u32[]{:S(2)}, u32[]{:S(2)}) collective-permute-start(bf16[64,1024]{1,0:T(8,128)(2,1)S(1)} %shard_map.124), channel_id=1, source_target_pairs={{4,0},{8,4},{12,8},{14,12},{10,14},{6,10},{2,6},{0,2},{5,1},{9,5},... | collective-permute-start | bytes 393224 | tf_op jit(solution)/shard_map/ppermute | solution.py:191
  66.6 1.6 %collective-permute-start.35 = (bf16[64,1024]{1,0:T(8,128)(2,1)S(1)}, bf16[64,1024]{1,0:T(8,128)(2,1)S(1)}, u32[]{:S(2)}, u32[]{:S(2)}) collective-permute-start(bf16[64,1024]{1,0:T(8,128)(2,1)S(1)} %shard_map.127), channel_id=1, source_target_pairs={{4,0},{8,4},{12,8},{14,12},{10,14},{6,10},{2,6},{0,2},{5,1},{9,5},... | collective-permute-start | bytes 393224 | tf_op jit(solution)/shard_map/ppermute | solution.py:191
  68.3 1.0 %collective-permute-start.26 = (bf16[64,1024]{1,0:T(8,128)(2,1)S(1)}, bf16[64,1024]{1,0:T(8,128)(2,1)S(1)}, u32[]{:S(2)}, u32[]{:S(2)}) collective-permute-start(bf16[64,1024]{1,0:T(8,128)(2,1)S(1)} %shard_map.120), channel_id=1, source_target_pairs={{0,4},{4,8},{8,12},{12,14},{14,10},{10,6},{6,2},{2,0},{1,5},{5,9},... | collective-permute-start | bytes 393224 | tf_op jit(solution)/shard_map/ppermute | solution.py:190
  69.3 1.4 %collective-permute-done.28.refs_2_ = bf16[64,1024]{1,0:T(8,128)(2,1)S(1)} collective-permute-done((bf16[64,1024]{1,0:T(8,128)(2,1)S(1)}, bf16[64,1024]{1,0:T(8,128)(2,1)S(1)}, u32[]{:S(2)}, u32[]{:S(2)}) %collective-permute-start.28) | collective-permute-done | bytes 131104 | tf_op jit(solution)/shard_map/ppermute | solution.py:190
  70.8 1.3 %collective-permute-start.29 = (bf16[64,1024]{1,0:T(8,128)(2,1)S(1)}, bf16[64,1024]{1,0:T(8,128)(2,1)S(1)}, u32[]{:S(2)}, u32[]{:S(2)}) collective-permute-start(bf16[64,1024]{1,0:T(8,128)(2,1)S(1)} %shard_map.123), channel_id=1, source_target_pairs={{0,4},{4,8},{8,12},{12,14},{14,10},{10,6},{6,2},{2,0},{1,5},{5,9},... | collective-permute-start | bytes 393224 | tf_op jit(solution)/shard_map/ppermute | solution.py:190
  73.0 1.7 %collective-permute-start.36 = (bf16[64,1024]{1,0:T(8,128)(2,1)S(1)}, bf16[64,1024]{1,0:T(8,128)(2,1)S(1)}, u32[]{:S(2)}, u32[]{:S(2)}) collective-permute-start(bf16[64,1024]{1,0:T(8,128)(2,1)S(1)} %shard_map.128), channel_id=1, source_target_pairs={{4,0},{8,4},{12,8},{14,12},{10,14},{6,10},{2,6},{0,2},{5,1},{9,5},... | collective-permute-start | bytes 393224 | tf_op jit(solution)/shard_map/ppermute | solution.py:191
  74.7 1.1 %collective-permute-done.29.ahead_two = bf16[64,1024]{1,0:T(8,128)(2,1)S(1)} collective-permute-done((bf16[64,1024]{1,0:T(8,128)(2,1)S(1)}, bf16[64,1024]{1,0:T(8,128)(2,1)S(1)}, u32[]{:S(2)}, u32[]{:S(2)}) %collective-permute-start.29) | collective-permute-done | bytes 131104 | tf_op jit(solution)/shard_map/ppermute | solution.py:190
  75.8 1.4 %collective-permute-done.32.back_one = bf16[64,1024]{1,0:T(8,128)(2,1)S(1)} collective-permute-done((bf16[64,1024]{1,0:T(8,128)(2,1)S(1)}, bf16[64,1024]{1,0:T(8,128)(2,1)S(1)}, u32[]{:S(2)}, u32[]{:S(2)}) %collective-permute-start.32) | collective-permute-done | bytes 131104 | tf_op jit(solution)/shard_map/ppermute | solution.py:191
  77.2 1.4 %collective-permute-done.36.back_two = bf16[64,1024]{1,0:T(8,128)(2,1)S(1)} collective-permute-done((bf16[64,1024]{1,0:T(8,128)(2,1)S(1)}, bf16[64,1024]{1,0:T(8,128)(2,1)S(1)}, u32[]{:S(2)}, u32[]{:S(2)}) %collective-permute-start.36) | collective-permute-done | bytes 131104 | tf_op jit(solution)/shard_map/ppermute | solution.py:191
  (89 shorter events, 12.1 us)
Async XLA Ops:
  1.7 9.8 %collective-permute-start.4 = (bf16[64,2176]{1,0:T(8,128)(2,1)S(1)}, bf16[64,2176]{1,0:T(8,128)(2,1)S(1)}, u32[]{:S(2)}, u32[]{:S(2)}) collective-permute-start(bf16[64,2176]{1,0:T(8,128)(2,1)S(1)} %get-tuple-element.28), channel_id=1, source_target_pairs={{4,0},{8,4},{12,8},{14,12},{10,14},{6,10},{2,6},{0,2},{5,1},{9,5},... | collective-permute-start | bytes 835592 | tf_op jit(solution)/shard_map/ppermute | solution.py:191
  4.8 8.4 %collective-permute-start.3 = (bf16[64,2176]{1,0:T(8,128)(2,1)S(1)}, bf16[64,2176]{1,0:T(8,128)(2,1)S(1)}, u32[]{:S(2)}, u32[]{:S(2)}) collective-permute-start(bf16[64,2176]{1,0:T(8,128)(2,1)S(1)} %get-tuple-element.28), channel_id=1, source_target_pairs={{0,4},{4,8},{8,12},{12,14},{14,10},{10,6},{6,2},{2,0},{1,5},{5,9},... | collective-permute-start | bytes 835592 | tf_op jit(solution)/shard_map/ppermute | solution.py:190
  11.5 7.8 %collective-permute-start.9 = (bf16[64,2176]{1,0:T(8,128)(2,1)S(1)}, bf16[64,2176]{1,0:T(8,128)(2,1)S(1)}, u32[]{:S(2)}, u32[]{:S(2)}) collective-permute-start(bf16[64,2176]{1,0:T(8,128)(2,1)S(1)} %collective-permute-done.4.refs_1_), channel_id=1, source_target_pairs={{4,0},{8,4},{12,8},{14,12},{10,14},{6,10},{2,6},{0,2},{5,1},{9,5},... | collective-permute-start | bytes 835592 | tf_op jit(solution)/shard_map/ppermute | solution.py:191
  13.2 7.5 %collective-permute-start.8 = (bf16[64,2176]{1,0:T(8,128)(2,1)S(1)}, bf16[64,2176]{1,0:T(8,128)(2,1)S(1)}, u32[]{:S(2)}, u32[]{:S(2)}) collective-permute-start(bf16[64,2176]{1,0:T(8,128)(2,1)S(1)} %collective-permute-done.3.refs_0_), channel_id=1, source_target_pairs={{0,4},{4,8},{8,12},{12,14},{14,10},{10,6},{6,2},{2,0},{1,5},{5,9},... | collective-permute-start | bytes 835592 | tf_op jit(solution)/shard_map/ppermute | solution.py:190
  13.5 16.7 %collective-permute-start = (bf16[128,2176]{1,0:T(8,128)(2,1)S(1)}, bf16[128,2176]{1,0:T(8,128)(2,1)S(1)}, u32[]{:S(2)}, u32[]{:S(2)}) collective-permute-start(bf16[128,2176]{1,0:T(8,128)(2,1)S(1)} %get-tuple-element.23.refs_0_), channel_id=1, source_target_pairs={{0,16},{16,0},{1,17},{17,1},{2,18},{18,2},{3,19},{19,3},{4,20},{20... | collective-permute-start | bytes 1671176 | tf_op jit(solution)/shard_map/ppermute | solution.py:193
  19.3 7.0 %collective-permute-start.14 = (bf16[64,2176]{1,0:T(8,128)(2,1)S(1)}, bf16[64,2176]{1,0:T(8,128)(2,1)S(1)}, u32[]{:S(2)}, u32[]{:S(2)}) collective-permute-start(bf16[64,2176]{1,0:T(8,128)(2,1)S(1)} %collective-permute-done.9.refs_1_), channel_id=1, source_target_pairs={{4,0},{8,4},{12,8},{14,12},{10,14},{6,10},{2,6},{0,2},{5,1},{9,5},... | collective-permute-start | bytes 835592 | tf_op jit(solution)/shard_map/ppermute | solution.py:191
  20.7 6.5 %collective-permute-start.13 = (bf16[64,2176]{1,0:T(8,128)(2,1)S(1)}, bf16[64,2176]{1,0:T(8,128)(2,1)S(1)}, u32[]{:S(2)}, u32[]{:S(2)}) collective-permute-start(bf16[64,2176]{1,0:T(8,128)(2,1)S(1)} %collective-permute-done.8.refs_0_), channel_id=1, source_target_pairs={{0,4},{4,8},{8,12},{12,14},{14,10},{10,6},{6,2},{2,0},{1,5},{5,9},... | collective-permute-start | bytes 835592 | tf_op jit(solution)/shard_map/ppermute | solution.py:190
  26.3 6.1 %collective-permute-start.16 = (bf16[64,2176]{1,0:T(8,128)(2,1)S(1)}, bf16[64,2176]{1,0:T(8,128)(2,1)S(1)}, u32[]{:S(2)}, u32[]{:S(2)}) collective-permute-start(bf16[64,2176]{1,0:T(8,128)(2,1)S(1)} %collective-permute-done.14.refs_1_), channel_id=1, source_target_pairs={{0,1},{1,0},{2,3},{3,2},{4,5},{5,4},{6,7},{7,6},{8,9},{9,8},{10,11... | collective-permute-start | bytes 835592 | tf_op jit(solution)/shard_map/ppermute | solution.py:192
  27.3 6.8 %collective-permute-start.15 = (bf16[64,2176]{1,0:T(8,128)(2,1)S(1)}, bf16[64,2176]{1,0:T(8,128)(2,1)S(1)}, u32[]{:S(2)}, u32[]{:S(2)}) collective-permute-start(bf16[64,2176]{1,0:T(8,128)(2,1)S(1)} %collective-permute-done.13.refs_0_), channel_id=1, source_target_pairs={{0,1},{1,0},{2,3},{3,2},{4,5},{5,4},{6,7},{7,6},{8,9},{9,8},{10,11... | collective-permute-start | bytes 835592 | tf_op jit(solution)/shard_map/ppermute | solution.py:192
  29.6 15.8 %collective-permute-start.6 = (bf16[64,2176]{1,0:T(8,128)(2,1)S(1)}, bf16[64,2176]{1,0:T(8,128)(2,1)S(1)}, u32[]{:S(2)}, u32[]{:S(2)}) collective-permute-start(bf16[64,2176]{1,0:T(8,128)(2,1)S(1)} %collective-permute-done.4.refs_1_), channel_id=1, source_target_pairs={{0,1},{1,0},{2,3},{3,2},{4,5},{5,4},{6,7},{7,6},{8,9},{9,8},{10,11... | collective-permute-start | bytes 835592 | tf_op jit(solution)/shard_map/ppermute | solution.py:192
  30.1 7.0 %collective-permute-start.11 = (bf16[64,2176]{1,0:T(8,128)(2,1)S(1)}, bf16[64,2176]{1,0:T(8,128)(2,1)S(1)}, u32[]{:S(2)}, u32[]{:S(2)}) collective-permute-start(bf16[64,2176]{1,0:T(8,128)(2,1)S(1)} %collective-permute-done.9.refs_1_), channel_id=1, source_target_pairs={{0,1},{1,0},{2,3},{3,2},{4,5},{5,4},{6,7},{7,6},{8,9},{9,8},{10,11... | collective-permute-start | bytes 835592 | tf_op jit(solution)/shard_map/ppermute | solution.py:192
  30.2 9.2 %collective-permute-start.10 = (bf16[64,2176]{1,0:T(8,128)(2,1)S(1)}, bf16[64,2176]{1,0:T(8,128)(2,1)S(1)}, u32[]{:S(2)}, u32[]{:S(2)}) collective-permute-start(bf16[64,2176]{1,0:T(8,128)(2,1)S(1)} %collective-permute-done.8.refs_0_), channel_id=1, source_target_pairs={{0,1},{1,0},{2,3},{3,2},{4,5},{5,4},{6,7},{7,6},{8,9},{9,8},{10,11... | collective-permute-start | bytes 835592 | tf_op jit(solution)/shard_map/ppermute | solution.py:192
  32.4 5.7 %collective-permute-start.19 = (bf16[32,2176]{1,0:T(8,128)(2,1)S(1)}, bf16[32,2176]{1,0:T(8,128)(2,1)S(1)}, u32[]{:S(2)}, u32[]{:S(2)}) collective-permute-start(bf16[32,2176]{1,0:T(8,128)(2,1)S(1)} %slice.15), channel_id=1, source_target_pairs={{4,0},{8,4},{12,8},{14,12},{10,14},{6,10},{2,6},{0,2},{5,1},{9,5},... | collective-permute-start | bytes 417800 | tf_op jit(solution)/shard_map/ppermute | solution.py:191
  34.0 5.4 %collective-permute-start.18 = (bf16[32,2176]{1,0:T(8,128)(2,1)S(1)}, bf16[32,2176]{1,0:T(8,128)(2,1)S(1)}, u32[]{:S(2)}, u32[]{:S(2)}) collective-permute-start(bf16[32,2176]{1,0:T(8,128)(2,1)S(1)} %slice.14), channel_id=1, source_target_pairs={{0,4},{4,8},{8,12},{12,14},{14,10},{10,6},{6,2},{2,0},{1,5},{5,9},... | collective-permute-start | bytes 417800 | tf_op jit(solution)/shard_map/ppermute | solution.py:190
  37.1 8.5 %collective-permute-start.5 = (bf16[64,2176]{1,0:T(8,128)(2,1)S(1)}, bf16[64,2176]{1,0:T(8,128)(2,1)S(1)}, u32[]{:S(2)}, u32[]{:S(2)}) collective-permute-start(bf16[64,2176]{1,0:T(8,128)(2,1)S(1)} %collective-permute-done.3.refs_0_), channel_id=1, source_target_pairs={{0,1},{1,0},{2,3},{3,2},{4,5},{5,4},{6,7},{7,6},{8,9},{9,8},{10,11... | collective-permute-start | bytes 835592 | tf_op jit(solution)/shard_map/ppermute | solution.py:192
  39.4 11.0 %collective-permute-start.17 = (bf16[256,1024]{1,0:T(8,128)(2,1)S(1)}, bf16[256,1024]{1,0:T(8,128)(2,1)S(1)}, u32[]{:S(2)}, u32[]{:S(2)}) collective-permute-start(bf16[256,1024]{1,0:T(8,128)(2,1)S(1)} %get-tuple-element.34), channel_id=1, source_target_pairs={{0,1},{1,0},{2,3},{3,2},{4,5},{5,4},{6,7},{7,6},{8,9},{9,8},{10,11... | collective-permute-start | bytes 1572872 | tf_op jit(solution)/shard_map/ppermute | solution.py:192
  42.6 14.7 %collective-permute-start.1 = (bf16[256,1024]{1,0:T(8,128)(2,1)S(1)}, bf16[256,1024]{1,0:T(8,128)(2,1)S(1)}, u32[]{:S(2)}, u32[]{:S(2)}) collective-permute-start(bf16[256,1024]{1,0:T(8,128)(2,1)S(1)} %get-tuple-element.27), channel_id=1, source_target_pairs={{0,1},{1,0},{2,3},{3,2},{4,5},{5,4},{6,7},{7,6},{8,9},{9,8},{10,11... | collective-permute-start | bytes 1572872 | tf_op jit(solution)/shard_map/ppermute | solution.py:192
  42.7 15.1 %collective-permute-start.12 = (bf16[256,1024]{1,0:T(8,128)(2,1)S(1)}, bf16[256,1024]{1,0:T(8,128)(2,1)S(1)}, u32[]{:S(2)}, u32[]{:S(2)}) collective-permute-start(bf16[256,1024]{1,0:T(8,128)(2,1)S(1)} %get-tuple-element.32), channel_id=1, source_target_pairs={{0,1},{1,0},{2,3},{3,2},{4,5},{5,4},{6,7},{7,6},{8,9},{9,8},{10,11... | collective-permute-start | bytes 1572872 | tf_op jit(solution)/shard_map/ppermute | solution.py:192
  48.2 18.4 %collective-permute-start.7 = (bf16[256,1024]{1,0:T(8,128)(2,1)S(1)}, bf16[256,1024]{1,0:T(8,128)(2,1)S(1)}, u32[]{:S(2)}, u32[]{:S(2)}) collective-permute-start(bf16[256,1024]{1,0:T(8,128)(2,1)S(1)} %get-tuple-element.30), channel_id=1, source_target_pairs={{0,1},{1,0},{2,3},{3,2},{4,5},{5,4},{6,7},{7,6},{8,9},{9,8},{10,11... | collective-permute-start | bytes 1572872 | tf_op jit(solution)/shard_map/ppermute | solution.py:192
  48.8 5.5 %collective-permute-start.33 = (bf16[64,1024]{1,0:T(8,128)(2,1)S(1)}, bf16[64,1024]{1,0:T(8,128)(2,1)S(1)}, u32[]{:S(2)}, u32[]{:S(2)}) collective-permute-start(bf16[64,1024]{1,0:T(8,128)(2,1)S(1)} %get-tuple-element.40), channel_id=1, source_target_pairs={{4,0},{8,4},{12,8},{14,12},{10,14},{6,10},{2,6},{0,2},{5,1},{9,5},... | collective-permute-start | bytes 393224 | tf_op jit(solution)/shard_map/ppermute | solution.py:191
  50.4 5.2 %collective-permute-start.23 = (bf16[64,1024]{1,0:T(8,128)(2,1)S(1)}, bf16[64,1024]{1,0:T(8,128)(2,1)S(1)}, u32[]{:S(2)}, u32[]{:S(2)}) collective-permute-start(bf16[64,1024]{1,0:T(8,128)(2,1)S(1)} %get-tuple-element.37), channel_id=1, source_target_pairs={{0,4},{4,8},{8,12},{12,14},{14,10},{10,6},{6,2},{2,0},{1,5},{5,9},... | collective-permute-start | bytes 393224 | tf_op jit(solution)/shard_map/ppermute | solution.py:190
  54.3 8.5 %collective-permute-start.27 = (bf16[64,1024]{1,0:T(8,128)(2,1)S(1)}, bf16[64,1024]{1,0:T(8,128)(2,1)S(1)}, u32[]{:S(2)}, u32[]{:S(2)}) collective-permute-start(bf16[64,1024]{1,0:T(8,128)(2,1)S(1)} %get-tuple-element.38), channel_id=1, source_target_pairs={{0,4},{4,8},{8,12},{12,14},{14,10},{10,6},{6,2},{2,0},{1,5},{5,9},... | collective-permute-start | bytes 393224 | tf_op jit(solution)/shard_map/ppermute | solution.py:190
  55.6 8.7 %collective-permute-start.30 = (bf16[64,1024]{1,0:T(8,128)(2,1)S(1)}, bf16[64,1024]{1,0:T(8,128)(2,1)S(1)}, u32[]{:S(2)}, u32[]{:S(2)}) collective-permute-start(bf16[64,1024]{1,0:T(8,128)(2,1)S(1)} %get-tuple-element.39), channel_id=1, source_target_pairs={{4,0},{8,4},{12,8},{14,12},{10,14},{6,10},{2,6},{0,2},{5,1},{9,5},... | collective-permute-start | bytes 393224 | tf_op jit(solution)/shard_map/ppermute | solution.py:191
  57.3 5.0 %collective-permute-start.24 = (bf16[64,1024]{1,0:T(8,128)(2,1)S(1)}, bf16[64,1024]{1,0:T(8,128)(2,1)S(1)}, u32[]{:S(2)}, u32[]{:S(2)}) collective-permute-start(bf16[64,1024]{1,0:T(8,128)(2,1)S(1)} %shard_map.118), channel_id=1, source_target_pairs={{0,4},{4,8},{8,12},{12,14},{14,10},{10,6},{6,2},{2,0},{1,5},{5,9},... | collective-permute-start | bytes 393224 | tf_op jit(solution)/shard_map/ppermute | solution.py:190
  57.8 7.5 %collective-permute-start.34 = (bf16[64,1024]{1,0:T(8,128)(2,1)S(1)}, bf16[64,1024]{1,0:T(8,128)(2,1)S(1)}, u32[]{:S(2)}, u32[]{:S(2)}) collective-permute-start(bf16[64,1024]{1,0:T(8,128)(2,1)S(1)} %shard_map.126), channel_id=1, source_target_pairs={{4,0},{8,4},{12,8},{14,12},{10,14},{6,10},{2,6},{0,2},{5,1},{9,5},... | collective-permute-start | bytes 393224 | tf_op jit(solution)/shard_map/ppermute | solution.py:191
  62.3 5.9 %collective-permute-start.25 = (bf16[64,1024]{1,0:T(8,128)(2,1)S(1)}, bf16[64,1024]{1,0:T(8,128)(2,1)S(1)}, u32[]{:S(2)}, u32[]{:S(2)}) collective-permute-start(bf16[64,1024]{1,0:T(8,128)(2,1)S(1)} %shard_map.119), channel_id=1, source_target_pairs={{0,4},{4,8},{8,12},{12,14},{14,10},{10,6},{6,2},{2,0},{1,5},{5,9},... | collective-permute-start | bytes 393224 | tf_op jit(solution)/shard_map/ppermute | solution.py:190
  62.8 11.9 %collective-permute-start.2 = (bf16[128,1024]{1,0:T(8,128)(2,1)S(1)}, bf16[128,1024]{1,0:T(8,128)(2,1)S(1)}, u32[]{:S(2)}, u32[]{:S(2)}) collective-permute-start(bf16[128,1024]{1,0:T(8,128)(2,1)S(1)} %slice.17), channel_id=1, source_target_pairs={{0,16},{16,0},{1,17},{17,1},{2,18},{18,2},{3,19},{19,3},{4,20},{20... | collective-permute-start | bytes 786440 | tf_op jit(solution)/shard_map/ppermute | solution.py:193
  64.4 6.3 %collective-permute-start.28 = (bf16[64,1024]{1,0:T(8,128)(2,1)S(1)}, bf16[64,1024]{1,0:T(8,128)(2,1)S(1)}, u32[]{:S(2)}, u32[]{:S(2)}) collective-permute-start(bf16[64,1024]{1,0:T(8,128)(2,1)S(1)} %shard_map.122), channel_id=1, source_target_pairs={{0,4},{4,8},{8,12},{12,14},{14,10},{10,6},{6,2},{2,0},{1,5},{5,9},... | collective-permute-start | bytes 393224 | tf_op jit(solution)/shard_map/ppermute | solution.py:190
  65.2 6.9 %collective-permute-start.31 = (bf16[64,1024]{1,0:T(8,128)(2,1)S(1)}, bf16[64,1024]{1,0:T(8,128)(2,1)S(1)}, u32[]{:S(2)}, u32[]{:S(2)}) collective-permute-start(bf16[64,1024]{1,0:T(8,128)(2,1)S(1)} %shard_map.124), channel_id=1, source_target_pairs={{4,0},{8,4},{12,8},{14,12},{10,14},{6,10},{2,6},{0,2},{5,1},{9,5},... | collective-permute-start | bytes 393224 | tf_op jit(solution)/shard_map/ppermute | solution.py:191
  66.6 6.3 %collective-permute-start.35 = (bf16[64,1024]{1,0:T(8,128)(2,1)S(1)}, bf16[64,1024]{1,0:T(8,128)(2,1)S(1)}, u32[]{:S(2)}, u32[]{:S(2)}) collective-permute-start(bf16[64,1024]{1,0:T(8,128)(2,1)S(1)} %shard_map.127), channel_id=1, source_target_pairs={{4,0},{8,4},{12,8},{14,12},{10,14},{6,10},{2,6},{0,2},{5,1},{9,5},... | collective-permute-start | bytes 393224 | tf_op jit(solution)/shard_map/ppermute | solution.py:191
  68.3 6.4 %collective-permute-start.26 = (bf16[64,1024]{1,0:T(8,128)(2,1)S(1)}, bf16[64,1024]{1,0:T(8,128)(2,1)S(1)}, u32[]{:S(2)}, u32[]{:S(2)}) collective-permute-start(bf16[64,1024]{1,0:T(8,128)(2,1)S(1)} %shard_map.120), channel_id=1, source_target_pairs={{0,4},{4,8},{8,12},{12,14},{14,10},{10,6},{6,2},{2,0},{1,5},{5,9},... | collective-permute-start | bytes 393224 | tf_op jit(solution)/shard_map/ppermute | solution.py:190
  73.0 5.6 %collective-permute-start.36 = (bf16[64,1024]{1,0:T(8,128)(2,1)S(1)}, bf16[64,1024]{1,0:T(8,128)(2,1)S(1)}, u32[]{:S(2)}, u32[]{:S(2)}) collective-permute-start(bf16[64,1024]{1,0:T(8,128)(2,1)S(1)} %shard_map.128), channel_id=1, source_target_pairs={{4,0},{8,4},{12,8},{14,12},{10,14},{6,10},{2,6},{0,2},{5,1},{9,5},... | collective-permute-start | bytes 393224 | tf_op jit(solution)/shard_map/ppermute | solution.py:191
  (16 other events, 117.0 us)

commit v3 on v2

--- a/solution.py
+++ b/solution.py
@@ -38,7 +38,7 @@
     out[...] = jnp.zeros_like(out)
 
 
-def prologue_body(expert_count, lead, tokens, gain, router, ids, modality, packed, part):
+def prologue_body(expert_count, lead, tokens, gain, router, ids, modality, packed, lower, upper):
     width = tokens.shape[1]
     values = tokens[...].astype(jnp.float32)
     scale = lax.rsqrt(jnp.mean(values * values, axis=1, keepdims=True) + epsilon)
@@ -57,9 +57,10 @@
     first = lax.broadcasted_iota(jnp.int32, (rows, image.shape[1]), 0) == 0
     table = jnp.concatenate([rounded, weights - rounded, jnp.where(first, image, 0.0)], axis=0)
     packed[:, width:] = table.T.astype(jnp.bfloat16)
-    half = part.shape[0]
-    start = pl.multiple_of(lax.axis_index("tensor") * half, half)
-    part[...] = packed[pl.ds(start, half), :]
+    part = lower.shape[0]
+    start = pl.multiple_of(lax.axis_index("tensor") * 2 * part, 2 * part)
+    lower[...] = packed[pl.ds(start, part), :]
+    upper[...] = packed[pl.ds(start + part, part), :]
 
 
 def side_rows(rows, width, lanes):
@@ -83,21 +84,30 @@
     return gated(dot(gate[...], rows, NT), dot(up[...], rows, NT), factor)
 
 
-def pair_body(expert_count, up_own, down_own, up_other, down_other, gate, up, down, keep, give, rows):
-    half = up_own.shape[0]
-    mine = pl.multiple_of(lax.axis_index("tensor") * half, half)
-    theirs = pl.multiple_of((1 - lax.axis_index("tensor")) * half, half)
-    for base, own, other in ((0, up_own, up_other), (2 * half, down_own, down_other)):
-        rows[pl.ds(base + mine, half), :] = own[...]
-        rows[pl.ds(base + theirs, half), :] = other[...]
+def pack_body(*refs):
+    part = refs[0].shape[0]
+    for index, piece in enumerate(refs[:-1]):
+        refs[-1][index * part : (index + 1) * part, :] = piece[...]
+
+
+def pair_body(expert_count, mine, theirs, gate, up, down, keep, give, rows):
+    half = mine.shape[0] // 2
+    core = lax.axis_index("tensor")
+    for index, pieces in ((core, mine), (1 - core, theirs)):
+        for block in range(2):
+            start = pl.multiple_of((2 * block + index) * half, half)
+            rows[pl.ds(start, half), :] = pieces[block * half : (block + 1) * half, :]
     split_down(expert_hidden(expert_count, rows[...], gate, up), down, keep, give)
 
 
-def column_halves(hidden, down):
+def column_place(down, whose):
     half = down.shape[1] // 2
     core = lax.axis_index("tensor")
-    places = [pl.ds(pl.multiple_of(i * half, half), half) for i in (core, 1 - core)]
-    return [dot(hidden, down[:, place], TN) for place in places]
+    return pl.ds(pl.multiple_of((1 - core if whose else core) * half, half), half)
+
+
+def column_halves(hidden, down):
+    return [dot(hidden, down[:, column_place(down, whose)], TN) for whose in range(2)]
 
 
 def split_down(hidden, down, keep, give):
@@ -111,15 +121,17 @@
     mine[...], theirs[...] = column_halves(hidden, down)
 
 
-def far_body(expert_count, up_own, down_own, up_other, down_other, gate, up, down, keep, give, rows):
-    part = up_own.shape[0]
-    mine = pl.multiple_of(lax.axis_index("tensor") * 2 * part, 2 * part)
-    theirs = pl.multiple_of((1 - lax.axis_index("tensor")) * 2 * part, 2 * part)
-    rows[pl.ds(mine, part), :] = up_own[...]
-    rows[pl.ds(mine + part, part), :] = down_own[...]
-    rows[pl.ds(theirs, part), :] = up_other[...]
-    rows[pl.ds(theirs + part, part), :] = down_other[...]
-    split_down(expert_hidden(expert_count, rows[...], gate, up), down, keep, give)
+def far_body(expert_count, mine, theirs, gate, up, down, give, hidden, rows):
+    half = mine.shape[0]
+    core = lax.axis_index("tensor")
+    for index, piece in ((core, mine), (1 - core, theirs)):
+        rows[pl.ds(pl.multiple_of(index * half, half), half), :] = piece[...]
+    hidden[...] = expert_hidden(expert_count, rows[...], gate, up)
+    give[...] = dot(hidden[...], down[:, column_place(down, 1)], TN).astype(give.dtype)
+
+
+def far_keep_body(hidden, down, keep):
+    keep[...] = dot(hidden[...], down[:, column_place(down, 0)], TN)
 
 
 def shared_body(expert_count, own, other, mine, theirs, gate, up, down, keep, give):
@@ -204,28 +216,48 @@
     )
     inputs = (tokens, norm_gain[None, :], router.T, expert_ids.T, modality[None, :])
     lead = call(lead_body, shape((8, LANES), f32), (), 1, 2**34, MIB)
-    own, part = call(
+    own, lower, upper = call(
         lambda *refs: prologue_body(experts, *refs),
-        (shape((count, width + side), bf16), shape((half, width + side), bf16)),
+        (shape((count, width + side), bf16),) + (shape((quarter, width + side), bf16),) * 2,
         (lead, *inputs),
         8,
         4 * MIB,
         MIB,
     )
     other = dp_swap(own)
-    up_block, down_block = ahead(part), back(part)
     weights = stored
 
-    def experts_of(body, *blocks):
-        rows = 4 * blocks[0].shape[0]
-        return call(
-            lambda *refs: body(experts, *refs),
+    def pair_part(mine, theirs):
+        rows = 2 * mine.shape[0]
+        return call(
+            lambda *refs: pair_body(experts, *refs),
             (shape((rows, columns), f32), shape((rows, columns), bf16)),
-            (*blocks, *weights[:3]),
+            (mine, theirs, *weights[:3]),
             16,
             6 * rows * width * hidden_units,
             6 * width * hidden_units,
             [pltpu.VMEM((rows, width + side), bf16)],
+        )
+
+    def far_part(mine, theirs):
+        return call(
+            lambda *refs: far_body(experts, *refs),
+            (shape((count, columns), bf16), shape((hidden_units, count), bf16)),
+            (mine, theirs, *weights[:3]),
+            16,
+            5 * count * width * hidden_units,
+            6 * width * hidden_units,
+            [pltpu.VMEM((count, width + side), bf16)],
+        )
+
+    def far_keep(hidden):
+        return call(
+            far_keep_body,
+            shape((count, columns), f32),
+            (hidden, weights[2]),
+            16,
+            count * width * hidden_units,
+            width * hidden_units,
         )
 
     def own_part(own):
@@ -256,29 +288,40 @@
             8,
         )
 
+    def travel(pair):
+        return ahead(pair[0]), back(pair[1])
+
+    def packed(pieces):
+        rows = len(pieces) * pieces[0].shape[0]
+        return call(pack_body, shape((rows, width + side), bf16), pieces, 4)
+
     keep, recv = {}, {}
     own_sums = own_part(own)
+    long, short = (lower, upper), (upper, lower)
     for k in range(1, middle + 1):
-        rows = [up_block, down_block]
-        if k == middle - 1:
-            up_block, down_block = up_block[:quarter], down_block[quarter:]
+        long = travel(long)
         if k < middle:
-            up_block = ahead(up_block)
-            down_block = back(down_block)
-        rows += [swap(rows[0]), swap(rows[1])]
-        keep[k], give = experts_of(pair_body if k < middle else far_body, *rows)
+            short = travel(short)
+            mine = packed((long[0], short[0], short[1], long[1]))
+            keep[k], give = pair_part(mine, swap(mine))
+        else:
+            mine = packed(long)
+            give, hidden = far_part(mine, swap(mine))
+            keep[k] = far_keep(hidden)
         recv[k] = swap(give)
 
     ahead_base, back_base = count, 0
     short = sums(middle - 1, (ahead_base + half, back_base))
-    long = call(far_add_body, (shape((half, columns), bf16),) * 2, (keep[middle], recv[middle]), 8)
-
-    def travel(pair):
-        return ahead(pair[0]), back(pair[1])
+    long = call(
+        far_add_body,
+        (shape((half, columns), bf16),) * 2,
+        (keep[middle], recv[middle]),
+        8,
+    )
 
     for k in range(middle - 1, 0, -1):
+        long = travel(long)
         short = travel(short)
-        long = travel(long)
         if k > 1:
             for way, base in enumerate((ahead_base + half, back_base)):
                 part = sums(k - 1, (base,), short[way])

time: 79.5 us -> 78.4 us (0.986)
  waiting for transfers between devices: 31.1 us -> 23.2 us
  starting transfers between devices: 30.7 us -> 37 us
    ppermute x11 -> x14, waiting for transfers between devices: 22.7 us -> 12.5 us  [per_device(): back = lambda x: lax.ppermute(x, 'expert', backward)]
    ppermute x11 -> x14, starting transfers between devices: 18 us -> 22.8 us  [per_device(): back = lambda x: lax.ppermute(x, 'expert', backward)]
    ppermute x11 -> x14, waiting for transfers between devices: 8.28 us -> 10.7 us  [per_device(): ahead = lambda x: lax.ppermute(x, 'expert', onward)]
    ppermute x11 -> x14, starting transfers between devices: 6.58 us -> 8.19 us  [per_device(): ahead = lambda x: lax.ppermute(x, 'expert', onward)]
    pallas_call x21 -> x26, Pallas kernels: 16 us -> 16.4 us  [call(): pl.pallas_call(body, out_shape=outs, in_specs=[vmem] * len(args), out_spe...]
    ppermute x13 -> x9, starting transfers between devices: 2.92 us -> 2.64 us  [per_device(): swap = lambda x: lax.ppermute(x, 'tensor', [(0, 1), (1, 0)])]
  transfers between devices with their start and end apart: 37 -> 39, of which waited for: 13 -> 16; matrix products, arithmetic and copies ran while one was open for 0% -> 0% of each run, Pallas kernels for 18% -> 19%
where the time goes in v3:
time: 78.4 us; the launch traced here: 78.3 us
  starting transfers between devices  37 us (47%)
  waiting for transfers between devices  23.2 us (30%)
  Pallas kernels  16.4 us (21%)
  local copies, waits for them, and re-layouts  1.12 us (1%)
    ppermute x14, starting transfers between devices, per_device(): back = lambda x: lax.ppermute(x, 'expert', backward)  22.8 us
    pallas_call x26, Pallas kernels, call(): pl.pallas_call(body, out_shape=outs, in_specs=[vmem] * len(args), out_spe...  16.4 us
    ppermute x14, waiting for transfers between devices, per_device(): back = lambda x: lax.ppermute(x, 'expert', backward)  12.5 us
    ppermute x14, waiting for transfers between devices, per_device(): ahead = lambda x: lax.ppermute(x, 'expert', onward)  10.7 us
    ppermute x14, starting transfers between devices, per_device(): ahead = lambda x: lax.ppermute(x, 'expert', onward)  8.19 us
    ppermute x2, starting transfers between devices, per_device(): dp_swap = lambda x: lax.ppermute(x, 'dp', [(0, 1), (1, 0)])  3.36 us
    ppermute x9, starting transfers between devices, per_device(): swap = lambda x: lax.ppermute(x, 'tensor', [(0, 1), (1, 0)])  2.64 us
  transfers between devices with their start and end apart: 39, of which 16 were waited for; matrix products, arithmetic and copies ran while one was open for 0% of the time, Pallas kernels for 19%

profile of v3, /device:TPU:0, one launch (start us, length us, event | category | flops | bytes accessed | tf_op | source)
XLA Modules:
  0.0 78.3 jit_solution(5663933263491744604)
XLA Ops:
  1.7 3.0 %collective-permute-start.5 = (bf16[32,2176]{1,0:T(8,128)(2,1)S(1)}, bf16[32,2176]{1,0:T(8,128)(2,1)S(1)}, u32[]{:S(2)}, u32[]{:S(2)}) collective-permute-start(bf16[32,2176]{1,0:T(8,128)(2,1)S(1)} %get-tuple-element.29), channel_id=1, source_target_pairs={{4,0},{8,4},{12,8},{14,12},{10,14},{6,10},{2,6},{0,2},{5,1},{9,5},... | collective-permute-start | bytes 417800 | tf_op jit(solution)/shard_map/ppermute | solution.py:203
  4.9 1.9 %collective-permute-start.6 = (bf16[32,2176]{1,0:T(8,128)(2,1)S(1)}, bf16[32,2176]{1,0:T(8,128)(2,1)S(1)}, u32[]{:S(2)}, u32[]{:S(2)}) collective-permute-start(bf16[32,2176]{1,0:T(8,128)(2,1)S(1)} %get-tuple-element.30), channel_id=1, source_target_pairs={{4,0},{8,4},{12,8},{14,12},{10,14},{6,10},{2,6},{0,2},{5,1},{9,5},... | collective-permute-start | bytes 417800 | tf_op jit(solution)/shard_map/ppermute | solution.py:203
  6.9 2.4 %collective-permute-done.5.refs_2_ = bf16[32,2176]{1,0:T(8,128)(2,1)S(1)} collective-permute-done((bf16[32,2176]{1,0:T(8,128)(2,1)S(1)}, bf16[32,2176]{1,0:T(8,128)(2,1)S(1)}, u32[]{:S(2)}, u32[]{:S(2)}) %collective-permute-start.5) | collective-permute-done | bytes 139296 | tf_op jit(solution)/shard_map/ppermute | solution.py:203
  9.4 2.0 %collective-permute-start.11 = (bf16[32,2176]{1,0:T(8,128)(2,1)S(1)}, bf16[32,2176]{1,0:T(8,128)(2,1)S(1)}, u32[]{:S(2)}, u32[]{:S(2)}) collective-permute-start(bf16[32,2176]{1,0:T(8,128)(2,1)S(1)} %collective-permute-done.5.refs_2_), channel_id=1, source_target_pairs={{4,0},{8,4},{12,8},{14,12},{10,14},{6,10},{2,6},{0,2},{5,1},{9,5},... | collective-permute-start | bytes 417800 | tf_op jit(solution)/shard_map/ppermute | solution.py:203
  12.3 2.0 %collective-permute-start.12 = (bf16[32,2176]{1,0:T(8,128)(2,1)S(1)}, bf16[32,2176]{1,0:T(8,128)(2,1)S(1)}, u32[]{:S(2)}, u32[]{:S(2)}) collective-permute-start(bf16[32,2176]{1,0:T(8,128)(2,1)S(1)} %collective-permute-done.6.refs_3_), channel_id=1, source_target_pairs={{4,0},{8,4},{12,8},{14,12},{10,14},{6,10},{2,6},{0,2},{5,1},{9,5},... | collective-permute-start | bytes 417800 | tf_op jit(solution)/shard_map/ppermute | solution.py:203
  14.4 1.2 %collective-permute-done.11.refs_2_ = bf16[32,2176]{1,0:T(8,128)(2,1)S(1)} collective-permute-done((bf16[32,2176]{1,0:T(8,128)(2,1)S(1)}, bf16[32,2176]{1,0:T(8,128)(2,1)S(1)}, u32[]{:S(2)}, u32[]{:S(2)}) %collective-permute-start.11) | collective-permute-done | bytes 139296 | tf_op jit(solution)/shard_map/ppermute | solution.py:203
  15.6 2.3 %collective-permute-start.17 = (bf16[32,2176]{1,0:T(8,128)(2,1)S(1)}, bf16[32,2176]{1,0:T(8,128)(2,1)S(1)}, u32[]{:S(2)}, u32[]{:S(2)}) collective-permute-start(bf16[32,2176]{1,0:T(8,128)(2,1)S(1)} %collective-permute-done.11.refs_2_), channel_id=1, source_target_pairs={{4,0},{8,4},{12,8},{14,12},{10,14},{6,10},{2,6},{0,2},{5,1},{9,5},... | collective-permute-start | bytes 417800 | tf_op jit(solution)/shard_map/ppermute | solution.py:203
  18.9 2.0 %collective-permute-start.18 = (bf16[32,2176]{1,0:T(8,128)(2,1)S(1)}, bf16[32,2176]{1,0:T(8,128)(2,1)S(1)}, u32[]{:S(2)}, u32[]{:S(2)}) collective-permute-start(bf16[32,2176]{1,0:T(8,128)(2,1)S(1)} %collective-permute-done.12.refs_3_), channel_id=1, source_target_pairs={{4,0},{8,4},{12,8},{14,12},{10,14},{6,10},{2,6},{0,2},{5,1},{9,5},... | collective-permute-start | bytes 417800 | tf_op jit(solution)/shard_map/ppermute | solution.py:203
  21.0 1.9 %collective-permute-start = (bf16[128,2176]{1,0:T(8,128)(2,1)S(1)}, bf16[128,2176]{1,0:T(8,128)(2,1)S(1)}, u32[]{:S(2)}, u32[]{:S(2)}) collective-permute-start(bf16[128,2176]{1,0:T(8,128)(2,1)S(1)} %get-tuple-element.24.refs_0_), channel_id=1, source_target_pairs={{0,16},{16,0},{1,17},{17,1},{2,18},{18,2},{3,19},{19,3},{4,20},{20... | collective-permute-start | bytes 1671176 | tf_op jit(solution)/shard_map/ppermute | solution.py:205
  23.9 2.0 %collective-permute-done.16.refs_1_ = bf16[32,2176]{1,0:T(8,128)(2,1)S(1)} collective-permute-done((bf16[32,2176]{1,0:T(8,128)(2,1)S(1)}, bf16[32,2176]{1,0:T(8,128)(2,1)S(1)}, u32[]{:S(2)}, u32[]{:S(2)}) %collective-permute-start.16) | collective-permute-done | bytes 139296 | tf_op jit(solution)/shard_map/ppermute | solution.py:202
  26.8 1.9 %collective-permute-start.22 = (bf16[32,2176]{1,0:T(8,128)(2,1)S(1)}, bf16[32,2176]{1,0:T(8,128)(2,1)S(1)}, u32[]{:S(2)}, u32[]{:S(2)}) collective-permute-start(bf16[32,2176]{1,0:T(8,128)(2,1)S(1)} %collective-permute-done.18.refs_3_), channel_id=1, source_target_pairs={{4,0},{8,4},{12,8},{14,12},{10,14},{6,10},{2,6},{0,2},{5,1},{9,5},... | collective-permute-start | bytes 417800 | tf_op jit(solution)/shard_map/ppermute | solution.py:203
  28.7 2.2 %shard_map.111 = (f32[128,1024]{1,0:T(8,128)S(1)}, f32[128,1024]{1,0:T(8,128)S(1)}) custom-call(bf16[128,2176]{1,0:T(8,128)(2,1)S(1)} %get-tuple-element.24.refs_0_, bf16[704,2048]{1,0:T(8,128)(2,1)S(1)} %bitcast.24, bf16[704,2048]{1,0:T(8,128)(2,1)S(1)} %bitcast.29, bf16[704,2048]{1,0:T(8,128)(2,1)S(1)} %bitcast.18), custom_call_target="tpu_custom_call" | custom-call | flops 1107296256 | bytes 8650752 | tf_op jit(solution)/shard_map/pallas_call | solution.py:26
  31.0 1.3 %collective-permute-done.21.refs_0_ = bf16[32,2176]{1,0:T(8,128)(2,1)S(1)} collective-permute-done((bf16[32,2176]{1,0:T(8,128)(2,1)S(1)}, bf16[32,2176]{1,0:T(8,128)(2,1)S(1)}, u32[]{:S(2)}, u32[]{:S(2)}) %collective-permute-start.21) | collective-permute-done | bytes 139296 | tf_op jit(solution)/shard_map/ppermute | solution.py:202
  32.9 1.7 %shard_map.112 = (f32[256,1024]{1,0:T(8,128)S(1)}, bf16[256,1024]{1,0:T(8,128)(2,1)S(1)}) custom-call(bf16[128,2176]{1,0:T(8,128)(2,1)S(1)} %get-tuple-element.24.refs_0_, bf16[128,2176]{1,0:T(8,128)(2,1)S(1)} %collective-permute-done.refs_1_, f32[128,1024]{1,0:T(8,128)S(1)} %get-tuple-element.25.refs_2_, f32[128,1024]{1,0:T(8,128)S(1)} %get-tuple-element.26.refs_3_, ...), custom_call_target="tpu_custom_call" | custom-call | flops 1107296256 | bytes 4325376 | tf_op jit(solution)/shard_map/pallas_call | solution.py:26
  34.7 2.6 %shard_map.118 = (f32[256,1024]{1,0:T(8,128)S(1)}, bf16[256,1024]{1,0:T(8,128)(2,1)S(1)}) custom-call(bf16[128,2176]{1,0:T(8,128)(2,1)S(1)} %shard_map.117.refs_0_, bf16[128,2176]{1,0:T(8,128)(2,1)S(1)} %collective-permute-done.19.refs_1_, bf16[704,2048]{1,0:T(8,128)(2,1)S(1)} %bitcast.25, bf16[704,2048]{1,0:T(8,128)(2,1)S(1)} %bitcast.30, ...), custom_call_target="tpu_custom_call" | custom-call | flops 2214592512 | bytes 8650752 | tf_op jit(solution)/shard_map/pallas_call | solution.py:26
  37.9 2.6 %shard_map.116 = (f32[256,1024]{1,0:T(8,128)S(1)}, bf16[256,1024]{1,0:T(8,128)(2,1)S(1)}) custom-call(bf16[128,2176]{1,0:T(8,128)(2,1)S(1)} %shard_map.115.refs_0_, bf16[128,2176]{1,0:T(8,128)(2,1)S(1)} %collective-permute-done.13.refs_1_, bf16[704,2048]{1,0:T(8,128)(2,1)S(1)} %bitcast.26, bf16[704,2048]{1,0:T(8,128)(2,1)S(1)} %bitcast.31, ...), custom_call_target="tpu_custom_call" | custom-call | flops 2214592512 | bytes 8650752 | tf_op jit(solution)/shard_map/pallas_call | solution.py:26
  40.7 2.1 %shard_map.120 = (bf16[128,1024]{1,0:T(8,128)(2,1)S(1)}, bf16[704,128]{1,0:T(8,128)(2,1)S(1)}) custom-call(bf16[64,2176]{1,0:T(8,128)(2,1)S(1)} %shard_map.119.refs_0_, bf16[64,2176]{1,0:T(8,128)(2,1)S(1)} %collective-permute-done.23.refs_1_, bf16[704,2048]{1,0:T(8,128)(2,1)S(1)} %bitcast.27, bf16[704,2048]{1,0:T(8,128)(2,1)S(1)} %bitcast.32, ...), custom_call_target="tpu_custom_call" | custom-call | flops 922746880 | bytes 8650752 | tf_op jit(solution)/shard_map/pallas_call | solution.py:26
  43.4 2.6 %shard_map.114 = (f32[256,1024]{1,0:T(8,128)S(1)}, bf16[256,1024]{1,0:T(8,128)(2,1)S(1)}) custom-call(bf16[128,2176]{1,0:T(8,128)(2,1)S(1)} %shard_map.113.refs_0_, bf16[128,2176]{1,0:T(8,128)(2,1)S(1)} %collective-permute-done.7.refs_1_, bf16[704,2048]{1,0:T(8,128)(2,1)S(1)} %bitcast.28, bf16[704,2048]{1,0:T(8,128)(2,1)S(1)} %bitcast.33, ...), custom_call_target="tpu_custom_call" | custom-call | flops 2214592512 | bytes 8650752 | tf_op jit(solution)/shard_map/pallas_call | solution.py:26
  46.6 1.7 %collective-permute-start.35 = (bf16[64,1024]{1,0:T(8,128)(2,1)S(1)}, bf16[64,1024]{1,0:T(8,128)(2,1)S(1)}, u32[]{:S(2)}, u32[]{:S(2)}) collective-permute-start(bf16[64,1024]{1,0:T(8,128)(2,1)S(1)} %get-tuple-element.42), channel_id=1, source_target_pairs={{4,0},{8,4},{12,8},{14,12},{10,14},{6,10},{2,6},{0,2},{5,1},{9,5},... | collective-permute-start | bytes 393224 | tf_op jit(solution)/shard_map/ppermute | solution.py:203
  48.8 3.7 %collective-permute-done.35.refs_2_ = bf16[64,1024]{1,0:T(8,128)(2,1)S(1)} collective-permute-done((bf16[64,1024]{1,0:T(8,128)(2,1)S(1)}, bf16[64,1024]{1,0:T(8,128)(2,1)S(1)}, u32[]{:S(2)}, u32[]{:S(2)}) %collective-permute-start.35) | collective-permute-done | bytes 131104 | tf_op jit(solution)/shard_map/ppermute | solution.py:203
  52.5 1.3 %collective-permute-start.29 = (bf16[64,1024]{1,0:T(8,128)(2,1)S(1)}, bf16[64,1024]{1,0:T(8,128)(2,1)S(1)}, u32[]{:S(2)}, u32[]{:S(2)}) collective-permute-start(bf16[64,1024]{1,0:T(8,128)(2,1)S(1)} %get-tuple-element.40), channel_id=1, source_target_pairs={{0,4},{4,8},{8,12},{12,14},{14,10},{10,6},{6,2},{2,0},{1,5},{5,9},... | collective-permute-start | bytes 393224 | tf_op jit(solution)/shard_map/ppermute | solution.py:202
  53.9 1.5 %collective-permute-start.32 = (bf16[64,1024]{1,0:T(8,128)(2,1)S(1)}, bf16[64,1024]{1,0:T(8,128)(2,1)S(1)}, u32[]{:S(2)}, u32[]{:S(2)}) collective-permute-start(bf16[64,1024]{1,0:T(8,128)(2,1)S(1)} %get-tuple-element.41), channel_id=1, source_target_pairs={{4,0},{8,4},{12,8},{14,12},{10,14},{6,10},{2,6},{0,2},{5,1},{9,5},... | collective-permute-start | bytes 393224 | tf_op jit(solution)/shard_map/ppermute | solution.py:203
  56.1 1.4 %collective-permute-start.36 = (bf16[64,1024]{1,0:T(8,128)(2,1)S(1)}, bf16[64,1024]{1,0:T(8,128)(2,1)S(1)}, u32[]{:S(2)}, u32[]{:S(2)}) collective-permute-start(bf16[64,1024]{1,0:T(8,128)(2,1)S(1)} %shard_map.131), channel_id=1, source_target_pairs={{4,0},{8,4},{12,8},{14,12},{10,14},{6,10},{2,6},{0,2},{5,1},{9,5},... | collective-permute-start | bytes 393224 | tf_op jit(solution)/shard_map/ppermute | solution.py:203
  57.7 2.7 %collective-permute-done.26.refs_2_ = bf16[64,1024]{1,0:T(8,128)(2,1)S(1)} collective-permute-done((bf16[64,1024]{1,0:T(8,128)(2,1)S(1)}, bf16[64,1024]{1,0:T(8,128)(2,1)S(1)}, u32[]{:S(2)}, u32[]{:S(2)}) %collective-permute-start.26) | collective-permute-done | bytes 131104 | tf_op jit(solution)/shard_map/ppermute | solution.py:202
  60.5 1.2 %collective-permute-start.27 = (bf16[64,1024]{1,0:T(8,128)(2,1)S(1)}, bf16[64,1024]{1,0:T(8,128)(2,1)S(1)}, u32[]{:S(2)}, u32[]{:S(2)}) collective-permute-start(bf16[64,1024]{1,0:T(8,128)(2,1)S(1)} %shard_map.124), channel_id=1, source_target_pairs={{0,4},{4,8},{8,12},{12,14},{14,10},{10,6},{6,2},{2,0},{1,5},{5,9},... | collective-permute-start | bytes 393224 | tf_op jit(solution)/shard_map/ppermute | solution.py:202
  61.7 1.5 %collective-permute-start.2 = (bf16[128,1024]{1,0:T(8,128)(2,1)S(1)}, bf16[128,1024]{1,0:T(8,128)(2,1)S(1)}, u32[]{:S(2)}, u32[]{:S(2)}) collective-permute-start(bf16[128,1024]{1,0:T(8,128)(2,1)S(1)} %slice.7), channel_id=1, source_target_pairs={{0,16},{16,0},{1,17},{17,1},{2,18},{18,2},{3,19},{19,3},{4,20},{20... | collective-permute-start | bytes 786440 | tf_op jit(solution)/shard_map/ppermute | solution.py:205
  63.3 1.5 %collective-permute-start.30 = (bf16[64,1024]{1,0:T(8,128)(2,1)S(1)}, bf16[64,1024]{1,0:T(8,128)(2,1)S(1)}, u32[]{:S(2)}, u32[]{:S(2)}) collective-permute-start(bf16[64,1024]{1,0:T(8,128)(2,1)S(1)} %shard_map.127), channel_id=1, source_target_pairs={{0,4},{4,8},{8,12},{12,14},{14,10},{10,6},{6,2},{2,0},{1,5},{5,9},... | collective-permute-start | bytes 393224 | tf_op jit(solution)/shard_map/ppermute | solution.py:202
  68.1 1.6 %collective-permute-done.30.refs_2_ = bf16[64,1024]{1,0:T(8,128)(2,1)S(1)} collective-permute-done((bf16[64,1024]{1,0:T(8,128)(2,1)S(1)}, bf16[64,1024]{1,0:T(8,128)(2,1)S(1)}, u32[]{:S(2)}, u32[]{:S(2)}) %collective-permute-start.30) | collective-permute-done | bytes 131104 | tf_op jit(solution)/shard_map/ppermute | solution.py:202
  69.8 1.2 %collective-permute-start.31 = (bf16[64,1024]{1,0:T(8,128)(2,1)S(1)}, bf16[64,1024]{1,0:T(8,128)(2,1)S(1)}, u32[]{:S(2)}, u32[]{:S(2)}) collective-permute-start(bf16[64,1024]{1,0:T(8,128)(2,1)S(1)} %shard_map.128), channel_id=1, source_target_pairs={{0,4},{4,8},{8,12},{12,14},{14,10},{10,6},{6,2},{2,0},{1,5},{5,9},... | collective-permute-start | bytes 393224 | tf_op jit(solution)/shard_map/ppermute | solution.py:202
  72.8 2.0 %collective-permute-done.31.ahead_two = bf16[64,1024]{1,0:T(8,128)(2,1)S(1)} collective-permute-done((bf16[64,1024]{1,0:T(8,128)(2,1)S(1)}, bf16[64,1024]{1,0:T(8,128)(2,1)S(1)}, u32[]{:S(2)}, u32[]{:S(2)}) %collective-permute-start.31) | collective-permute-done | bytes 131104 | tf_op jit(solution)/shard_map/ppermute | solution.py:202
  74.8 1.3 %collective-permute-done.34.back_one = bf16[64,1024]{1,0:T(8,128)(2,1)S(1)} collective-permute-done((bf16[64,1024]{1,0:T(8,128)(2,1)S(1)}, bf16[64,1024]{1,0:T(8,128)(2,1)S(1)}, u32[]{:S(2)}, u32[]{:S(2)}) %collective-permute-start.34) | collective-permute-done | bytes 131104 | tf_op jit(solution)/shard_map/ppermute | solution.py:203
  76.1 1.4 %collective-permute-done.38.back_two = bf16[64,1024]{1,0:T(8,128)(2,1)S(1)} collective-permute-done((bf16[64,1024]{1,0:T(8,128)(2,1)S(1)}, bf16[64,1024]{1,0:T(8,128)(2,1)S(1)}, u32[]{:S(2)}, u32[]{:S(2)}) %collective-permute-start.38) | collective-permute-done | bytes 131104 | tf_op jit(solution)/shard_map/ppermute | solution.py:203
  (96 shorter events, 16.1 us)
Async XLA Ops:
  1.7 7.6 %collective-permute-start.5 = (bf16[32,2176]{1,0:T(8,128)(2,1)S(1)}, bf16[32,2176]{1,0:T(8,128)(2,1)S(1)}, u32[]{:S(2)}, u32[]{:S(2)}) collective-permute-start(bf16[32,2176]{1,0:T(8,128)(2,1)S(1)} %get-tuple-element.29), channel_id=1, source_target_pairs={{4,0},{8,4},{12,8},{14,12},{10,14},{6,10},{2,6},{0,2},{5,1},{9,5},... | collective-permute-start | bytes 417800 | tf_op jit(solution)/shard_map/ppermute | solution.py:203
  4.8 6.5 %collective-permute-start.3 = (bf16[32,2176]{1,0:T(8,128)(2,1)S(1)}, bf16[32,2176]{1,0:T(8,128)(2,1)S(1)}, u32[]{:S(2)}, u32[]{:S(2)}) collective-permute-start(bf16[32,2176]{1,0:T(8,128)(2,1)S(1)} %get-tuple-element.29), channel_id=1, source_target_pairs={{0,4},{4,8},{8,12},{12,14},{14,10},{10,6},{6,2},{2,0},{1,5},{5,9},... | collective-permute-start | bytes 417800 | tf_op jit(solution)/shard_map/ppermute | solution.py:202
  4.9 7.4 %collective-permute-start.6 = (bf16[32,2176]{1,0:T(8,128)(2,1)S(1)}, bf16[32,2176]{1,0:T(8,128)(2,1)S(1)}, u32[]{:S(2)}, u32[]{:S(2)}) collective-permute-start(bf16[32,2176]{1,0:T(8,128)(2,1)S(1)} %get-tuple-element.30), channel_id=1, source_target_pairs={{4,0},{8,4},{12,8},{14,12},{10,14},{6,10},{2,6},{0,2},{5,1},{9,5},... | collective-permute-start | bytes 417800 | tf_op jit(solution)/shard_map/ppermute | solution.py:203
  6.8 7.5 %collective-permute-start.4 = (bf16[32,2176]{1,0:T(8,128)(2,1)S(1)}, bf16[32,2176]{1,0:T(8,128)(2,1)S(1)}, u32[]{:S(2)}, u32[]{:S(2)}) collective-permute-start(bf16[32,2176]{1,0:T(8,128)(2,1)S(1)} %get-tuple-element.30), channel_id=1, source_target_pairs={{0,4},{4,8},{8,12},{12,14},{14,10},{10,6},{6,2},{2,0},{1,5},{5,9},... | collective-permute-start | bytes 417800 | tf_op jit(solution)/shard_map/ppermute | solution.py:202
  9.4 6.2 %collective-permute-start.11 = (bf16[32,2176]{1,0:T(8,128)(2,1)S(1)}, bf16[32,2176]{1,0:T(8,128)(2,1)S(1)}, u32[]{:S(2)}, u32[]{:S(2)}) collective-permute-start(bf16[32,2176]{1,0:T(8,128)(2,1)S(1)} %collective-permute-done.5.refs_2_), channel_id=1, source_target_pairs={{4,0},{8,4},{12,8},{14,12},{10,14},{6,10},{2,6},{0,2},{5,1},{9,5},... | collective-permute-start | bytes 417800 | tf_op jit(solution)/shard_map/ppermute | solution.py:203
  11.3 6.5 %collective-permute-start.9 = (bf16[32,2176]{1,0:T(8,128)(2,1)S(1)}, bf16[32,2176]{1,0:T(8,128)(2,1)S(1)}, u32[]{:S(2)}, u32[]{:S(2)}) collective-permute-start(bf16[32,2176]{1,0:T(8,128)(2,1)S(1)} %collective-permute-done.3.refs_0_), channel_id=1, source_target_pairs={{0,4},{4,8},{8,12},{12,14},{14,10},{10,6},{6,2},{2,0},{1,5},{5,9},... | collective-permute-start | bytes 417800 | tf_op jit(solution)/shard_map/ppermute | solution.py:202
  12.3 6.5 %collective-permute-start.12 = (bf16[32,2176]{1,0:T(8,128)(2,1)S(1)}, bf16[32,2176]{1,0:T(8,128)(2,1)S(1)}, u32[]{:S(2)}, u32[]{:S(2)}) collective-permute-start(bf16[32,2176]{1,0:T(8,128)(2,1)S(1)} %collective-permute-done.6.refs_3_), channel_id=1, source_target_pairs={{4,0},{8,4},{12,8},{14,12},{10,14},{6,10},{2,6},{0,2},{5,1},{9,5},... | collective-permute-start | bytes 417800 | tf_op jit(solution)/shard_map/ppermute | solution.py:203
  14.3 6.5 %collective-permute-start.10 = (bf16[32,2176]{1,0:T(8,128)(2,1)S(1)}, bf16[32,2176]{1,0:T(8,128)(2,1)S(1)}, u32[]{:S(2)}, u32[]{:S(2)}) collective-permute-start(bf16[32,2176]{1,0:T(8,128)(2,1)S(1)} %collective-permute-done.4.refs_1_), channel_id=1, source_target_pairs={{0,4},{4,8},{8,12},{12,14},{14,10},{10,6},{6,2},{2,0},{1,5},{5,9},... | collective-permute-start | bytes 417800 | tf_op jit(solution)/shard_map/ppermute | solution.py:202
  15.6 7.2 %collective-permute-start.17 = (bf16[32,2176]{1,0:T(8,128)(2,1)S(1)}, bf16[32,2176]{1,0:T(8,128)(2,1)S(1)}, u32[]{:S(2)}, u32[]{:S(2)}) collective-permute-start(bf16[32,2176]{1,0:T(8,128)(2,1)S(1)} %collective-permute-done.11.refs_2_), channel_id=1, source_target_pairs={{4,0},{8,4},{12,8},{14,12},{10,14},{6,10},{2,6},{0,2},{5,1},{9,5},... | collective-permute-start | bytes 417800 | tf_op jit(solution)/shard_map/ppermute | solution.py:203
  17.9 5.6 %collective-permute-start.15 = (bf16[32,2176]{1,0:T(8,128)(2,1)S(1)}, bf16[32,2176]{1,0:T(8,128)(2,1)S(1)}, u32[]{:S(2)}, u32[]{:S(2)}) collective-permute-start(bf16[32,2176]{1,0:T(8,128)(2,1)S(1)} %collective-permute-done.9.refs_0_), channel_id=1, source_target_pairs={{0,4},{4,8},{8,12},{12,14},{14,10},{10,6},{6,2},{2,0},{1,5},{5,9},... | collective-permute-start | bytes 417800 | tf_op jit(solution)/shard_map/ppermute | solution.py:202
  21.0 11.9 %collective-permute-start = (bf16[128,2176]{1,0:T(8,128)(2,1)S(1)}, bf16[128,2176]{1,0:T(8,128)(2,1)S(1)}, u32[]{:S(2)}, u32[]{:S(2)}) collective-permute-start(bf16[128,2176]{1,0:T(8,128)(2,1)S(1)} %get-tuple-element.24.refs_0_), channel_id=1, source_target_pairs={{0,16},{16,0},{1,17},{17,1},{2,18},{18,2},{3,19},{19,3},{4,20},{20... | collective-permute-start | bytes 1671176 | tf_op jit(solution)/shard_map/ppermute | solution.py:205
  25.9 8.8 %collective-permute-start.19 = (bf16[128,2176]{1,0:T(8,128)(2,1)S(1)}, bf16[128,2176]{1,0:T(8,128)(2,1)S(1)}, u32[]{:S(2)}, u32[]{:S(2)}) collective-permute-start(bf16[128,2176]{1,0:T(8,128)(2,1)S(1)} %shard_map.117.refs_0_), channel_id=1, source_target_pairs={{0,1},{1,0},{2,3},{3,2},{4,5},{5,4},{6,7},{7,6},{8,9},{9,8},{10,11... | collective-permute-start | bytes 1671176 | tf_op jit(solution)/shard_map/ppermute | solution.py:204
  26.1 11.8 %collective-permute-start.13 = (bf16[128,2176]{1,0:T(8,128)(2,1)S(1)}, bf16[128,2176]{1,0:T(8,128)(2,1)S(1)}, u32[]{:S(2)}, u32[]{:S(2)}) collective-permute-start(bf16[128,2176]{1,0:T(8,128)(2,1)S(1)} %shard_map.115.refs_0_), channel_id=1, source_target_pairs={{0,1},{1,0},{2,3},{3,2},{4,5},{5,4},{6,7},{7,6},{8,9},{9,8},{10,11... | collective-permute-start | bytes 1671176 | tf_op jit(solution)/shard_map/ppermute | solution.py:204
  26.6 5.6 %collective-permute-start.21 = (bf16[32,2176]{1,0:T(8,128)(2,1)S(1)}, bf16[32,2176]{1,0:T(8,128)(2,1)S(1)}, u32[]{:S(2)}, u32[]{:S(2)}) collective-permute-start(bf16[32,2176]{1,0:T(8,128)(2,1)S(1)} %collective-permute-done.15.refs_0_), channel_id=1, source_target_pairs={{0,4},{4,8},{8,12},{12,14},{14,10},{10,6},{6,2},{2,0},{1,5},{5,9},... | collective-permute-start | bytes 417800 | tf_op jit(solution)/shard_map/ppermute | solution.py:202
  26.8 5.6 %collective-permute-start.22 = (bf16[32,2176]{1,0:T(8,128)(2,1)S(1)}, bf16[32,2176]{1,0:T(8,128)(2,1)S(1)}, u32[]{:S(2)}, u32[]{:S(2)}) collective-permute-start(bf16[32,2176]{1,0:T(8,128)(2,1)S(1)} %collective-permute-done.18.refs_3_), channel_id=1, source_target_pairs={{4,0},{8,4},{12,8},{14,12},{10,14},{6,10},{2,6},{0,2},{5,1},{9,5},... | collective-permute-start | bytes 417800 | tf_op jit(solution)/shard_map/ppermute | solution.py:203
  32.3 11.1 %collective-permute-start.7 = (bf16[128,2176]{1,0:T(8,128)(2,1)S(1)}, bf16[128,2176]{1,0:T(8,128)(2,1)S(1)}, u32[]{:S(2)}, u32[]{:S(2)}) collective-permute-start(bf16[128,2176]{1,0:T(8,128)(2,1)S(1)} %shard_map.113.refs_0_), channel_id=1, source_target_pairs={{0,1},{1,0},{2,3},{3,2},{4,5},{5,4},{6,7},{7,6},{8,9},{9,8},{10,11... | collective-permute-start | bytes 1671176 | tf_op jit(solution)/shard_map/ppermute | solution.py:204
  32.4 8.3 %collective-permute-start.23 = (bf16[64,2176]{1,0:T(8,128)(2,1)S(1)}, bf16[64,2176]{1,0:T(8,128)(2,1)S(1)}, u32[]{:S(2)}, u32[]{:S(2)}) collective-permute-start(bf16[64,2176]{1,0:T(8,128)(2,1)S(1)} %shard_map.119.refs_0_), channel_id=1, source_target_pairs={{0,1},{1,0},{2,3},{3,2},{4,5},{5,4},{6,7},{7,6},{8,9},{9,8},{10,11... | collective-permute-start | bytes 835592 | tf_op jit(solution)/shard_map/ppermute | solution.py:204
  34.6 20.8 %collective-permute-start.1 = (bf16[256,1024]{1,0:T(8,128)(2,1)S(1)}, bf16[256,1024]{1,0:T(8,128)(2,1)S(1)}, u32[]{:S(2)}, u32[]{:S(2)}) collective-permute-start(bf16[256,1024]{1,0:T(8,128)(2,1)S(1)} %get-tuple-element.28), channel_id=1, source_target_pairs={{0,1},{1,0},{2,3},{3,2},{4,5},{5,4},{6,7},{7,6},{8,9},{9,8},{10,11... | collective-permute-start | bytes 1572872 | tf_op jit(solution)/shard_map/ppermute | solution.py:204
  37.4 11.0 %collective-permute-start.20 = (bf16[256,1024]{1,0:T(8,128)(2,1)S(1)}, bf16[256,1024]{1,0:T(8,128)(2,1)S(1)}, u32[]{:S(2)}, u32[]{:S(2)}) collective-permute-start(bf16[256,1024]{1,0:T(8,128)(2,1)S(1)} %get-tuple-element.36), channel_id=1, source_target_pairs={{0,1},{1,0},{2,3},{3,2},{4,5},{5,4},{6,7},{7,6},{8,9},{9,8},{10,11... | collective-permute-start | bytes 1572872 | tf_op jit(solution)/shard_map/ppermute | solution.py:204
  40.6 15.5 %collective-permute-start.14 = (bf16[256,1024]{1,0:T(8,128)(2,1)S(1)}, bf16[256,1024]{1,0:T(8,128)(2,1)S(1)}, u32[]{:S(2)}, u32[]{:S(2)}) collective-permute-start(bf16[256,1024]{1,0:T(8,128)(2,1)S(1)} %get-tuple-element.34), channel_id=1, source_target_pairs={{0,1},{1,0},{2,3},{3,2},{4,5},{5,4},{6,7},{7,6},{8,9},{9,8},{10,11... | collective-permute-start | bytes 1572872 | tf_op jit(solution)/shard_map/ppermute | solution.py:204
  46.0 19.5 %collective-permute-start.8 = (bf16[256,1024]{1,0:T(8,128)(2,1)S(1)}, bf16[256,1024]{1,0:T(8,128)(2,1)S(1)}, u32[]{:S(2)}, u32[]{:S(2)}) collective-permute-start(bf16[256,1024]{1,0:T(8,128)(2,1)S(1)} %get-tuple-element.32), channel_id=1, source_target_pairs={{0,1},{1,0},{2,3},{3,2},{4,5},{5,4},{6,7},{7,6},{8,9},{9,8},{10,11... | collective-permute-start | bytes 1572872 | tf_op jit(solution)/shard_map/ppermute | solution.py:204
  46.6 5.9 %collective-permute-start.35 = (bf16[64,1024]{1,0:T(8,128)(2,1)S(1)}, bf16[64,1024]{1,0:T(8,128)(2,1)S(1)}, u32[]{:S(2)}, u32[]{:S(2)}) collective-permute-start(bf16[64,1024]{1,0:T(8,128)(2,1)S(1)} %get-tuple-element.42), channel_id=1, source_target_pairs={{4,0},{8,4},{12,8},{14,12},{10,14},{6,10},{2,6},{0,2},{5,1},{9,5},... | collective-permute-start | bytes 393224 | tf_op jit(solution)/shard_map/ppermute | solution.py:203
  48.4 5.5 %collective-permute-start.25 = (bf16[64,1024]{1,0:T(8,128)(2,1)S(1)}, bf16[64,1024]{1,0:T(8,128)(2,1)S(1)}, u32[]{:S(2)}, u32[]{:S(2)}) collective-permute-start(bf16[64,1024]{1,0:T(8,128)(2,1)S(1)} %get-tuple-element.39), channel_id=1, source_target_pairs={{0,4},{4,8},{8,12},{12,14},{14,10},{10,6},{6,2},{2,0},{1,5},{5,9},... | collective-permute-start | bytes 393224 | tf_op jit(solution)/shard_map/ppermute | solution.py:202
  52.5 9.2 %collective-permute-start.29 = (bf16[64,1024]{1,0:T(8,128)(2,1)S(1)}, bf16[64,1024]{1,0:T(8,128)(2,1)S(1)}, u32[]{:S(2)}, u32[]{:S(2)}) collective-permute-start(bf16[64,1024]{1,0:T(8,128)(2,1)S(1)} %get-tuple-element.40), channel_id=1, source_target_pairs={{0,4},{4,8},{8,12},{12,14},{14,10},{10,6},{6,2},{2,0},{1,5},{5,9},... | collective-permute-start | bytes 393224 | tf_op jit(solution)/shard_map/ppermute | solution.py:202
  53.9 9.4 %collective-permute-start.32 = (bf16[64,1024]{1,0:T(8,128)(2,1)S(1)}, bf16[64,1024]{1,0:T(8,128)(2,1)S(1)}, u32[]{:S(2)}, u32[]{:S(2)}) collective-permute-start(bf16[64,1024]{1,0:T(8,128)(2,1)S(1)} %get-tuple-element.41), channel_id=1, source_target_pairs={{4,0},{8,4},{12,8},{14,12},{10,14},{6,10},{2,6},{0,2},{5,1},{9,5},... | collective-permute-start | bytes 393224 | tf_op jit(solution)/shard_map/ppermute | solution.py:203
  56.1 8.7 %collective-permute-start.36 = (bf16[64,1024]{1,0:T(8,128)(2,1)S(1)}, bf16[64,1024]{1,0:T(8,128)(2,1)S(1)}, u32[]{:S(2)}, u32[]{:S(2)}) collective-permute-start(bf16[64,1024]{1,0:T(8,128)(2,1)S(1)} %shard_map.131), channel_id=1, source_target_pairs={{4,0},{8,4},{12,8},{14,12},{10,14},{6,10},{2,6},{0,2},{5,1},{9,5},... | collective-permute-start | bytes 393224 | tf_op jit(solution)/shard_map/ppermute | solution.py:203
  60.5 6.4 %collective-permute-start.27 = (bf16[64,1024]{1,0:T(8,128)(2,1)S(1)}, bf16[64,1024]{1,0:T(8,128)(2,1)S(1)}, u32[]{:S(2)}, u32[]{:S(2)}) collective-permute-start(bf16[64,1024]{1,0:T(8,128)(2,1)S(1)} %shard_map.124), channel_id=1, source_target_pairs={{0,4},{4,8},{8,12},{12,14},{14,10},{10,6},{6,2},{2,0},{1,5},{5,9},... | collective-permute-start | bytes 393224 | tf_op jit(solution)/shard_map/ppermute | solution.py:202
  61.7 11.0 %collective-permute-start.2 = (bf16[128,1024]{1,0:T(8,128)(2,1)S(1)}, bf16[128,1024]{1,0:T(8,128)(2,1)S(1)}, u32[]{:S(2)}, u32[]{:S(2)}) collective-permute-start(bf16[128,1024]{1,0:T(8,128)(2,1)S(1)} %slice.7), channel_id=1, source_target_pairs={{0,16},{16,0},{1,17},{17,1},{2,18},{18,2},{3,19},{19,3},{4,20},{20... | collective-permute-start | bytes 786440 | tf_op jit(solution)/shard_map/ppermute | solution.py:205
  63.3 6.5 %collective-permute-start.30 = (bf16[64,1024]{1,0:T(8,128)(2,1)S(1)}, bf16[64,1024]{1,0:T(8,128)(2,1)S(1)}, u32[]{:S(2)}, u32[]{:S(2)}) collective-permute-start(bf16[64,1024]{1,0:T(8,128)(2,1)S(1)} %shard_map.127), channel_id=1, source_target_pairs={{0,4},{4,8},{8,12},{12,14},{14,10},{10,6},{6,2},{2,0},{1,5},{5,9},... | collective-permute-start | bytes 393224 | tf_op jit(solution)/shard_map/ppermute | solution.py:202
  64.8 6.2 %collective-permute-start.33 = (bf16[64,1024]{1,0:T(8,128)(2,1)S(1)}, bf16[64,1024]{1,0:T(8,128)(2,1)S(1)}, u32[]{:S(2)}, u32[]{:S(2)}) collective-permute-start(bf16[64,1024]{1,0:T(8,128)(2,1)S(1)} %shard_map.129), channel_id=1, source_target_pairs={{4,0},{8,4},{12,8},{14,12},{10,14},{6,10},{2,6},{0,2},{5,1},{9,5},... | collective-permute-start | bytes 393224 | tf_op jit(solution)/shard_map/ppermute | solution.py:203
  65.5 6.5 %collective-permute-start.37 = (bf16[64,1024]{1,0:T(8,128)(2,1)S(1)}, bf16[64,1024]{1,0:T(8,128)(2,1)S(1)}, u32[]{:S(2)}, u32[]{:S(2)}) collective-permute-start(bf16[64,1024]{1,0:T(8,128)(2,1)S(1)} %shard_map.132), channel_id=1, source_target_pairs={{4,0},{8,4},{12,8},{14,12},{10,14},{6,10},{2,6},{0,2},{5,1},{9,5},... | collective-permute-start | bytes 393224 | tf_op jit(solution)/shard_map/ppermute | solution.py:203
  67.0 5.8 %collective-permute-start.28 = (bf16[64,1024]{1,0:T(8,128)(2,1)S(1)}, bf16[64,1024]{1,0:T(8,128)(2,1)S(1)}, u32[]{:S(2)}, u32[]{:S(2)}) collective-permute-start(bf16[64,1024]{1,0:T(8,128)(2,1)S(1)} %shard_map.125), channel_id=1, source_target_pairs={{0,4},{4,8},{8,12},{12,14},{14,10},{10,6},{6,2},{2,0},{1,5},{5,9},... | collective-permute-start | bytes 393224 | tf_op jit(solution)/shard_map/ppermute | solution.py:202
  (18 other events, 137.0 us)

commit v4 on v3

--- a/solution.py
+++ b/solution.py
@@ -38,7 +38,7 @@
     out[...] = jnp.zeros_like(out)
 
 
-def prologue_body(expert_count, lead, tokens, gain, router, ids, modality, packed, lower, upper):
+def prologue_body(expert_count, lead, tokens, gain, router, ids, modality, packed, *parts):
     width = tokens.shape[1]
     values = tokens[...].astype(jnp.float32)
     scale = lax.rsqrt(jnp.mean(values * values, axis=1, keepdims=True) + epsilon)
@@ -53,14 +53,23 @@
     weights = scores / jnp.sum(scores, axis=0, keepdims=True)
     rounded = weights.astype(jnp.bfloat16).astype(jnp.float32)
     image = (modality[...] == 1).astype(jnp.float32)
-    rows = packed.shape[1] - width - 2 * expert_count
-    first = lax.broadcasted_iota(jnp.int32, (rows, image.shape[1]), 0) == 0
+    count = image.shape[1]
+    group = (packed.shape[1] - width) // 2
+    rows = group - 2 * expert_count
+    first = lax.broadcasted_iota(jnp.int32, (rows, count), 0) == 0
     table = jnp.concatenate([rounded, weights - rounded, jnp.where(first, image, 0.0)], axis=0)
-    packed[:, width:] = table.T.astype(jnp.bfloat16)
-    part = lower.shape[0]
+    up_long, down_long, up_short, down_short, both = parts
+    part = up_long.shape[0]
     start = pl.multiple_of(lax.axis_index("tensor") * 2 * part, 2 * part)
-    lower[...] = packed[pl.ds(start, part), :]
-    upper[...] = packed[pl.ds(start + part, part), :]
+    places = (pl.ds(start, part), pl.ds(start + part, part))
+    for out, place, shift in ((up_long, places[0], count - part), (down_long, places[1], part)):
+        pair = jnp.concatenate([table, pltpu.roll(table, shift, 1)], axis=0)
+        both[...] = pair.T
+        out[:, :width] = packed[place, :width]
+        out[:, width:] = both[place, :].astype(jnp.bfloat16)
+    up_short[...] = packed[places[1], :width]
+    down_short[...] = packed[places[0], :width]
+    packed[:, width:] = jnp.concatenate([table, jnp.zeros_like(table)], axis=0).T.astype(jnp.bfloat16)
 
 
 def side_rows(rows, width, lanes):
@@ -79,15 +88,26 @@
 def expert_hidden(expert_count, rows, gate, up):
     width = gate.shape[1]
     me = lax.axis_index("expert")
-    factor = side_rows(rows, width, (me, me + expert_count))
+    group = (rows.shape[1] - width) // 2
+    lanes = [me + base + group * i for base in (0, expert_count) for i in range(2)]
+    factor = side_rows(rows, width, lanes)
     rows = rows[:, :width]
     return gated(dot(gate[...], rows, NT), dot(up[...], rows, NT), factor)
 
 
-def pack_body(*refs):
-    part = refs[0].shape[0]
-    for index, piece in enumerate(refs[:-1]):
-        refs[-1][index * part : (index + 1) * part, :] = piece[...]
+def pack_body(width, *refs):
+    pieces, out = refs[:-1], refs[-1]
+    part = pieces[0].shape[0]
+    long = (pieces[0], pieces[-1])
+    lane = lax.broadcasted_iota(jnp.int32, (part, out.shape[1] - width), 1)
+    led = lane >= lane.shape[1] // 2
+    for index, piece in enumerate(pieces):
+        place = slice(index * part, (index + 1) * part)
+        side = long[2 * index // len(pieces)][:, width:].astype(jnp.float32)
+        brought = piece.shape[1] == width
+        side = jnp.where(led if brought else jnp.logical_not(led), side, 0.0)
+        out[place, :width] = piece[:, :width]
+        out[place, width:] = side.astype(out.dtype)
 
 
 def pair_body(expert_count, mine, theirs, gate, up, down, keep, give, rows):
@@ -191,7 +211,7 @@
     half, columns = count // 2, width // 2
     quarter = half // 2
     experts = lax.axis_size("expert")
-    side = -(-(2 * experts + 1) // LANES) * LANES
+    side = -(-2 * (2 * experts + 1) // LANES) * LANES
     middle = experts // 2
     shape = jax.ShapeDtypeStruct
     f32, bf16 = jnp.float32, jnp.bfloat16
@@ -216,13 +236,16 @@
     )
     inputs = (tokens, norm_gain[None, :], router.T, expert_ids.T, modality[None, :])
     lead = call(lead_body, shape((8, LANES), f32), (), 1, 2**34, MIB)
-    own, lower, upper = call(
+    own, *parts = call(
         lambda *refs: prologue_body(experts, *refs),
-        (shape((count, width + side), bf16),) + (shape((quarter, width + side), bf16),) * 2,
+        (shape((count, width + side), bf16),)
+        + (shape((quarter, width + side), bf16),) * 2
+        + (shape((quarter, width), bf16),) * 2,
         (lead, *inputs),
         8,
         4 * MIB,
         MIB,
+        [pltpu.VMEM((count, side), f32)],
     )
     other = dp_swap(own)
     weights = stored
@@ -293,11 +316,14 @@
 
     def packed(pieces):
         rows = len(pieces) * pieces[0].shape[0]
-        return call(pack_body, shape((rows, width + side), bf16), pieces, 4)
+        return call(
+            lambda *refs: pack_body(width, *refs),
+            shape((rows, width + side), bf16), pieces, 4,
+        )
 
     keep, recv = {}, {}
     own_sums = own_part(own)
-    long, short = (lower, upper), (upper, lower)
+    long, short = parts[:2], parts[2:]
     for k in range(1, middle + 1):
         long = travel(long)
         if k < middle:
@@ -312,12 +338,7 @@
 
     ahead_base, back_base = count, 0
     short = sums(middle - 1, (ahead_base + half, back_base))
-    long = call(
-        far_add_body,
-        (shape((half, columns), bf16),) * 2,
-        (keep[middle], recv[middle]),
-        8,
-    )
+    long = call(far_add_body, (shape((half, columns), bf16),) * 2, (keep[middle], recv[middle]), 8)
 
     for k in range(middle - 1, 0, -1):
         long = travel(long)

time: 78.4 us -> 77.5 us (0.989)
    ppermute x14, starting transfers between devices: 22.8 us -> 4.02 us  [per_device(): back = lambda x: lax.ppermute(x, 'expert', backward)]
    ppermute x14, starting transfers between devices: 8.19 us -> 26.8 us  [per_device(): ahead = lambda x: lax.ppermute(x, 'expert', onward)]
  transfers between devices with their start and end apart: 39 -> 39, of which waited for: 16 -> 15; matrix products, arithmetic and copies ran while one was open for 0% -> 0% of each run, Pallas kernels for 19% -> 19%
where the time goes in v4:
time: 77.5 us; the launch traced here: 77.3 us
  starting transfers between devices  36.7 us (47%)
  waiting for transfers between devices  22.5 us (29%)
  Pallas kernels  16.5 us (21%)
  local copies, waits for them, and re-layouts  1.12 us (1%)
    ppermute x14, starting transfers between devices, per_device(): ahead = lambda x: lax.ppermute(x, 'expert', onward)  26.8 us
    pallas_call x26, Pallas kernels, call(): pl.pallas_call(body, out_shape=outs, in_specs=[vmem] * len(args), out_spe...  16.5 us
    ppermute x14, waiting for transfers between devices, per_device(): back = lambda x: lax.ppermute(x, 'expert', backward)  12.4 us
    ppermute x14, waiting for transfers between devices, per_device(): ahead = lambda x: lax.ppermute(x, 'expert', onward)  10.1 us
    ppermute x14, starting transfers between devices, per_device(): back = lambda x: lax.ppermute(x, 'expert', backward)  4.02 us
    ppermute x2, starting transfers between devices, per_device(): dp_swap = lambda x: lax.ppermute(x, 'dp', [(0, 1), (1, 0)])  3.29 us
    ppermute x9, starting transfers between devices, per_device(): swap = lambda x: lax.ppermute(x, 'tensor', [(0, 1), (1, 0)])  2.61 us
  transfers between devices with their start and end apart: 39, of which 15 were waited for; matrix products, arithmetic and copies ran while one was open for 0% of the time, Pallas kernels for 19%

profile of v4, /device:TPU:0, one launch (start us, length us, event | category | flops | bytes accessed | tf_op | source)
XLA Modules:
  0.0 77.3 jit_solution(7389445727900810946)
XLA Ops:
  1.8 3.1 %collective-permute-start.3 = (bf16[32,2176]{1,0:T(8,128)(2,1)S(1)}, bf16[32,2176]{1,0:T(8,128)(2,1)S(1)}, u32[]{:S(2)}, u32[]{:S(2)}) collective-permute-start(bf16[32,2176]{1,0:T(8,128)(2,1)S(1)} %get-tuple-element.31), channel_id=1, source_target_pairs={{0,4},{4,8},{8,12},{12,14},{14,10},{10,6},{6,2},{2,0},{1,5},{5,9},... | collective-permute-start | bytes 417800 | tf_op jit(solution)/shard_map/ppermute | solution.py:222
  4.9 2.0 %collective-permute-start.4 = (bf16[32,2048]{1,0:T(8,128)(2,1)S(1)}, bf16[32,2048]{1,0:T(8,128)(2,1)S(1)}, u32[]{:S(2)}, u32[]{:S(2)}) collective-permute-start(bf16[32,2048]{1,0:T(8,128)(2,1)S(1)} %get-tuple-element.32), channel_id=1, source_target_pairs={{0,4},{4,8},{8,12},{12,14},{14,10},{10,6},{6,2},{2,0},{1,5},{5,9},... | collective-permute-start | bytes 393224 | tf_op jit(solution)/shard_map/ppermute | solution.py:222
  7.0 2.4 %collective-permute-done.3.refs_0_ = bf16[32,2176]{1,0:T(8,128)(2,1)S(1)} collective-permute-done((bf16[32,2176]{1,0:T(8,128)(2,1)S(1)}, bf16[32,2176]{1,0:T(8,128)(2,1)S(1)}, u32[]{:S(2)}, u32[]{:S(2)}) %collective-permute-start.3) | collective-permute-done | bytes 139296 | tf_op jit(solution)/shard_map/ppermute | solution.py:222
  9.4 2.1 %collective-permute-start.9 = (bf16[32,2176]{1,0:T(8,128)(2,1)S(1)}, bf16[32,2176]{1,0:T(8,128)(2,1)S(1)}, u32[]{:S(2)}, u32[]{:S(2)}) collective-permute-start(bf16[32,2176]{1,0:T(8,128)(2,1)S(1)} %collective-permute-done.3.refs_0_), channel_id=1, source_target_pairs={{0,4},{4,8},{8,12},{12,14},{14,10},{10,6},{6,2},{2,0},{1,5},{5,9},... | collective-permute-start | bytes 417800 | tf_op jit(solution)/shard_map/ppermute | solution.py:222
  12.2 2.1 %collective-permute-start.10 = (bf16[32,2048]{1,0:T(8,128)(2,1)S(1)}, bf16[32,2048]{1,0:T(8,128)(2,1)S(1)}, u32[]{:S(2)}, u32[]{:S(2)}) collective-permute-start(bf16[32,2048]{1,0:T(8,128)(2,1)S(1)} %collective-permute-done.4.refs_1_), channel_id=1, source_target_pairs={{0,4},{4,8},{8,12},{12,14},{14,10},{10,6},{6,2},{2,0},{1,5},{5,9},... | collective-permute-start | bytes 393224 | tf_op jit(solution)/shard_map/ppermute | solution.py:222
  14.3 1.4 %collective-permute-done.9.refs_0_ = bf16[32,2176]{1,0:T(8,128)(2,1)S(1)} collective-permute-done((bf16[32,2176]{1,0:T(8,128)(2,1)S(1)}, bf16[32,2176]{1,0:T(8,128)(2,1)S(1)}, u32[]{:S(2)}, u32[]{:S(2)}) %collective-permute-start.9) | collective-permute-done | bytes 139296 | tf_op jit(solution)/shard_map/ppermute | solution.py:222
  15.7 2.2 %collective-permute-start.15 = (bf16[32,2176]{1,0:T(8,128)(2,1)S(1)}, bf16[32,2176]{1,0:T(8,128)(2,1)S(1)}, u32[]{:S(2)}, u32[]{:S(2)}) collective-permute-start(bf16[32,2176]{1,0:T(8,128)(2,1)S(1)} %collective-permute-done.9.refs_0_), channel_id=1, source_target_pairs={{0,4},{4,8},{8,12},{12,14},{14,10},{10,6},{6,2},{2,0},{1,5},{5,9},... | collective-permute-start | bytes 417800 | tf_op jit(solution)/shard_map/ppermute | solution.py:222
  18.6 2.1 %collective-permute-start.16 = (bf16[32,2048]{1,0:T(8,128)(2,1)S(1)}, bf16[32,2048]{1,0:T(8,128)(2,1)S(1)}, u32[]{:S(2)}, u32[]{:S(2)}) collective-permute-start(bf16[32,2048]{1,0:T(8,128)(2,1)S(1)} %collective-permute-done.10.refs_1_), channel_id=1, source_target_pairs={{0,4},{4,8},{8,12},{12,14},{14,10},{10,6},{6,2},{2,0},{1,5},{5,9},... | collective-permute-start | bytes 393224 | tf_op jit(solution)/shard_map/ppermute | solution.py:222
  20.8 1.8 %collective-permute-start = (bf16[128,2176]{1,0:T(8,128)(2,1)S(1)}, bf16[128,2176]{1,0:T(8,128)(2,1)S(1)}, u32[]{:S(2)}, u32[]{:S(2)}) collective-permute-start(bf16[128,2176]{1,0:T(8,128)(2,1)S(1)} %get-tuple-element.26.refs_0_), channel_id=1, source_target_pairs={{0,16},{16,0},{1,17},{17,1},{2,18},{18,2},{3,19},{19,3},{4,20},{20... | collective-permute-start | bytes 1671176 | tf_op jit(solution)/shard_map/ppermute | solution.py:225
  23.7 2.0 %collective-permute-done.17.refs_2_ = bf16[32,2048]{1,0:T(8,128)(2,1)S(1)} collective-permute-done((bf16[32,2048]{1,0:T(8,128)(2,1)S(1)}, bf16[32,2048]{1,0:T(8,128)(2,1)S(1)}, u32[]{:S(2)}, u32[]{:S(2)}) %collective-permute-start.17) | collective-permute-done | bytes 131104 | tf_op jit(solution)/shard_map/ppermute | solution.py:223
  26.4 1.6 %collective-permute-start.21 = (bf16[32,2176]{1,0:T(8,128)(2,1)S(1)}, bf16[32,2176]{1,0:T(8,128)(2,1)S(1)}, u32[]{:S(2)}, u32[]{:S(2)}) collective-permute-start(bf16[32,2176]{1,0:T(8,128)(2,1)S(1)} %collective-permute-done.15.refs_0_), channel_id=1, source_target_pairs={{0,4},{4,8},{8,12},{12,14},{14,10},{10,6},{6,2},{2,0},{1,5},{5,9},... | collective-permute-start | bytes 417800 | tf_op jit(solution)/shard_map/ppermute | solution.py:222
  28.5 2.2 %shard_map.111 = (f32[128,1024]{1,0:T(8,128)S(1)}, f32[128,1024]{1,0:T(8,128)S(1)}) custom-call(bf16[128,2176]{1,0:T(8,128)(2,1)S(1)} %get-tuple-element.26.refs_0_, bf16[704,2048]{1,0:T(8,128)(2,1)S(1)} %bitcast.24, bf16[704,2048]{1,0:T(8,128)(2,1)S(1)} %bitcast.29, bf16[704,2048]{1,0:T(8,128)(2,1)S(1)} %bitcast.18), custom_call_target="tpu_custom_call" | custom-call | flops 1107296256 | bytes 8650752 | tf_op jit(solution)/shard_map/pallas_call | solution.py:26
  30.8 1.3 %collective-permute-done.21.refs_0_ = bf16[32,2176]{1,0:T(8,128)(2,1)S(1)} collective-permute-done((bf16[32,2176]{1,0:T(8,128)(2,1)S(1)}, bf16[32,2176]{1,0:T(8,128)(2,1)S(1)}, u32[]{:S(2)}, u32[]{:S(2)}) %collective-permute-start.21) | collective-permute-done | bytes 139296 | tf_op jit(solution)/shard_map/ppermute | solution.py:222
  32.0 1.3 %collective-permute-done.22.refs_1_ = bf16[32,2176]{1,0:T(8,128)(2,1)S(1)} collective-permute-done((bf16[32,2176]{1,0:T(8,128)(2,1)S(1)}, bf16[32,2176]{1,0:T(8,128)(2,1)S(1)}, u32[]{:S(2)}, u32[]{:S(2)}) %collective-permute-start.22) | collective-permute-done | bytes 139296 | tf_op jit(solution)/shard_map/ppermute | solution.py:223
  33.5 1.7 %shard_map.112 = (f32[256,1024]{1,0:T(8,128)S(1)}, bf16[256,1024]{1,0:T(8,128)(2,1)S(1)}) custom-call(bf16[128,2176]{1,0:T(8,128)(2,1)S(1)} %get-tuple-element.26.refs_0_, bf16[128,2176]{1,0:T(8,128)(2,1)S(1)} %collective-permute-done.refs_1_, f32[128,1024]{1,0:T(8,128)S(1)} %get-tuple-element.27.refs_2_, f32[128,1024]{1,0:T(8,128)S(1)} %get-tuple-element.28.refs_3_, ...), custom_call_target="tpu_custom_call" | custom-call | flops 1107296256 | bytes 4325376 | tf_op jit(solution)/shard_map/pallas_call | solution.py:26
  35.7 2.6 %shard_map.118 = (f32[256,1024]{1,0:T(8,128)S(1)}, bf16[256,1024]{1,0:T(8,128)(2,1)S(1)}) custom-call(bf16[128,2176]{1,0:T(8,128)(2,1)S(1)} %shard_map.117.refs_0_, bf16[128,2176]{1,0:T(8,128)(2,1)S(1)} %collective-permute-done.19.refs_1_, bf16[704,2048]{1,0:T(8,128)(2,1)S(1)} %bitcast.25, bf16[704,2048]{1,0:T(8,128)(2,1)S(1)} %bitcast.30, ...), custom_call_target="tpu_custom_call" | custom-call | flops 2214592512 | bytes 8650752 | tf_op jit(solution)/shard_map/pallas_call | solution.py:26
  38.5 2.6 %shard_map.116 = (f32[256,1024]{1,0:T(8,128)S(1)}, bf16[256,1024]{1,0:T(8,128)(2,1)S(1)}) custom-call(bf16[128,2176]{1,0:T(8,128)(2,1)S(1)} %shard_map.115.refs_0_, bf16[128,2176]{1,0:T(8,128)(2,1)S(1)} %collective-permute-done.13.refs_1_, bf16[704,2048]{1,0:T(8,128)(2,1)S(1)} %bitcast.26, bf16[704,2048]{1,0:T(8,128)(2,1)S(1)} %bitcast.31, ...), custom_call_target="tpu_custom_call" | custom-call | flops 2214592512 | bytes 8650752 | tf_op jit(solution)/shard_map/pallas_call | solution.py:26
  41.7 2.1 %shard_map.120 = (bf16[128,1024]{1,0:T(8,128)(2,1)S(1)}, bf16[704,128]{1,0:T(8,128)(2,1)S(1)}) custom-call(bf16[64,2176]{1,0:T(8,128)(2,1)S(1)} %shard_map.119.refs_0_, bf16[64,2176]{1,0:T(8,128)(2,1)S(1)} %collective-permute-done.23.refs_1_, bf16[704,2048]{1,0:T(8,128)(2,1)S(1)} %bitcast.27, bf16[704,2048]{1,0:T(8,128)(2,1)S(1)} %bitcast.32, ...), custom_call_target="tpu_custom_call" | custom-call | flops 922746880 | bytes 8650752 | tf_op jit(solution)/shard_map/pallas_call | solution.py:26
  43.9 2.6 %shard_map.114 = (f32[256,1024]{1,0:T(8,128)S(1)}, bf16[256,1024]{1,0:T(8,128)(2,1)S(1)}) custom-call(bf16[128,2176]{1,0:T(8,128)(2,1)S(1)} %shard_map.113.refs_0_, bf16[128,2176]{1,0:T(8,128)(2,1)S(1)} %collective-permute-done.7.refs_1_, bf16[704,2048]{1,0:T(8,128)(2,1)S(1)} %bitcast.28, bf16[704,2048]{1,0:T(8,128)(2,1)S(1)} %bitcast.33, ...), custom_call_target="tpu_custom_call" | custom-call | flops 2214592512 | bytes 8650752 | tf_op jit(solution)/shard_map/pallas_call | solution.py:26
  48.1 1.6 %collective-permute-start.25 = (bf16[64,1024]{1,0:T(8,128)(2,1)S(1)}, bf16[64,1024]{1,0:T(8,128)(2,1)S(1)}, u32[]{:S(2)}, u32[]{:S(2)}) collective-permute-start(bf16[64,1024]{1,0:T(8,128)(2,1)S(1)} %get-tuple-element.43), channel_id=1, source_target_pairs={{0,4},{4,8},{8,12},{12,14},{14,10},{10,6},{6,2},{2,0},{1,5},{5,9},... | collective-permute-start | bytes 393224 | tf_op jit(solution)/shard_map/ppermute | solution.py:222
  49.8 3.3 %collective-permute-done.35.refs_2_ = bf16[64,1024]{1,0:T(8,128)(2,1)S(1)} collective-permute-done((bf16[64,1024]{1,0:T(8,128)(2,1)S(1)}, bf16[64,1024]{1,0:T(8,128)(2,1)S(1)}, u32[]{:S(2)}, u32[]{:S(2)}) %collective-permute-start.35) | collective-permute-done | bytes 131104 | tf_op jit(solution)/shard_map/ppermute | solution.py:223
  53.1 1.6 %collective-permute-start.29 = (bf16[64,1024]{1,0:T(8,128)(2,1)S(1)}, bf16[64,1024]{1,0:T(8,128)(2,1)S(1)}, u32[]{:S(2)}, u32[]{:S(2)}) collective-permute-start(bf16[64,1024]{1,0:T(8,128)(2,1)S(1)} %get-tuple-element.44), channel_id=1, source_target_pairs={{0,4},{4,8},{8,12},{12,14},{14,10},{10,6},{6,2},{2,0},{1,5},{5,9},... | collective-permute-start | bytes 393224 | tf_op jit(solution)/shard_map/ppermute | solution.py:222
  55.3 1.6 %collective-permute-start.26 = (bf16[64,1024]{1,0:T(8,128)(2,1)S(1)}, bf16[64,1024]{1,0:T(8,128)(2,1)S(1)}, u32[]{:S(2)}, u32[]{:S(2)}) collective-permute-start(bf16[64,1024]{1,0:T(8,128)(2,1)S(1)} %shard_map.123), channel_id=1, source_target_pairs={{0,4},{4,8},{8,12},{12,14},{14,10},{10,6},{6,2},{2,0},{1,5},{5,9},... | collective-permute-start | bytes 393224 | tf_op jit(solution)/shard_map/ppermute | solution.py:222
  57.6 1.9 %collective-permute-done.29.refs_2_ = bf16[64,1024]{1,0:T(8,128)(2,1)S(1)} collective-permute-done((bf16[64,1024]{1,0:T(8,128)(2,1)S(1)}, bf16[64,1024]{1,0:T(8,128)(2,1)S(1)}, u32[]{:S(2)}, u32[]{:S(2)}) %collective-permute-start.29) | collective-permute-done | bytes 131104 | tf_op jit(solution)/shard_map/ppermute | solution.py:222
  59.5 1.6 %collective-permute-start.30 = (bf16[64,1024]{1,0:T(8,128)(2,1)S(1)}, bf16[64,1024]{1,0:T(8,128)(2,1)S(1)}, u32[]{:S(2)}, u32[]{:S(2)}) collective-permute-start(bf16[64,1024]{1,0:T(8,128)(2,1)S(1)} %shard_map.127), channel_id=1, source_target_pairs={{0,4},{4,8},{8,12},{12,14},{14,10},{10,6},{6,2},{2,0},{1,5},{5,9},... | collective-permute-start | bytes 393224 | tf_op jit(solution)/shard_map/ppermute | solution.py:222
  61.1 1.5 %collective-permute-start.2 = (bf16[128,1024]{1,0:T(8,128)(2,1)S(1)}, bf16[128,1024]{1,0:T(8,128)(2,1)S(1)}, u32[]{:S(2)}, u32[]{:S(2)}) collective-permute-start(bf16[128,1024]{1,0:T(8,128)(2,1)S(1)} %slice.7), channel_id=1, source_target_pairs={{0,16},{16,0},{1,17},{17,1},{2,18},{18,2},{3,19},{19,3},{4,20},{20... | collective-permute-start | bytes 786440 | tf_op jit(solution)/shard_map/ppermute | solution.py:225
  63.2 1.6 %collective-permute-start.27 = (bf16[64,1024]{1,0:T(8,128)(2,1)S(1)}, bf16[64,1024]{1,0:T(8,128)(2,1)S(1)}, u32[]{:S(2)}, u32[]{:S(2)}) collective-permute-start(bf16[64,1024]{1,0:T(8,128)(2,1)S(1)} %shard_map.124), channel_id=1, source_target_pairs={{0,4},{4,8},{8,12},{12,14},{14,10},{10,6},{6,2},{2,0},{1,5},{5,9},... | collective-permute-start | bytes 393224 | tf_op jit(solution)/shard_map/ppermute | solution.py:222
  66.0 1.6 %collective-permute-start.31 = (bf16[64,1024]{1,0:T(8,128)(2,1)S(1)}, bf16[64,1024]{1,0:T(8,128)(2,1)S(1)}, u32[]{:S(2)}, u32[]{:S(2)}) collective-permute-start(bf16[64,1024]{1,0:T(8,128)(2,1)S(1)} %shard_map.128), channel_id=1, source_target_pairs={{0,4},{4,8},{8,12},{12,14},{14,10},{10,6},{6,2},{2,0},{1,5},{5,9},... | collective-permute-start | bytes 393224 | tf_op jit(solution)/shard_map/ppermute | solution.py:222
  67.6 1.5 %collective-permute-done.33.refs_2_ = bf16[64,1024]{1,0:T(8,128)(2,1)S(1)} collective-permute-done((bf16[64,1024]{1,0:T(8,128)(2,1)S(1)}, bf16[64,1024]{1,0:T(8,128)(2,1)S(1)}, u32[]{:S(2)}, u32[]{:S(2)}) %collective-permute-start.33) | collective-permute-done | bytes 131104 | tf_op jit(solution)/shard_map/ppermute | solution.py:223
  69.3 2.0 %collective-permute-start.28 = (bf16[64,1024]{1,0:T(8,128)(2,1)S(1)}, bf16[64,1024]{1,0:T(8,128)(2,1)S(1)}, u32[]{:S(2)}, u32[]{:S(2)}) collective-permute-start(bf16[64,1024]{1,0:T(8,128)(2,1)S(1)} %shard_map.125), channel_id=1, source_target_pairs={{0,4},{4,8},{8,12},{12,14},{14,10},{10,6},{6,2},{2,0},{1,5},{5,9},... | collective-permute-start | bytes 393224 | tf_op jit(solution)/shard_map/ppermute | solution.py:222
  72.0 2.1 %collective-permute-done.34.back_one = bf16[64,1024]{1,0:T(8,128)(2,1)S(1)} collective-permute-done((bf16[64,1024]{1,0:T(8,128)(2,1)S(1)}, bf16[64,1024]{1,0:T(8,128)(2,1)S(1)}, u32[]{:S(2)}, u32[]{:S(2)}) %collective-permute-start.34) | collective-permute-done | bytes 131104 | tf_op jit(solution)/shard_map/ppermute | solution.py:223
  74.3 2.2 %collective-permute-done.38.back_two = bf16[64,1024]{1,0:T(8,128)(2,1)S(1)} collective-permute-done((bf16[64,1024]{1,0:T(8,128)(2,1)S(1)}, bf16[64,1024]{1,0:T(8,128)(2,1)S(1)}, u32[]{:S(2)}, u32[]{:S(2)}) %collective-permute-start.38) | collective-permute-done | bytes 131104 | tf_op jit(solution)/shard_map/ppermute | solution.py:223
  (96 shorter events, 13.6 us)
Async XLA Ops:
  1.8 7.6 %collective-permute-start.3 = (bf16[32,2176]{1,0:T(8,128)(2,1)S(1)}, bf16[32,2176]{1,0:T(8,128)(2,1)S(1)}, u32[]{:S(2)}, u32[]{:S(2)}) collective-permute-start(bf16[32,2176]{1,0:T(8,128)(2,1)S(1)} %get-tuple-element.31), channel_id=1, source_target_pairs={{0,4},{4,8},{8,12},{12,14},{14,10},{10,6},{6,2},{2,0},{1,5},{5,9},... | collective-permute-start | bytes 417800 | tf_op jit(solution)/shard_map/ppermute | solution.py:222
  4.9 6.6 %collective-permute-start.6 = (bf16[32,2176]{1,0:T(8,128)(2,1)S(1)}, bf16[32,2176]{1,0:T(8,128)(2,1)S(1)}, u32[]{:S(2)}, u32[]{:S(2)}) collective-permute-start(bf16[32,2176]{1,0:T(8,128)(2,1)S(1)} %get-tuple-element.34), channel_id=1, source_target_pairs={{4,0},{8,4},{12,8},{14,12},{10,14},{6,10},{2,6},{0,2},{5,1},{9,5},... | collective-permute-start | bytes 417800 | tf_op jit(solution)/shard_map/ppermute | solution.py:223
  4.9 7.3 %collective-permute-start.4 = (bf16[32,2048]{1,0:T(8,128)(2,1)S(1)}, bf16[32,2048]{1,0:T(8,128)(2,1)S(1)}, u32[]{:S(2)}, u32[]{:S(2)}) collective-permute-start(bf16[32,2048]{1,0:T(8,128)(2,1)S(1)} %get-tuple-element.32), channel_id=1, source_target_pairs={{0,4},{4,8},{8,12},{12,14},{14,10},{10,6},{6,2},{2,0},{1,5},{5,9},... | collective-permute-start | bytes 393224 | tf_op jit(solution)/shard_map/ppermute | solution.py:222
  6.9 7.3 %collective-permute-start.5 = (bf16[32,2048]{1,0:T(8,128)(2,1)S(1)}, bf16[32,2048]{1,0:T(8,128)(2,1)S(1)}, u32[]{:S(2)}, u32[]{:S(2)}) collective-permute-start(bf16[32,2048]{1,0:T(8,128)(2,1)S(1)} %get-tuple-element.33), channel_id=1, source_target_pairs={{4,0},{8,4},{12,8},{14,12},{10,14},{6,10},{2,6},{0,2},{5,1},{9,5},... | collective-permute-start | bytes 393224 | tf_op jit(solution)/shard_map/ppermute | solution.py:223
  9.4 6.3 %collective-permute-start.9 = (bf16[32,2176]{1,0:T(8,128)(2,1)S(1)}, bf16[32,2176]{1,0:T(8,128)(2,1)S(1)}, u32[]{:S(2)}, u32[]{:S(2)}) collective-permute-start(bf16[32,2176]{1,0:T(8,128)(2,1)S(1)} %collective-permute-done.3.refs_0_), channel_id=1, source_target_pairs={{0,4},{4,8},{8,12},{12,14},{14,10},{10,6},{6,2},{2,0},{1,5},{5,9},... | collective-permute-start | bytes 417800 | tf_op jit(solution)/shard_map/ppermute | solution.py:222
  11.5 6.4 %collective-permute-start.12 = (bf16[32,2176]{1,0:T(8,128)(2,1)S(1)}, bf16[32,2176]{1,0:T(8,128)(2,1)S(1)}, u32[]{:S(2)}, u32[]{:S(2)}) collective-permute-start(bf16[32,2176]{1,0:T(8,128)(2,1)S(1)} %collective-permute-done.6.refs_3_), channel_id=1, source_target_pairs={{4,0},{8,4},{12,8},{14,12},{10,14},{6,10},{2,6},{0,2},{5,1},{9,5},... | collective-permute-start | bytes 417800 | tf_op jit(solution)/shard_map/ppermute | solution.py:223
  12.2 6.4 %collective-permute-start.10 = (bf16[32,2048]{1,0:T(8,128)(2,1)S(1)}, bf16[32,2048]{1,0:T(8,128)(2,1)S(1)}, u32[]{:S(2)}, u32[]{:S(2)}) collective-permute-start(bf16[32,2048]{1,0:T(8,128)(2,1)S(1)} %collective-permute-done.4.refs_1_), channel_id=1, source_target_pairs={{0,4},{4,8},{8,12},{12,14},{14,10},{10,6},{6,2},{2,0},{1,5},{5,9},... | collective-permute-start | bytes 393224 | tf_op jit(solution)/shard_map/ppermute | solution.py:222
  14.3 6.4 %collective-permute-start.11 = (bf16[32,2048]{1,0:T(8,128)(2,1)S(1)}, bf16[32,2048]{1,0:T(8,128)(2,1)S(1)}, u32[]{:S(2)}, u32[]{:S(2)}) collective-permute-start(bf16[32,2048]{1,0:T(8,128)(2,1)S(1)} %collective-permute-done.5.refs_2_), channel_id=1, source_target_pairs={{4,0},{8,4},{12,8},{14,12},{10,14},{6,10},{2,6},{0,2},{5,1},{9,5},... | collective-permute-start | bytes 393224 | tf_op jit(solution)/shard_map/ppermute | solution.py:223
  15.7 10.0 %collective-permute-start.15 = (bf16[32,2176]{1,0:T(8,128)(2,1)S(1)}, bf16[32,2176]{1,0:T(8,128)(2,1)S(1)}, u32[]{:S(2)}, u32[]{:S(2)}) collective-permute-start(bf16[32,2176]{1,0:T(8,128)(2,1)S(1)} %collective-permute-done.9.refs_0_), channel_id=1, source_target_pairs={{0,4},{4,8},{8,12},{12,14},{14,10},{10,6},{6,2},{2,0},{1,5},{5,9},... | collective-permute-start | bytes 417800 | tf_op jit(solution)/shard_map/ppermute | solution.py:222
  17.9 7.8 %collective-permute-start.18 = (bf16[32,2176]{1,0:T(8,128)(2,1)S(1)}, bf16[32,2176]{1,0:T(8,128)(2,1)S(1)}, u32[]{:S(2)}, u32[]{:S(2)}) collective-permute-start(bf16[32,2176]{1,0:T(8,128)(2,1)S(1)} %collective-permute-done.12.refs_3_), channel_id=1, source_target_pairs={{4,0},{8,4},{12,8},{14,12},{10,14},{6,10},{2,6},{0,2},{5,1},{9,5},... | collective-permute-start | bytes 417800 | tf_op jit(solution)/shard_map/ppermute | solution.py:223
  20.8 12.6 %collective-permute-start = (bf16[128,2176]{1,0:T(8,128)(2,1)S(1)}, bf16[128,2176]{1,0:T(8,128)(2,1)S(1)}, u32[]{:S(2)}, u32[]{:S(2)}) collective-permute-start(bf16[128,2176]{1,0:T(8,128)(2,1)S(1)} %get-tuple-element.26.refs_0_), channel_id=1, source_target_pairs={{0,16},{16,0},{1,17},{17,1},{2,18},{18,2},{3,19},{19,3},{4,20},{20... | collective-permute-start | bytes 1671176 | tf_op jit(solution)/shard_map/ppermute | solution.py:225
  25.7 10.0 %collective-permute-start.19 = (bf16[128,2176]{1,0:T(8,128)(2,1)S(1)}, bf16[128,2176]{1,0:T(8,128)(2,1)S(1)}, u32[]{:S(2)}, u32[]{:S(2)}) collective-permute-start(bf16[128,2176]{1,0:T(8,128)(2,1)S(1)} %shard_map.117.refs_0_), channel_id=1, source_target_pairs={{0,1},{1,0},{2,3},{3,2},{4,5},{5,4},{6,7},{7,6},{8,9},{9,8},{10,11... | collective-permute-start | bytes 1671176 | tf_op jit(solution)/shard_map/ppermute | solution.py:224
  25.8 12.7 %collective-permute-start.13 = (bf16[128,2176]{1,0:T(8,128)(2,1)S(1)}, bf16[128,2176]{1,0:T(8,128)(2,1)S(1)}, u32[]{:S(2)}, u32[]{:S(2)}) collective-permute-start(bf16[128,2176]{1,0:T(8,128)(2,1)S(1)} %shard_map.115.refs_0_), channel_id=1, source_target_pairs={{0,1},{1,0},{2,3},{3,2},{4,5},{5,4},{6,7},{7,6},{8,9},{9,8},{10,11... | collective-permute-start | bytes 1671176 | tf_op jit(solution)/shard_map/ppermute | solution.py:224
  26.4 5.6 %collective-permute-start.21 = (bf16[32,2176]{1,0:T(8,128)(2,1)S(1)}, bf16[32,2176]{1,0:T(8,128)(2,1)S(1)}, u32[]{:S(2)}, u32[]{:S(2)}) collective-permute-start(bf16[32,2176]{1,0:T(8,128)(2,1)S(1)} %collective-permute-done.15.refs_0_), channel_id=1, source_target_pairs={{0,4},{4,8},{8,12},{12,14},{14,10},{10,6},{6,2},{2,0},{1,5},{5,9},... | collective-permute-start | bytes 417800 | tf_op jit(solution)/shard_map/ppermute | solution.py:222
  32.0 11.9 %collective-permute-start.7 = (bf16[128,2176]{1,0:T(8,128)(2,1)S(1)}, bf16[128,2176]{1,0:T(8,128)(2,1)S(1)}, u32[]{:S(2)}, u32[]{:S(2)}) collective-permute-start(bf16[128,2176]{1,0:T(8,128)(2,1)S(1)} %shard_map.113.refs_0_), channel_id=1, source_target_pairs={{0,1},{1,0},{2,3},{3,2},{4,5},{5,4},{6,7},{7,6},{8,9},{9,8},{10,11... | collective-permute-start | bytes 1671176 | tf_op jit(solution)/shard_map/ppermute | solution.py:224
  33.4 8.3 %collective-permute-start.23 = (bf16[64,2176]{1,0:T(8,128)(2,1)S(1)}, bf16[64,2176]{1,0:T(8,128)(2,1)S(1)}, u32[]{:S(2)}, u32[]{:S(2)}) collective-permute-start(bf16[64,2176]{1,0:T(8,128)(2,1)S(1)} %shard_map.119.refs_0_), channel_id=1, source_target_pairs={{0,1},{1,0},{2,3},{3,2},{4,5},{5,4},{6,7},{7,6},{8,9},{9,8},{10,11... | collective-permute-start | bytes 835592 | tf_op jit(solution)/shard_map/ppermute | solution.py:224
  35.2 20.1 %collective-permute-start.1 = (bf16[256,1024]{1,0:T(8,128)(2,1)S(1)}, bf16[256,1024]{1,0:T(8,128)(2,1)S(1)}, u32[]{:S(2)}, u32[]{:S(2)}) collective-permute-start(bf16[256,1024]{1,0:T(8,128)(2,1)S(1)} %get-tuple-element.30), channel_id=1, source_target_pairs={{0,1},{1,0},{2,3},{3,2},{4,5},{5,4},{6,7},{7,6},{8,9},{9,8},{10,11... | collective-permute-start | bytes 1572872 | tf_op jit(solution)/shard_map/ppermute | solution.py:224
  38.4 9.8 %collective-permute-start.20 = (bf16[256,1024]{1,0:T(8,128)(2,1)S(1)}, bf16[256,1024]{1,0:T(8,128)(2,1)S(1)}, u32[]{:S(2)}, u32[]{:S(2)}) collective-permute-start(bf16[256,1024]{1,0:T(8,128)(2,1)S(1)} %get-tuple-element.40), channel_id=1, source_target_pairs={{0,1},{1,0},{2,3},{3,2},{4,5},{5,4},{6,7},{7,6},{8,9},{9,8},{10,11... | collective-permute-start | bytes 1572872 | tf_op jit(solution)/shard_map/ppermute | solution.py:224
  41.1 15.8 %collective-permute-start.14 = (bf16[256,1024]{1,0:T(8,128)(2,1)S(1)}, bf16[256,1024]{1,0:T(8,128)(2,1)S(1)}, u32[]{:S(2)}, u32[]{:S(2)}) collective-permute-start(bf16[256,1024]{1,0:T(8,128)(2,1)S(1)} %get-tuple-element.38), channel_id=1, source_target_pairs={{0,1},{1,0},{2,3},{3,2},{4,5},{5,4},{6,7},{7,6},{8,9},{9,8},{10,11... | collective-permute-start | bytes 1572872 | tf_op jit(solution)/shard_map/ppermute | solution.py:224
  46.6 18.3 %collective-permute-start.8 = (bf16[256,1024]{1,0:T(8,128)(2,1)S(1)}, bf16[256,1024]{1,0:T(8,128)(2,1)S(1)}, u32[]{:S(2)}, u32[]{:S(2)}) collective-permute-start(bf16[256,1024]{1,0:T(8,128)(2,1)S(1)} %get-tuple-element.36), channel_id=1, source_target_pairs={{0,1},{1,0},{2,3},{3,2},{4,5},{5,4},{6,7},{7,6},{8,9},{9,8},{10,11... | collective-permute-start | bytes 1572872 | tf_op jit(solution)/shard_map/ppermute | solution.py:224
  47.6 5.5 %collective-permute-start.35 = (bf16[64,1024]{1,0:T(8,128)(2,1)S(1)}, bf16[64,1024]{1,0:T(8,128)(2,1)S(1)}, u32[]{:S(2)}, u32[]{:S(2)}) collective-permute-start(bf16[64,1024]{1,0:T(8,128)(2,1)S(1)} %get-tuple-element.46), channel_id=1, source_target_pairs={{4,0},{8,4},{12,8},{14,12},{10,14},{6,10},{2,6},{0,2},{5,1},{9,5},... | collective-permute-start | bytes 393224 | tf_op jit(solution)/shard_map/ppermute | solution.py:223
  48.1 6.6 %collective-permute-start.25 = (bf16[64,1024]{1,0:T(8,128)(2,1)S(1)}, bf16[64,1024]{1,0:T(8,128)(2,1)S(1)}, u32[]{:S(2)}, u32[]{:S(2)}) collective-permute-start(bf16[64,1024]{1,0:T(8,128)(2,1)S(1)} %get-tuple-element.43), channel_id=1, source_target_pairs={{0,4},{4,8},{8,12},{12,14},{14,10},{10,6},{6,2},{2,0},{1,5},{5,9},... | collective-permute-start | bytes 393224 | tf_op jit(solution)/shard_map/ppermute | solution.py:222
  53.1 6.4 %collective-permute-start.29 = (bf16[64,1024]{1,0:T(8,128)(2,1)S(1)}, bf16[64,1024]{1,0:T(8,128)(2,1)S(1)}, u32[]{:S(2)}, u32[]{:S(2)}) collective-permute-start(bf16[64,1024]{1,0:T(8,128)(2,1)S(1)} %get-tuple-element.44), channel_id=1, source_target_pairs={{0,4},{4,8},{8,12},{12,14},{14,10},{10,6},{6,2},{2,0},{1,5},{5,9},... | collective-permute-start | bytes 393224 | tf_op jit(solution)/shard_map/ppermute | solution.py:222
  54.7 6.4 %collective-permute-start.32 = (bf16[64,1024]{1,0:T(8,128)(2,1)S(1)}, bf16[64,1024]{1,0:T(8,128)(2,1)S(1)}, u32[]{:S(2)}, u32[]{:S(2)}) collective-permute-start(bf16[64,1024]{1,0:T(8,128)(2,1)S(1)} %get-tuple-element.45), channel_id=1, source_target_pairs={{4,0},{8,4},{12,8},{14,12},{10,14},{6,10},{2,6},{0,2},{5,1},{9,5},... | collective-permute-start | bytes 393224 | tf_op jit(solution)/shard_map/ppermute | solution.py:223
  55.3 7.4 %collective-permute-start.26 = (bf16[64,1024]{1,0:T(8,128)(2,1)S(1)}, bf16[64,1024]{1,0:T(8,128)(2,1)S(1)}, u32[]{:S(2)}, u32[]{:S(2)}) collective-permute-start(bf16[64,1024]{1,0:T(8,128)(2,1)S(1)} %shard_map.123), channel_id=1, source_target_pairs={{0,4},{4,8},{8,12},{12,14},{14,10},{10,6},{6,2},{2,0},{1,5},{5,9},... | collective-permute-start | bytes 393224 | tf_op jit(solution)/shard_map/ppermute | solution.py:222
  56.9 6.3 %collective-permute-start.36 = (bf16[64,1024]{1,0:T(8,128)(2,1)S(1)}, bf16[64,1024]{1,0:T(8,128)(2,1)S(1)}, u32[]{:S(2)}, u32[]{:S(2)}) collective-permute-start(bf16[64,1024]{1,0:T(8,128)(2,1)S(1)} %shard_map.131), channel_id=1, source_target_pairs={{4,0},{8,4},{12,8},{14,12},{10,14},{6,10},{2,6},{0,2},{5,1},{9,5},... | collective-permute-start | bytes 393224 | tf_op jit(solution)/shard_map/ppermute | solution.py:223
  59.5 6.4 %collective-permute-start.30 = (bf16[64,1024]{1,0:T(8,128)(2,1)S(1)}, bf16[64,1024]{1,0:T(8,128)(2,1)S(1)}, u32[]{:S(2)}, u32[]{:S(2)}) collective-permute-start(bf16[64,1024]{1,0:T(8,128)(2,1)S(1)} %shard_map.127), channel_id=1, source_target_pairs={{0,4},{4,8},{8,12},{12,14},{14,10},{10,6},{6,2},{2,0},{1,5},{5,9},... | collective-permute-start | bytes 393224 | tf_op jit(solution)/shard_map/ppermute | solution.py:222
  61.1 10.9 %collective-permute-start.2 = (bf16[128,1024]{1,0:T(8,128)(2,1)S(1)}, bf16[128,1024]{1,0:T(8,128)(2,1)S(1)}, u32[]{:S(2)}, u32[]{:S(2)}) collective-permute-start(bf16[128,1024]{1,0:T(8,128)(2,1)S(1)} %slice.7), channel_id=1, source_target_pairs={{0,16},{16,0},{1,17},{17,1},{2,18},{18,2},{3,19},{19,3},{4,20},{20... | collective-permute-start | bytes 786440 | tf_op jit(solution)/shard_map/ppermute | solution.py:225
  62.7 6.4 %collective-permute-start.33 = (bf16[64,1024]{1,0:T(8,128)(2,1)S(1)}, bf16[64,1024]{1,0:T(8,128)(2,1)S(1)}, u32[]{:S(2)}, u32[]{:S(2)}) collective-permute-start(bf16[64,1024]{1,0:T(8,128)(2,1)S(1)} %shard_map.129), channel_id=1, source_target_pairs={{4,0},{8,4},{12,8},{14,12},{10,14},{6,10},{2,6},{0,2},{5,1},{9,5},... | collective-permute-start | bytes 393224 | tf_op jit(solution)/shard_map/ppermute | solution.py:223
  63.2 6.0 %collective-permute-start.27 = (bf16[64,1024]{1,0:T(8,128)(2,1)S(1)}, bf16[64,1024]{1,0:T(8,128)(2,1)S(1)}, u32[]{:S(2)}, u32[]{:S(2)}) collective-permute-start(bf16[64,1024]{1,0:T(8,128)(2,1)S(1)} %shard_map.124), channel_id=1, source_target_pairs={{0,4},{4,8},{8,12},{12,14},{14,10},{10,6},{6,2},{2,0},{1,5},{5,9},... | collective-permute-start | bytes 393224 | tf_op jit(solution)/shard_map/ppermute | solution.py:222
  64.9 6.4 %collective-permute-start.37 = (bf16[64,1024]{1,0:T(8,128)(2,1)S(1)}, bf16[64,1024]{1,0:T(8,128)(2,1)S(1)}, u32[]{:S(2)}, u32[]{:S(2)}) collective-permute-start(bf16[64,1024]{1,0:T(8,128)(2,1)S(1)} %shard_map.132), channel_id=1, source_target_pairs={{4,0},{8,4},{12,8},{14,12},{10,14},{6,10},{2,6},{0,2},{5,1},{9,5},... | collective-permute-start | bytes 393224 | tf_op jit(solution)/shard_map/ppermute | solution.py:223
  66.0 6.0 %collective-permute-start.31 = (bf16[64,1024]{1,0:T(8,128)(2,1)S(1)}, bf16[64,1024]{1,0:T(8,128)(2,1)S(1)}, u32[]{:S(2)}, u32[]{:S(2)}) collective-permute-start(bf16[64,1024]{1,0:T(8,128)(2,1)S(1)} %shard_map.128), channel_id=1, source_target_pairs={{0,4},{4,8},{8,12},{12,14},{14,10},{10,6},{6,2},{2,0},{1,5},{5,9},... | collective-permute-start | bytes 393224 | tf_op jit(solution)/shard_map/ppermute | solution.py:222
  (18 other events, 138.7 us)
